TPU v7x, 256 devices: a whole 4x4x8 slice. The times are simulated.
256 devices in a mesh: cluster: 64 (over z, x, core), sub: 4 (over y).
Axes of the slice: x: 4, y: 4, z: 8, core: 2. Of those that a mesh axis runs over, the one named last changes fastest.
Arguments:
- mantissas: int32 [64, 64, 168, 128], P('cluster', 'sub'), may hold values from -128 to 127
- exponents: int32 [64, 64, 14], P('cluster', 'sub'), may hold values from -9 to -6
- channel: bfloat16 [64, 64, 2, 64, 128], P('cluster', 'sub'), may hold values from -0.5 to 0.5
- inverses: bfloat16 [64, 64, 2, 128, 128], P('cluster', 'sub'), may hold values from -4 to 4, as said below
Outputs:
- detected: bfloat16 [64, 168, 256], P('sub')
Inputs may be any that keep to these rules, and one draw needn't show every extreme that they name: `inverses`: each real part has a positive diagonal; the matrices are otherwise dense.
All inputs are finite; a program needn't handle non-finite values.
Results may differ from a plain program's by a relative error of at most 0.0074.
Values may be sent and summed in bfloat16 or wider, within the bound.
No kernel may reach another device: no remote copies, remote signals or barrier semaphores. Data moves between devices by JAX's collectives and lax.ppermute only.
A program may use at most 64 MiB of HBM per device.

v0:
```python
import jax
import jax.numpy as jnp
from jax import lax
from jax.sharding import PartitionSpec as P

ITERS = 3


RHO = 0.5


def in_blocks(shard, dim, size):
    before, after = (shard.shape[:dim], shard.shape[dim + 1 :])
    return jnp.moveaxis(shard.reshape(*before, size, -1, *after), dim, 0)


def sent_and_summed(shard, axis, dim):
    size = lax.axis_size(axis)
    parts = lax.all_to_all(in_blocks(shard, dim, size), axis, 0, 0, tiled=True)
    return jnp.sum(parts.astype(jnp.float32), axis=0)


def sent_to_all(shard, axis):
    copies = jnp.broadcast_to(shard, (lax.axis_size(axis), *shard.shape))
    return lax.all_to_all(copies, axis, split_axis=0, concat_axis=0, tiled=True)


def in_order(parts, dim):
    lengths = list(parts.shape[1:])
    lengths[dim] *= parts.shape[0]
    return jnp.moveaxis(parts, 0, dim).reshape(lengths)


def gather_directly(shard, axis, dim):
    parts = sent_to_all(shard, axis)
    return in_order(parts, dim)


def taken_together(shard, axis):
    everything = sent_to_all(shard, axis)
    return jnp.sum(everything, axis=0)


def complex_block(real, imag):
    top = jnp.concatenate([real, -imag], axis=-1)
    bottom = jnp.concatenate([imag, real], axis=-1)
    return jnp.concatenate([top, bottom], axis=-2)


def per_device(mantissas, exponents, channel, inverses):
    clusters = lax.axis_size("cluster")
    mant = mantissas[0]
    blocks, vectors, _ = mant.shape
    expo = exponents[0]
    scale = jnp.repeat(jnp.exp2(expo.astype(jnp.float32)), vectors // expo.shape[1], axis=1)
    signal = (mant.astype(jnp.float32) * scale[:, :, None]).astype(jnp.bfloat16)
    match = complex_block(channel[0, :, 0], channel[0, :, 1])
    matched_filter = jnp.einsum("rsa,rau->rsu", signal, match, preferred_element_type=jnp.float32)
    solve_block = complex_block(inverses[0, :, 0], inverses[0, :, 1])
    width = matched_filter.shape[2]
    consensus = jnp.zeros(matched_filter.shape, jnp.float32)
    dual = jnp.zeros(matched_filter.shape, jnp.float32)
    for step in range(ITERS):
        rhs = (matched_filter + RHO * (consensus - dual)).astype(jnp.bfloat16)
        local = jnp.einsum("rsk,rjk->rsj", rhs, solve_block, preferred_element_type=jnp.float32)
        term = local + dual
        flat = term.reshape(blocks * vectors, width)
        share = sent_and_summed(flat.astype(jnp.bfloat16), "cluster", 0)
        average = (share / clusters).astype(jnp.bfloat16)
        gathered = gather_directly(average, "cluster", 0)
        consensus = gathered.reshape(blocks, vectors, width).astype(jnp.float32)
        dual = term - consensus
    users = width // 2
    column_list = jnp.sum(consensus * consensus, axis=(0, 1))
    partial_value = column_list[:users] + column_list[users:]
    total_power = taken_together(partial_value, "sub")
    power = total_power / (blocks * lax.axis_size("sub") * vectors)
    factor = lax.rsqrt(power + 1e-06)
    factor = jnp.concatenate([factor, factor])
    return (consensus * factor).astype(jnp.bfloat16)


def solution(mesh):
    placed = (
        P("cluster", "sub", None, None),
        P("cluster", "sub", None),
        P("cluster", "sub", None, None, None),
        P("cluster", "sub", None, None, None),
    )
    return jax.shard_map(
        per_device, mesh=mesh, in_specs=placed, out_specs=P("sub", None, None), check_vma=False
    )
```

profile of v0, /device:TPU:2, one launch (start us, length us, event | category | flops | bytes accessed | tf_op | source)
XLA Modules:
  0.0 334.4 jit_solution(9471531085499084590)
XLA Ops:
  0.0 1.1 fusion.18
  1.1 1.9 slice_bitcast_fusion.2
  2.9 1.1 fusion.19
  4.1 1.1 slice_bitcast_fusion
  5.5 2.2 fusion.5
  7.7 2.8 fusion.20
  10.5 3.3 convert_element_type.91
  13.9 52.0 %all_to_all.36 = bf16[64,42,256]{2,1,0:T(8,128)(2,1)S(1)} all-to-all(bf16[64,42,256]{2,1,0:T(8,128)(2,1)} %convert_element_type.91), channel_id=1, replica_groups=mesh['cluster'=64,'sub'=4] {'cluster'}, dimensions={0} | all-to-all | bytes 2752512 | tf_op jit(solution)/shard_map/all_to_all | solution.py:19
  66.3 45.3 %all_to_all.37 = bf16[64,42,256]{2,1,0:T(8,128)(2,1)} all-to-all(bf16[64,42,256]{2,1,0:T(8,128)(2,1)S(1)} %broadcast_in_dim.17), channel_id=1, replica_groups=mesh['cluster'=64,'sub'=4] {'cluster'}, dimensions={0} | all-to-all | bytes 2752512 | tf_op jit(solution)/shard_map/all_to_all | solution.py:25
  111.6 3.4 %reshape.29 = f32[16,168,256]{2,1,0:T(8,128)} reshape(bf16[64,42,256]{2,1,0:T(8,128)(2,1)} %all_to_all.37) | data formatting | bytes 4128768 | tf_op jit(solution)/shard_map/convert_element_type | solution.py:71
  115.0 7.8 %fusion.21 = (bf16[16,168,256]{2,1,0:T(8,128)(2,1)}, f32[16,168,256]{2,1,0:T(8,128)}) fusion(f32[16,168,256]{2,1,0:T(8,128)} %get-tuple-element.10, f32[16,168,256]{2,1,0:T(8,128)} %reshape.29, bf16[16,128,128]{2,1,0:T(8,128)(2,1)} %get-tuple-element.6, bf16[16,128,128]{2,1,0:T(8,128)(2,1)} %get-tuple-element.5, bf16[16,128,128]{2,1,0:T(8,128)(2,1)S(1)} %fusion.19, ...), kind=kOutput, calls=%fused_computation.42 | convolution fusion | flops 366215168 | bytes 13959168 | tf_op jit(solution)/shard_map/rsk,rjk->rsj/dot_general | solution.py:65
  122.8 3.3 convert_element_type.98
  126.1 45.4 %all_to_all.38 = bf16[64,42,256]{2,1,0:T(8,128)(2,1)S(1)} all-to-all(bf16[64,42,256]{2,1,0:T(8,128)(2,1)} %convert_element_type.98), channel_id=1, replica_groups=mesh['cluster'=64,'sub'=4] {'cluster'}, dimensions={0} | all-to-all | bytes 2752512 | tf_op jit(solution)/shard_map/all_to_all | solution.py:19
  171.9 45.3 %all_to_all.39 = bf16[64,42,256]{2,1,0:T(8,128)(2,1)} all-to-all(bf16[64,42,256]{2,1,0:T(8,128)(2,1)S(1)} %broadcast_in_dim.18), channel_id=1, replica_groups=mesh['cluster'=64,'sub'=4] {'cluster'}, dimensions={0} | all-to-all | bytes 2752512 | tf_op jit(solution)/shard_map/all_to_all | solution.py:25
  217.3 3.4 %reshape.30 = f32[16,168,256]{2,1,0:T(8,128)} reshape(bf16[64,42,256]{2,1,0:T(8,128)(2,1)} %all_to_all.39) | data formatting | bytes 4128768 | tf_op jit(solution)/shard_map/convert_element_type | solution.py:71
  220.7 6.8 %add_convert_fusion = bf16[16,168,256]{2,1,0:T(8,128)(2,1)} fusion(f32[16,168,256]{2,1,0:T(8,128)} %get-tuple-element.12, f32[16,168,256]{2,1,0:T(8,128)} %reshape.30, f32[16,168,256]{2,1,0:T(8,128)S(1)} %fusion.5, bf16[16,128,128]{2,1,0:T(8,128)(2,1)} %get-tuple-element.6, bf16[16,128,128]{2,1,0:T(8,128)(2,1)} %get-tuple-element.5, ...), kind=kOutput, calls=%fused_computation.5 | convolution fusion | flops 366215168 | bytes 11206656 | tf_op jit(solution)/shard_map/rsk,rjk->rsj/dot_general | solution.py:65
  227.5 2.3 convert_element_type.105
  229.8 45.2 %all_to_all.40 = bf16[64,42,256]{2,1,0:T(8,128)(2,1)S(1)} all-to-all(bf16[64,42,256]{2,1,0:T(8,128)(2,1)S(1)} %convert_element_type.105), channel_id=1, replica_groups=mesh['cluster'=64,'sub'=4] {'cluster'}, dimensions={0} | all-to-all | bytes 2752512 | tf_op jit(solution)/shard_map/all_to_all | solution.py:19
  275.4 45.2 %all_to_all.41 = bf16[64,42,256]{2,1,0:T(8,128)(2,1)S(1)} all-to-all(bf16[64,42,256]{2,1,0:T(8,128)(2,1)S(1)} %broadcast_in_dim.19), channel_id=1, replica_groups=mesh['cluster'=64,'sub'=4] {'cluster'}, dimensions={0} | all-to-all | bytes 2752512 | tf_op jit(solution)/shard_map/all_to_all | solution.py:25
  321.1 0.6 broadcast_in_dim.20
  321.7 4.5 %all-to-all-start.6 = ((f32[4,1,128]{2,1,0:T(1,128)}), f32[4,1,128]{2,1,0:T(1,128)S(1)}, u32[]{:S(2)}, u32[]{:S(2)}) async-start(f32[4,1,128]{2,1,0:T(1,128)} %broadcast_in_dim.20), calls=%async_computation.6 | async-start | bytes 4096 | tf_op jit(solution)/shard_map/all_to_all | solution.py:25
  326.1 1.7 reshape.31
  327.8 3.5 %all-to-all-done.6 = f32[4,1,128]{2,1,0:T(1,128)S(1)} async-done(((f32[4,1,128]{2,1,0:T(1,128)}), f32[4,1,128]{2,1,0:T(1,128)S(1)}, u32[]{:S(2)}, u32[]{:S(2)}) %all-to-all-start.6) | async-done | bytes 2080 | tf_op jit(solution)/shard_map/all_to_all | solution.py:25
  331.4 3.1 multiply_convert_fusion
  (26 shorter events, 1.9 us)
Async XLA Ops:
  0.0 4.1 %copy-start = (bf16[1,16,2,128,128]{4,3,2,1,0:T(8,128)(2,1)S(1)}, bf16[1,16,2,128,128]{4,3,2,1,0:T(8,128)(2,1)}, u32[]{:S(2)}) copy-start(bf16[1,16,2,128,128]{4,3,2,1,0:T(8,128)(2,1)} %param.7) | copy-start | bytes 3145732
  0.0 5.2 %copy-start.3 = (s32[1,16,14]{1,0,2:T(1,128)S(1)}, s32[1,16,14]{1,0,2:T(1,128)}, u32[]{:S(2)}) copy-start(s32[1,16,14]{1,0,2:T(1,128)} %param.5) | copy-start | bytes 2692
  5.5 2.2 copy-start.1
  5.5 2.2 copy-start.2
  321.7 9.7 %all-to-all-start.6 = ((f32[4,1,128]{2,1,0:T(1,128)}), f32[4,1,128]{2,1,0:T(1,128)S(1)}, u32[]{:S(2)}, u32[]{:S(2)}) async-start(f32[4,1,128]{2,1,0:T(1,128)} %broadcast_in_dim.20), calls=%async_computation.6 | async-start | bytes 4096 | tf_op jit(solution)/shard_map/all_to_all | solution.py:25
where the time goes:
time: 335 us; the launch traced here: 334 us
  blocking collectives  279 us (83%)
  local copies, waits for them, and re-layouts  21.6 us (6%)
  matrix products  19.6 us (6%)
  other arithmetic  6.57 us (2%)
  starting transfers between devices  4.46 us (1%)
  waiting for transfers between devices  3.48 us (1%)
    all_to_all x3, blocking collectives, sent_and_summed(): parts = lax.all_to_all(in_blocks(shard, dim, size), axis, 0, 0, tiled=True)  143 us
    all_to_all x3, blocking collectives, sent_to_all(): return lax.all_to_all(copies, axis, split_axis=0, concat_axis=0, tiled=True)  136 us
    dot_general x3, matrix products, per_device(): jnp.einsum('rsk,rjk->rsj', rhs, solve_block, preferred_element_type=jnp.f...  17.4 us
    convert_element_type x3, local copies, waits for them, and re-layouts, per_device(): share = sent_and_summed(flat.astype(jnp.bfloat16), 'cluster', 0)  8.87 us
    convert_element_type x3, local copies, waits for them, and re-layouts, per_device(): consensus = gathered.reshape(blocks, vectors, width).astype(jnp.float32)  8.61 us
  transfers between devices with their start and end apart: 1, of which 1 were waited for; matrix products, arithmetic and copies ran while one was open for 1% of the time, Pallas kernels for 0%

commit v1 on v0

v1 whole, which is shorter than its diff:
```python
import jax
import jax.numpy as jnp
from jax import lax
from jax.experimental import pallas as pl
from jax.experimental.pallas import tpu as pltpu
from jax.sharding import PartitionSpec as P


Z, X, C = 8, 4, 2
CLUSTERS = Z * X * C
PART = 48
BF, F32 = jnp.bfloat16, jnp.float32


def place(z, x, c):
    return (z * X + x) * C + c


def shifted(dz=0, dx=0, dc=0):
    return [
        (place(z, x, c), place((z + dz) % Z, (x + dx) % X, c ^ dc))
        for z in range(Z)
        for x in range(X)
        for c in range(C)
    ]


def pair_shifted(dx, dp):
    return [
        (place(z, x, c), place(z ^ dp, (x + dx) % X, c))
        for z in range(Z)
        for x in range(X)
        for c in range(C)
    ]


Z_RINGS = [[place(z, x, c) for z in range(Z)] for x in range(X) for c in range(C)]
SLOTS = ((0, 0), (1, 0), (3, 0), (0, 1), (2, 0), (1, 1), (3, 1), (2, 1))


def moved(value, pairs):
    return lax.ppermute(value, "cluster", pairs)


def dot(a, b):
    return jnp.dot(a, b, preferred_element_type=F32)


def complex_square(x, y):
    top = jnp.concatenate([x, y], axis=1)
    return top, jnp.concatenate([top, jnp.concatenate([-y, x], axis=1)], axis=0)


def pack_kernel(here_ref, mant_ref, expo_ref, chan_ref, inv_ref, *outs):
    x, pair, c = here_ref[0], here_ref[1], here_ref[2]
    row = lax.broadcasted_iota(jnp.int32, (168, 14), 0)
    first = lax.broadcasted_iota(jnp.int32, (168, 14), 1) * 12
    inside = (row >= first) & (row < first + 12)
    for out, (dx, dp) in zip(outs, SLOTS):
        for k, side in enumerate((c, 1 - c)):
            r = side * 8 + lax.rem(x + dx, X) * 2 + (1 - pair if dp else pair)
            out[k, 0:256, :] = inv_ref[r]
            out[k, 256:384, :] = chan_ref[r]
            scale = jnp.exp2(expo_ref[pl.ds(r, 1), :].astype(F32))
            scale = jnp.sum(jnp.where(inside, scale, 0.0), axis=1, keepdims=True)
            out[k, 384:552, :] = (mant_ref[r].astype(F32) * scale).astype(BF)


def packed(here, mant, expo, chan, inv):
    vmem = pl.BlockSpec(memory_space=pltpu.VMEM)
    return pl.pallas_call(
        pack_kernel,
        in_specs=[pl.BlockSpec(memory_space=pltpu.SMEM)] + [vmem] * 4,
        out_specs=[vmem] * 8,
        out_shape=[jax.ShapeDtypeStruct((2, 552, 128), BF)] * 8,
        cost_estimate=pl.CostEstimate(flops=6000000, bytes_accessed=5000000, transcendentals=0),
    )(here, mant, expo, chan, inv)


def add_clusters(held, p1, p2, t, av):
    def one(raw):
        top, square = complex_square(raw[0:128, :].T, raw[128:256, :].T)
        cr, ci = raw[256:320, :], raw[320:384, :]
        match = jnp.concatenate(
            [jnp.concatenate([cr, -ci], axis=1), jnp.concatenate([ci, cr], axis=1)], axis=0
        )
        m = dot(raw[384:552, :], match).astype(BF)
        t1 = dot(m, square)
        t2 = dot(t1.astype(BF), square)
        t3 = dot(t2.astype(BF), square)
        return t1, t2, t3, top.astype(F32), dot(top, square)

    def two(k, carry):
        a, b = one(held[2 * k]), one(held[2 * k + 1])
        t1, t2, t3, top, second = (u + v for u, v in zip(a, b))
        p1[0:168, :] += t1
        p2[0:168, :] += t2 - 2.0 * t1
        t[0:168, :] += 3.0 * t1 - 1.5 * t2 + 0.25 * t3
        av[0:128, :] += top
        av[128:256, :] += second
        return carry

    lax.fori_loop(0, 4, two, 0)


def first_kernel(*refs):
    raws, (p1, p2, t, av), held = refs[:8], refs[8:12], refs[12]
    for k in range(8):
        held[k] = raws[k][0]
    for ref in (p1, p2, t, av):
        ref[...] = jnp.zeros_like(ref)
    add_clusters(held, p1, p2, t, av)


def second_kernel(q_ref, *refs):
    raws, before, outs = refs[:8], refs[8:12], refs[12:16]
    held, (p1, p2, t, av) = refs[16], refs[17:]
    for k in range(8):
        held[k] = raws[k][0]
    for ref, old in zip((p1, p2, t, av), before):
        ref[...] = old[...]
    add_clusters(held, p1, p2, t, av)
    ones = (
        lax.broadcasted_iota(jnp.int32, (128, 256), 0) == lax.broadcasted_iota(jnp.int32, (128, 256), 1)
    ).astype(F32) * 16.0
    first = av[0:128, :]
    av[0:128, :] = first - ones
    av[128:256, :] = av[128:256, :] - 2.0 * first + ones
    for d, out in enumerate(outs):
        q = lax.rem(q_ref[0] + d, 4)
        rows = pl.ds(pl.multiple_of(q * PART, PART), PART)
        out[0:48, :] = p1[rows, :].astype(BF)
        out[48:96, :] = p2[rows, :].astype(BF)
        out[96:144, :] = t[rows, :].astype(BF)
        out[144:208, :] = av[pl.ds(pl.multiple_of(q * 64, 64), 64), :].astype(BF)


SUMS = ((192, 256), (192, 256), (192, 256), (256, 256))


def cluster_specs():
    own = pl.BlockSpec((1, 552, 128), lambda i, *_: (0, 0, 0))
    other = pl.BlockSpec((1, 552, 128), lambda i, *_: (1, 0, 0))
    return [own] * 4 + [other] * 4


def first_partials(raws):
    full = [pl.BlockSpec(shape, lambda i: (0, 0)) for shape in SUMS]
    return pl.pallas_call(
        first_kernel,
        grid=(1,),
        in_specs=cluster_specs(),
        out_specs=full,
        out_shape=[jax.ShapeDtypeStruct(shape, F32) for shape in SUMS],
        scratch_shapes=[pltpu.VMEM((8, 552, 128), BF)],
        cost_estimate=pl.CostEstimate(flops=2000000000, bytes_accessed=3000000, transcendentals=0),
    )(*raws)


def second_partials(q, raws, before):
    full = [pl.BlockSpec(shape, lambda i, q: (0, 0)) for shape in SUMS]
    return pl.pallas_call(
        second_kernel,
        grid_spec=pltpu.PrefetchScalarGridSpec(
            num_scalar_prefetch=1,
            grid=(1,),
            in_specs=cluster_specs() + full,
            out_specs=[pl.BlockSpec((208, 256), lambda i, q: (0, 0))] * 4,
            scratch_shapes=[pltpu.VMEM((8, 552, 128), BF)] + [pltpu.VMEM(shape, F32) for shape in SUMS],
        ),
        out_shape=[jax.ShapeDtypeStruct((208, 256), BF)] * 4,
        cost_estimate=pl.CostEstimate(flops=2000000000, bytes_accessed=3000000, transcendentals=0),
    )(q, *raws, *before)


def total_kernel(*refs):
    parts, (p_ref, av_ref) = refs[:4], refs[4:]
    total = parts[0][...].astype(F32)
    for part in parts[1:]:
        total += part[...].astype(F32)
    total = total * (1.0 / CLUSTERS)
    p_ref[...] = total[0:144, :]
    av_ref[...] = total[144:208, :].astype(BF)


def totals(parts):
    return pl.pallas_call(
        total_kernel,
        out_shape=(
            jax.ShapeDtypeStruct((144, 256), F32),
            jax.ShapeDtypeStruct((64, 256), BF),
        ),
    )(*parts)


def dot_wide(a, b):
    high = a.astype(BF)
    low = (a - high.astype(F32)).astype(BF)
    return dot(high, b) + dot(low, b)


def solve_kernel(quarter_ref, p_ref, a0, a1, a2, a3, out_ref, av):
    for d, part in enumerate((a0, a1, a2, a3)):
        av[lax.rem(quarter_ref[0] + 4 - d, 4)] = part[...]
    mean = jnp.concatenate([av[0], av[1]], axis=0)
    second = jnp.concatenate([av[2], av[3]], axis=0)
    _, mean = complex_square(mean[:, 0:128], mean[:, 128:256])
    _, second = complex_square(second[:, 0:128], second[:, 128:256])
    z1, p2, t = p_ref[0:48, :], p_ref[48:96, :], p_ref[96:144, :]
    g = dot_wide(z1, mean)
    z3 = t + 1.5 * g - 0.5 * dot_wide(z1, second) + dot_wide(g - 0.5 * p2, mean)
    out_ref[...] = z3.astype(BF)


def solved(quarter, p, avs):
    vmem = pl.BlockSpec(memory_space=pltpu.VMEM)
    return pl.pallas_call(
        solve_kernel,
        in_specs=[pl.BlockSpec(memory_space=pltpu.SMEM)] + [vmem] * 5,
        out_specs=vmem,
        out_shape=jax.ShapeDtypeStruct((PART, 256), BF),
        scratch_shapes=[pltpu.VMEM((4, 64, 256), BF)],
    )(quarter, p, *avs)


def power_kernel(order_ref, *refs):
    parts, out_ref, rows = refs[:8], refs[8], refs[9]
    for k, part in enumerate(parts):
        value = part[...].astype(F32)
        rows[order_ref[k]] = jnp.sum(value * value, axis=(0, 1))[None, :]
    total = rows[0]
    for k in range(1, 8):
        total += rows[k]
    out_ref[...] = total[:, 0:128] + total[:, 128:256]


def power_of(order, parts):
    vmem = pl.BlockSpec(memory_space=pltpu.VMEM)
    return pl.pallas_call(
        power_kernel,
        in_specs=[pl.BlockSpec(memory_space=pltpu.SMEM)] + [vmem] * 8,
        out_specs=vmem,
        out_shape=jax.ShapeDtypeStruct((1, 128), F32),
        scratch_shapes=[pltpu.VMEM((8, 1, 256), F32)],
    )(order, *parts)


def finish_kernel(vectors, order_ref, power_ref, *refs):
    parts, out_ref = refs[:8], refs[8]
    power = power_ref[0] + power_ref[1] + power_ref[2] + power_ref[3]
    factor = lax.rsqrt(power * (1.0 / vectors) + 1e-06)
    factor = jnp.concatenate([factor, factor], axis=1)
    for k, part in enumerate(parts):
        for zz in range(Z):
            start = zz // 2 * PART
            size = min(168 - start, PART)
            value = part[zz, 0:size, :].astype(F32) * factor
            out_ref[order_ref[k], zz % 2, start : start + size, :] = value.astype(BF)


def finished(order, power, parts, vectors):
    vmem = pl.BlockSpec(memory_space=pltpu.VMEM)
    return pl.pallas_call(
        lambda *refs: finish_kernel(vectors, *refs),
        in_specs=[pl.BlockSpec(memory_space=pltpu.SMEM)] + [vmem] * 9,
        out_specs=vmem,
        out_shape=jax.ShapeDtypeStruct((8, 2, 168, 256), BF),
    )(order, power, *parts)


def per_device(mantissas, exponents, channel, inverses):
    place_here = lax.axis_index("cluster")
    c = place_here % C
    x = place_here // C % X
    z = place_here // (C * X)
    mant, expo = mantissas[0], exponents[0]
    blocks, vectors, _ = mant.shape
    here = jnp.stack([x, z % 2, c]).astype(jnp.int32)
    sent = packed(
        here, mant, expo, channel[0].reshape(blocks, 128, 128), inverses[0].reshape(blocks, 256, 128)
    )
    raws = [sent[0]]
    for k in range(1, 8):
        raws.append(moved(sent[k], pair_shifted(*SLOTS[k])))
    swapped = []
    for k in range(8):
        swapped.append(moved(raws[k], shifted(dc=1)))
    q = (z // 2).reshape(1).astype(jnp.int32)
    before = first_partials(raws[:4] + swapped[:4])
    sums = second_partials(q, raws[4:] + swapped[4:], before)
    parts = [sums[0]] + [moved(sums[d], shifted(dz=2 * d)) for d in (2, 1, 3)]
    p, av = totals(parts)
    avs = [av] + [moved(av, shifted(dz=2 * d)) for d in (1, 2, 3)]
    share = solved(q, p, avs)
    copies = jnp.broadcast_to(share, (Z, PART, 256))
    mine = lax.all_to_all(copies, "cluster", 0, 0, tiled=True, axis_index_groups=Z_RINGS)
    same = [mine] + [moved(mine, shifted(dx=d)) for d in (1, 2, 3)]
    other = [moved(value, shifted(dc=1)) for value in same]
    order = jnp.stack(
        [side * X + (x + X - d) % X for side in (c, 1 - c) for d in range(X)]
    ).astype(jnp.int32)
    power = power_of(order, same + other)
    power = lax.all_to_all(jnp.broadcast_to(power, (4, 1, 128)), "sub", 0, 0, tiled=True)
    total = blocks * lax.axis_size("sub") * vectors
    return finished(order, power, same + other, total).reshape(blocks, vectors, 256)


def solution(mesh):
    placed = (
        P("cluster", "sub", None, None),
        P("cluster", "sub", None),
        P("cluster", "sub", None, None, None),
        P("cluster", "sub", None, None, None),
    )
    return jax.shard_map(
        per_device, mesh=mesh, in_specs=placed, out_specs=P("sub", None, None), check_vma=False
    )
```

time: 335 us -> 127 us (0.38)
  blocking collectives: 279 us -> 23.6 us
  starting transfers between devices: 4.46 us -> 44.7 us
  waiting for transfers between devices: 3.48 us -> 28.1 us
  Pallas kernels: 0 us -> 22.7 us
  matrix products: 19.6 us -> 0 us
  local copies, waits for them, and re-layouts: 21.6 us -> 6.69 us
  other arithmetic: 6.57 us -> 0.6 us
    all_to_all x6 -> x2, blocking collectives: 279 us -> 23.6 us  [the longest x1 14.1 us: per_device(): lax.all_to_all(copies, 'cluster', 0, 0, tiled=True, axis_index_groups=Z_R...]
    ppermute x0 -> x28, starting transfers between devices: none -> 44.7 us  [moved(): return lax.ppermute(value, 'cluster', pairs)]
    ppermute x0 -> x28, waiting for transfers between devices: none -> 28.1 us  [moved(): return lax.ppermute(value, 'cluster', pairs)]
    pallas_call x0 -> x7, Pallas kernels: none -> 22.7 us  [the longest x1 5.5 us: second_partials(): pl.pallas_call(second_kernel, grid_spec=pltpu.PrefetchScalarGridSpec(num_...]
    dot_general x4 -> x0, matrix products: 19.6 us -> none  [the longest x3 17.4 us: per_device(): jnp.einsum('rsk,rjk->rsj', rhs, solve_block, preferred_element_type=jnp.f...]
    convert_element_type x6 -> x0, local copies, waits for them, and re-layouts: 17.5 us -> none  [the longest x3 8.87 us: per_device(): share = sent_and_summed(flat.astype(jnp.bfloat16), 'cluster', 0)]
    unnamed x8 -> x53, local copies, waits for them, and re-layouts: 0.02 us -> 4.66 us
    all_to_all x1 -> x0, starting transfers between devices: 4.46 us -> none  [sent_to_all(): return lax.all_to_all(copies, axis, split_axis=0, concat_axis=0, tiled=True)]
  transfers between devices with their start and end apart: 1 -> 28, of which waited for: 1 -> 12; matrix products, arithmetic and copies ran while one was open for 1% -> 0% of each run, Pallas kernels for 0% -> 4%
where the time goes in v1:
time: 127 us
  starting transfers between devices  44.7 us (35%)
  waiting for transfers between devices  28.1 us (22%)
  blocking collectives  23.6 us (19%)
  Pallas kernels  22.7 us (18%)
  local copies, waits for them, and re-layouts  6.69 us (5%)
    ppermute x28, starting transfers between devices, moved(): return lax.ppermute(value, 'cluster', pairs)  44.7 us
    ppermute x28, waiting for transfers between devices, moved(): return lax.ppermute(value, 'cluster', pairs)  28.1 us
    all_to_all x1, blocking collectives, per_device(): lax.all_to_all(copies, 'cluster', 0, 0, tiled=True, axis_index_groups=Z_R...  14.1 us
    all_to_all x1, blocking collectives, per_device(): lax.all_to_all(jnp.broadcast_to(power, (4, 1, 128)), 'sub', 0, 0, tiled=T...  9.49 us
    pallas_call x1, Pallas kernels, second_partials(): pl.pallas_call(second_kernel, grid_spec=pltpu.PrefetchScalarGridSpec(num_...  5.5 us
    pallas_call x1, Pallas kernels, first_partials(): pl.pallas_call(first_kernel, grid=(1,), in_specs=cluster_specs(), out_spe...  5.13 us
    unnamed x53, local copies, waits for them, and re-layouts  4.66 us
    pallas_call x1, Pallas kernels, packed(): pl.pallas_call(pack_kernel, in_specs=[pl.BlockSpec(memory_space=pltpu.SME...  3.56 us
  transfers between devices with their start and end apart: 28, of which 12 were waited for; matrix products, arithmetic and copies ran while one was open for 0% of the time, Pallas kernels for 4%

profile of v1, /device:TPU:2, one launch (start us, length us, event | category | flops | bytes accessed | tf_op | source)
XLA Modules:
  0.0 126.6 jit_solution(13977883741670637875)
XLA Ops:
  2.0 3.6 %shard_map.46 = (bf16[2,552,128]{2,1,0:T(8,128)(2,1)}, bf16[2,552,128]{2,1,0:T(8,128)(2,1)}, bf16[2,552,128]{2,1,0:T(8,128)(2,1)}, bf16[2,552,128]{2,1,0:T(8,128...) custom-call(s32[3]{0:T(128)} %pad_add_fusion.here_ref, ...), custom_call_target="tpu_custom_call" | custom-call | flops 6000000 | bytes 5000000 | tf_op jit(solution)/shard_map/pallas_call | solution.py:71
  9.5 2.1 %collective-permute-start = (bf16[2,552,128]{2,1,0:T(8,128)(2,1)}, bf16[2,552,128]{2,1,0:T(8,128)(2,1)S(1)}, u32[]{:S(2)}, u32[]{:S(2)}) collective-permute-start(bf16[2,552,128]{2,1,0:T(8,128)(2,1)} %get-tuple-element.23), channel_id=1, source_target_pairs={{0,16},{4,20},{8,24},{12,28},{16,0},{20,4},{24,8},{28,12},{32,48},... | collective-permute-start | bytes 847880 | tf_op jit(solution)/shard_map/ppermute | solution.py:42
  11.6 2.6 %collective-permute-done.8.refs_1_ = bf16[2,552,128]{2,1,0:T(8,128)(2,1)S(1)} collective-permute-done((bf16[2,552,128]{2,1,0:T(8,128)(2,1)}, bf16[2,552,128]{2,1,0:T(8,128)(2,1)S(1)}, u32[]{:S(2)}, u32[]{:S(2)}) %collective-permute-start.8) | collective-permute-done | bytes 282656 | tf_op jit(solution)/shard_map/ppermute | solution.py:42
  14.2 4.0 %collective-permute-start.1 = (bf16[2,552,128]{2,1,0:T(8,128)(2,1)}, bf16[2,552,128]{2,1,0:T(8,128)(2,1)S(1)}, u32[]{:S(2)}, u32[]{:S(2)}) collective-permute-start(bf16[2,552,128]{2,1,0:T(8,128)(2,1)} %get-tuple-element.24), channel_id=1, source_target_pairs={{0,40},{4,44},{8,48},{12,52},{16,56},{20,60},{24,32},{28,36},{32,8... | collective-permute-start | bytes 847880 | tf_op jit(solution)/shard_map/ppermute | solution.py:42
  18.2 6.2 %collective-permute-start.2 = (bf16[2,552,128]{2,1,0:T(8,128)(2,1)}, bf16[2,552,128]{2,1,0:T(8,128)(2,1)S(1)}, u32[]{:S(2)}, u32[]{:S(2)}) collective-permute-start(bf16[2,552,128]{2,1,0:T(8,128)(2,1)} %get-tuple-element.25), channel_id=1, source_target_pairs={{0,56},{4,60},{8,32},{12,36},{16,40},{20,44},{24,48},{28,52},{32,2... | collective-permute-start | bytes 847880 | tf_op jit(solution)/shard_map/ppermute | solution.py:42
  24.4 2.7 %collective-permute-start.3 = (bf16[2,552,128]{2,1,0:T(8,128)(2,1)}, bf16[2,552,128]{2,1,0:T(8,128)(2,1)S(1)}, u32[]{:S(2)}, u32[]{:S(2)}) collective-permute-start(bf16[2,552,128]{2,1,0:T(8,128)(2,1)} %get-tuple-element.26), channel_id=1, source_target_pairs={{0,48},{4,52},{8,56},{12,60},{16,32},{20,36},{24,40},{28,44},{32,1... | collective-permute-start | bytes 847880 | tf_op jit(solution)/shard_map/ppermute | solution.py:42
  27.7 5.4 %collective-permute-done.2.refs_2_ = bf16[2,552,128]{2,1,0:T(8,128)(2,1)S(1)} collective-permute-done((bf16[2,552,128]{2,1,0:T(8,128)(2,1)}, bf16[2,552,128]{2,1,0:T(8,128)(2,1)S(1)}, u32[]{:S(2)}, u32[]{:S(2)}) %collective-permute-start.2) | collective-permute-done | bytes 282656 | tf_op jit(solution)/shard_map/ppermute | solution.py:42
  33.1 3.6 %collective-permute-done.3.refs_3_ = bf16[2,552,128]{2,1,0:T(8,128)(2,1)S(1)} collective-permute-done((bf16[2,552,128]{2,1,0:T(8,128)(2,1)}, bf16[2,552,128]{2,1,0:T(8,128)(2,1)S(1)}, u32[]{:S(2)}, u32[]{:S(2)}) %collective-permute-start.3) | collective-permute-done | bytes 282656 | tf_op jit(solution)/shard_map/ppermute | solution.py:42
  37.9 5.1 %shard_map.47 = (f32[192,256]{1,0:T(8,128)}, f32[192,256]{1,0:T(8,128)}, f32[192,256]{1,0:T(8,128)}, f32[256,256]{1,0:T(8,128)}) custom-call(bf16[2,552,128]{2,1,0:T(8,128)(2,1)} %get-tuple-element.27.refs_0_, bf16[2,552,128]{2,1,0:T(8,128)(2,1)} %copy-done.16, bf16[2,552,128]{2,1,0:T(8,128)(2,1)} %copy-done.17, bf16[2,552,128]{2,1,0:T(8,128)(2,1)} %copy-done.19, ...), custom_call_target="tpu_custom_call" | custom-call | flops 2000000000 | bytes 3000000 | tf_op jit(solution)/shard_map/pallas_call | solution.py:149
  43.9 5.5 %shard_map.48 = (bf16[208,256]{1,0:T(8,128)(2,1)}, bf16[208,256]{1,0:T(8,128)(2,1)}, bf16[208,256]{1,0:T(8,128)(2,1)}, bf16[208,256]{1,0:T(8,128)(2,1)}) custom-call(s32[1]{0:T(128)} %bitcast.8.q_ref.quarter_ref, bf16[2,552,128]{2,1,0:T(8,128)(2,1)} %copy-done.14, bf16[2,552,128]{2,1,0:T(8,128)(2,1)} %copy-done.15, bf16[2,552,128]{2,1,0:T(8,128)(2,1)} %copy-done.18, ...), custom_call_target="tpu_custom_call" | custom-call | flops 2000000000 | bytes 3000000 | tf_op jit(solution)/shard_map/pallas_call | solution.py:162
  49.4 7.3 %collective-permute-start.15 = (bf16[208,256]{1,0:T(8,128)(2,1)}, bf16[208,256]{1,0:T(8,128)(2,1)S(1)}, u32[]{:S(2)}, u32[]{:S(2)}) collective-permute-start(bf16[208,256]{1,0:T(8,128)(2,1)} %get-tuple-element.36), channel_id=1, source_target_pairs={{0,128},{4,132},{8,136},{12,140},{16,144},{20,148},{24,152},{28,15... | collective-permute-start | bytes 319496 | tf_op jit(solution)/shard_map/ppermute | solution.py:42
  58.2 2.7 %collective-permute-start.17 = (bf16[208,256]{1,0:T(8,128)(2,1)}, bf16[208,256]{1,0:T(8,128)(2,1)S(1)}, u32[]{:S(2)}, u32[]{:S(2)}) collective-permute-start(bf16[208,256]{1,0:T(8,128)(2,1)} %get-tuple-element.38), channel_id=1, source_target_pairs={{0,192},{4,196},{8,200},{12,204},{16,208},{20,212},{24,216},{28,22... | collective-permute-start | bytes 319496 | tf_op jit(solution)/shard_map/ppermute | solution.py:42
  62.5 3.4 %collective-permute-done.16.refs_2_ = bf16[208,256]{1,0:T(8,128)(2,1)S(1)} collective-permute-done((bf16[208,256]{1,0:T(8,128)(2,1)}, bf16[208,256]{1,0:T(8,128)(2,1)S(1)}, u32[]{:S(2)}, u32[]{:S(2)}) %collective-permute-start.16) | collective-permute-done | bytes 106528 | tf_op jit(solution)/shard_map/ppermute | solution.py:42
  65.8 1.8 %collective-permute-done.17.refs_3_ = bf16[208,256]{1,0:T(8,128)(2,1)S(1)} collective-permute-done((bf16[208,256]{1,0:T(8,128)(2,1)}, bf16[208,256]{1,0:T(8,128)(2,1)S(1)}, u32[]{:S(2)}, u32[]{:S(2)}) %collective-permute-start.17) | collective-permute-done | bytes 106528 | tf_op jit(solution)/shard_map/ppermute | solution.py:42
  68.3 1.8 %shard_map.49 = (f32[144,256]{1,0:T(8,128)}, bf16[64,256]{1,0:T(8,128)(2,1)}) custom-call(bf16[208,256]{1,0:T(8,128)(2,1)} %get-tuple-element.35.refs_0_, bf16[208,256]{1,0:T(8,128)(2,1)} %copy-done.8, bf16[208,256]{1,0:T(8,128)(2,1)} %copy-done.9, bf16[208,256]{1,0:T(8,128)(2,1)} %copy-done.10), custom_call_target="tpu_custom_call" | custom-call | tf_op jit(solution)/shard_map/pallas_call | solution.py:187
  71.5 4.5 %collective-permute-start.19 = (bf16[64,256]{1,0:T(8,128)(2,1)}, bf16[64,256]{1,0:T(8,128)(2,1)S(1)}, u32[]{:S(2)}, u32[]{:S(2)}) collective-permute-start(bf16[64,256]{1,0:T(8,128)(2,1)} %get-tuple-element.40.a0), channel_id=1, source_target_pairs={{0,128},{4,132},{8,136},{12,140},{16,144},{20,148},{24,152},{28,15... | collective-permute-start | bytes 98312 | tf_op jit(solution)/shard_map/ppermute | solution.py:42
  76.0 2.4 %collective-permute-start.20 = (bf16[64,256]{1,0:T(8,128)(2,1)}, bf16[64,256]{1,0:T(8,128)(2,1)S(1)}, u32[]{:S(2)}, u32[]{:S(2)}) collective-permute-start(bf16[64,256]{1,0:T(8,128)(2,1)} %get-tuple-element.40.a0), channel_id=1, source_target_pairs={{0,192},{4,196},{8,200},{12,204},{16,208},{20,212},{24,216},{28,22... | collective-permute-start | bytes 98312 | tf_op jit(solution)/shard_map/ppermute | solution.py:42
  82.0 1.9 %shard_map.50 = bf16[48,256]{1,0:T(8,128)(2,1)} custom-call(s32[1]{0:T(128)} %bitcast.8.q_ref.quarter_ref, f32[144,256]{1,0:T(8,128)} %get-tuple-element.39.p_ref, bf16[64,256]{1,0:T(8,128)(2,1)} %get-tuple-element.40.a0, bf16[64,256]{1,0:T(8,128)(2,1)} %copy-done.11, bf16[64,256]{1,0:T(8,128)(2,1)} %copy-done.12, bf16[64,256]{1,0:T(8,128)(2,1)} %copy-done.13), custom_call_target="tpu_custom_call" | custom-call | tf_op jit(solution)/shard_map/pallas_call | solution.py:217
  84.7 14.1 %all_to_all.10.refs_0_.refs_2_ = bf16[8,48,256]{2,1,0:T(8,128)(2,1)S(1)} all-to-all(bf16[8,48,256]{2,1,0:T(8,128)(2,1)S(1)} %broadcast_in_dim.6), channel_id=1, replica_groups={{0,32,64,96,128,160,192,224},{4,36,68,100,132,164,196,228},{8,40,72,104..., dimensions={0} | all-to-all | bytes 393216 | tf_op jit(solution)/shard_map/all_to_all | solution.py:296
  104.9 2.5 %collective-permute-done.22.refs_2_.refs_4_ = bf16[8,48,256]{2,1,0:T(8,128)(2,1)S(1)} collective-permute-done((bf16[8,48,256]{2,1,0:T(8,128)(2,1)S(1)}, bf16[8,48,256]{2,1,0:T(8,128)(2,1)S(1)}, u32[]{:S(2)}, u32[]{:S(2)}) %collective-permute-start.22) | collective-permute-done | bytes 196640 | tf_op jit(solution)/shard_map/ppermute | solution.py:42
  107.4 2.0 %collective-permute-done.23.refs_3_.refs_5_ = bf16[8,48,256]{2,1,0:T(8,128)(2,1)S(1)} collective-permute-done((bf16[8,48,256]{2,1,0:T(8,128)(2,1)S(1)}, bf16[8,48,256]{2,1,0:T(8,128)(2,1)S(1)}, u32[]{:S(2)}, u32[]{:S(2)}) %collective-permute-start.23) | collective-permute-done | bytes 196640 | tf_op jit(solution)/shard_map/ppermute | solution.py:42
  111.6 2.1 %shard_map.51 = f32[1,128]{1,0:T(1,128)} custom-call(s32[8]{0:T(128)} %stack.47.order_ref.refs_0_, bf16[8,48,256]{2,1,0:T(8,128)(2,1)} %copy-done, bf16[8,48,256]{2,1,0:T(8,128)(2,1)} %copy-done.1, bf16[8,48,256]{2,1,0:T(8,128)(2,1)} %copy-done.2, bf16[8,48,256]{2,1,0:T(8,128)(2,1)} %copy-done.3, bf16[8,48,256]{2,1,0:T(8,128)(2,1)} %copy-done.4, ...), custom_call_target="tpu_custom_call" | custom-call | tf_op jit(solution)/shard_map/pallas_call | solution.py:239
  114.3 9.5 %all_to_all.11.refs_1_ = f32[4,1,128]{2,1,0:T(1,128)} all-to-all(f32[4,1,128]{2,1,0:T(1,128)S(1)} %broadcast_in_dim.7), channel_id=1, replica_groups=mesh['cluster'=64,'sub'=4] {'sub'}, dimensions={0} | all-to-all | bytes 4096 | tf_op jit(solution)/shard_map/all_to_all | solution.py:303
  123.8 2.8 %shard_map.52 = bf16[8,2,168,256]{3,2,1,0:T(8,128)(2,1)} custom-call(s32[8]{0:T(128)} %stack.47.order_ref.refs_0_, f32[4,1,128]{2,1,0:T(1,128)} %all_to_all.11.refs_1_, bf16[8,48,256]{2,1,0:T(8,128)(2,1)} %copy-done, bf16[8,48,256]{2,1,0:T(8,128)(2,1)} %copy-done.1, bf16[8,48,256]{2,1,0:T(8,128)(2,1)} %copy-done.2, bf16[8,48,256]{2,1,0:T(8,128)(2,1)} %copy-done.3, ...), custom_call_target="tpu_custom_call" | custom-call | tf_op jit(solution)/shard_map/pallas_call | solution.py:263
  (98 shorter events, 26.9 us)
Async XLA Ops:
  5.5 8.7 %collective-permute-start.8 = (bf16[2,552,128]{2,1,0:T(8,128)(2,1)}, bf16[2,552,128]{2,1,0:T(8,128)(2,1)S(1)}, u32[]{:S(2)}, u32[]{:S(2)}) collective-permute-start(bf16[2,552,128]{2,1,0:T(8,128)(2,1)} %get-tuple-element.28), channel_id=1, source_target_pairs={{0,8},{4,12},{8,16},{12,20},{16,24},{20,28},{24,0},{28,4},{32,40},... | collective-permute-start | bytes 847880 | tf_op jit(solution)/shard_map/ppermute | solution.py:42
  7.0 11.2 %collective-permute-start.9 = (bf16[2,552,128]{2,1,0:T(8,128)(2,1)}, bf16[2,552,128]{2,1,0:T(8,128)(2,1)S(1)}, u32[]{:S(2)}, u32[]{:S(2)}) collective-permute-start(bf16[2,552,128]{2,1,0:T(8,128)(2,1)} %get-tuple-element.29), channel_id=1, source_target_pairs={{0,24},{4,28},{8,0},{12,4},{16,8},{20,12},{24,16},{28,20},{32,56},... | collective-permute-start | bytes 847880 | tf_op jit(solution)/shard_map/ppermute | solution.py:42
  7.8 16.6 %collective-permute-start.10 = (bf16[2,552,128]{2,1,0:T(8,128)(2,1)}, bf16[2,552,128]{2,1,0:T(8,128)(2,1)S(1)}, u32[]{:S(2)}, u32[]{:S(2)}) collective-permute-start(bf16[2,552,128]{2,1,0:T(8,128)(2,1)} %get-tuple-element.30), channel_id=1, source_target_pairs={{0,32},{4,36},{8,40},{12,44},{16,48},{20,52},{24,56},{28,60},{32,0... | collective-permute-start | bytes 847880 | tf_op jit(solution)/shard_map/ppermute | solution.py:42
  9.5 17.6 %collective-permute-start.11 = (bf16[2,552,128]{2,1,0:T(8,128)(2,1)}, bf16[2,552,128]{2,1,0:T(8,128)(2,1)S(1)}, u32[]{:S(2)}, u32[]{:S(2)}) collective-permute-start(bf16[2,552,128]{2,1,0:T(8,128)(2,1)} %get-tuple-element.27.refs_0_), channel_id=1, source_target_pairs={{0,4},{4,0},{8,12},{12,8},{16,20},{20,16},{24,28},{28,24},{32,36},... | collective-permute-start | bytes 847880 | tf_op jit(solution)/shard_map/ppermute | solution.py:42
  9.5 17.6 %collective-permute-start = (bf16[2,552,128]{2,1,0:T(8,128)(2,1)}, bf16[2,552,128]{2,1,0:T(8,128)(2,1)S(1)}, u32[]{:S(2)}, u32[]{:S(2)}) collective-permute-start(bf16[2,552,128]{2,1,0:T(8,128)(2,1)} %get-tuple-element.23), channel_id=1, source_target_pairs={{0,16},{4,20},{8,24},{12,28},{16,0},{20,4},{24,8},{28,12},{32,48},... | collective-permute-start | bytes 847880 | tf_op jit(solution)/shard_map/ppermute | solution.py:42
  14.2 13.4 %collective-permute-start.1 = (bf16[2,552,128]{2,1,0:T(8,128)(2,1)}, bf16[2,552,128]{2,1,0:T(8,128)(2,1)S(1)}, u32[]{:S(2)}, u32[]{:S(2)}) collective-permute-start(bf16[2,552,128]{2,1,0:T(8,128)(2,1)} %get-tuple-element.24), channel_id=1, source_target_pairs={{0,40},{4,44},{8,48},{12,52},{16,56},{20,60},{24,32},{28,36},{32,8... | collective-permute-start | bytes 847880 | tf_op jit(solution)/shard_map/ppermute | solution.py:42
  18.2 14.9 %collective-permute-start.2 = (bf16[2,552,128]{2,1,0:T(8,128)(2,1)}, bf16[2,552,128]{2,1,0:T(8,128)(2,1)S(1)}, u32[]{:S(2)}, u32[]{:S(2)}) collective-permute-start(bf16[2,552,128]{2,1,0:T(8,128)(2,1)} %get-tuple-element.25), channel_id=1, source_target_pairs={{0,56},{4,60},{8,32},{12,36},{16,40},{20,44},{24,48},{28,52},{32,2... | collective-permute-start | bytes 847880 | tf_op jit(solution)/shard_map/ppermute | solution.py:42
  24.4 12.3 %collective-permute-start.3 = (bf16[2,552,128]{2,1,0:T(8,128)(2,1)}, bf16[2,552,128]{2,1,0:T(8,128)(2,1)S(1)}, u32[]{:S(2)}, u32[]{:S(2)}) collective-permute-start(bf16[2,552,128]{2,1,0:T(8,128)(2,1)} %get-tuple-element.26), channel_id=1, source_target_pairs={{0,48},{4,52},{8,56},{12,60},{16,32},{20,36},{24,40},{28,44},{32,1... | collective-permute-start | bytes 847880 | tf_op jit(solution)/shard_map/ppermute | solution.py:42
  27.1 9.6 %collective-permute-start.12 = (bf16[2,552,128]{2,1,0:T(8,128)(2,1)S(1)}, bf16[2,552,128]{2,1,0:T(8,128)(2,1)S(1)}, u32[]{:S(2)}, u32[]{:S(2)}) collective-permute-start(bf16[2,552,128]{2,1,0:T(8,128)(2,1)S(1)} %collective-permute-done.8.refs_1_), channel_id=1, source_target_pairs={{0,4},{4,0},{8,12},{12,8},{16,20},{20,16},{24,28},{28,24},{32,36},... | collective-permute-start | bytes 847880 | tf_op jit(solution)/shard_map/ppermute | solution.py:42
  27.1 10.1 %collective-permute-start.13 = (bf16[2,552,128]{2,1,0:T(8,128)(2,1)S(1)}, bf16[2,552,128]{2,1,0:T(8,128)(2,1)S(1)}, u32[]{:S(2)}, u32[]{:S(2)}) collective-permute-start(bf16[2,552,128]{2,1,0:T(8,128)(2,1)S(1)} %collective-permute-done.9.refs_2_), channel_id=1, source_target_pairs={{0,4},{4,0},{8,12},{12,8},{16,20},{20,16},{24,28},{28,24},{32,36},... | collective-permute-start | bytes 847880 | tf_op jit(solution)/shard_map/ppermute | solution.py:42
  27.6 9.7 %collective-permute-start.14 = (bf16[2,552,128]{2,1,0:T(8,128)(2,1)S(1)}, bf16[2,552,128]{2,1,0:T(8,128)(2,1)}, u32[]{:S(2)}, u32[]{:S(2)}) collective-permute-start(bf16[2,552,128]{2,1,0:T(8,128)(2,1)S(1)} %collective-permute-done.10.refs_3_), channel_id=1, source_target_pairs={{0,4},{4,0},{8,12},{12,8},{16,20},{20,16},{24,28},{28,24},{32,36},... | collective-permute-start | bytes 847880 | tf_op jit(solution)/shard_map/ppermute | solution.py:42
  33.1 10.0 %collective-permute-start.4 = (bf16[2,552,128]{2,1,0:T(8,128)(2,1)S(1)}, bf16[2,552,128]{2,1,0:T(8,128)(2,1)S(1)}, u32[]{:S(2)}, u32[]{:S(2)}) collective-permute-start(bf16[2,552,128]{2,1,0:T(8,128)(2,1)S(1)} %collective-permute-done.refs_0_), channel_id=1, source_target_pairs={{0,4},{4,0},{8,12},{12,8},{16,20},{20,16},{24,28},{28,24},{32,36},... | collective-permute-start | bytes 847880 | tf_op jit(solution)/shard_map/ppermute | solution.py:42
  36.7 6.4 %collective-permute-start.5 = (bf16[2,552,128]{2,1,0:T(8,128)(2,1)S(1)}, bf16[2,552,128]{2,1,0:T(8,128)(2,1)S(1)}, u32[]{:S(2)}, u32[]{:S(2)}) collective-permute-start(bf16[2,552,128]{2,1,0:T(8,128)(2,1)S(1)} %collective-permute-done.1.refs_1_), channel_id=1, source_target_pairs={{0,4},{4,0},{8,12},{12,8},{16,20},{20,16},{24,28},{28,24},{32,36},... | collective-permute-start | bytes 847880 | tf_op jit(solution)/shard_map/ppermute | solution.py:42
  36.7 6.4 %collective-permute-start.6 = (bf16[2,552,128]{2,1,0:T(8,128)(2,1)S(1)}, bf16[2,552,128]{2,1,0:T(8,128)(2,1)}, u32[]{:S(2)}, u32[]{:S(2)}) collective-permute-start(bf16[2,552,128]{2,1,0:T(8,128)(2,1)S(1)} %collective-permute-done.2.refs_2_), channel_id=1, source_target_pairs={{0,4},{4,0},{8,12},{12,8},{16,20},{20,16},{24,28},{28,24},{32,36},... | collective-permute-start | bytes 847880 | tf_op jit(solution)/shard_map/ppermute | solution.py:42
  37.2 5.9 %collective-permute-start.7 = (bf16[2,552,128]{2,1,0:T(8,128)(2,1)S(1)}, bf16[2,552,128]{2,1,0:T(8,128)(2,1)}, u32[]{:S(2)}, u32[]{:S(2)}) collective-permute-start(bf16[2,552,128]{2,1,0:T(8,128)(2,1)S(1)} %collective-permute-done.3.refs_3_), channel_id=1, source_target_pairs={{0,4},{4,0},{8,12},{12,8},{16,20},{20,16},{24,28},{28,24},{32,36},... | collective-permute-start | bytes 847880 | tf_op jit(solution)/shard_map/ppermute | solution.py:42
  49.4 13.0 %collective-permute-start.15 = (bf16[208,256]{1,0:T(8,128)(2,1)}, bf16[208,256]{1,0:T(8,128)(2,1)S(1)}, u32[]{:S(2)}, u32[]{:S(2)}) collective-permute-start(bf16[208,256]{1,0:T(8,128)(2,1)} %get-tuple-element.36), channel_id=1, source_target_pairs={{0,128},{4,132},{8,136},{12,140},{16,144},{20,148},{24,152},{28,15... | collective-permute-start | bytes 319496 | tf_op jit(solution)/shard_map/ppermute | solution.py:42
  56.7 9.1 %collective-permute-start.16 = (bf16[208,256]{1,0:T(8,128)(2,1)}, bf16[208,256]{1,0:T(8,128)(2,1)S(1)}, u32[]{:S(2)}, u32[]{:S(2)}) collective-permute-start(bf16[208,256]{1,0:T(8,128)(2,1)} %get-tuple-element.37), channel_id=1, source_target_pairs={{0,64},{4,68},{8,72},{12,76},{16,80},{20,84},{24,88},{28,92},{32,9... | collective-permute-start | bytes 319496 | tf_op jit(solution)/shard_map/ppermute | solution.py:42
  58.2 9.4 %collective-permute-start.17 = (bf16[208,256]{1,0:T(8,128)(2,1)}, bf16[208,256]{1,0:T(8,128)(2,1)S(1)}, u32[]{:S(2)}, u32[]{:S(2)}) collective-permute-start(bf16[208,256]{1,0:T(8,128)(2,1)} %get-tuple-element.38), channel_id=1, source_target_pairs={{0,192},{4,196},{8,200},{12,204},{16,208},{20,212},{24,216},{28,22... | collective-permute-start | bytes 319496 | tf_op jit(solution)/shard_map/ppermute | solution.py:42
  70.0 8.4 %collective-permute-start.18 = (bf16[64,256]{1,0:T(8,128)(2,1)}, bf16[64,256]{1,0:T(8,128)(2,1)S(1)}, u32[]{:S(2)}, u32[]{:S(2)}) collective-permute-start(bf16[64,256]{1,0:T(8,128)(2,1)} %get-tuple-element.40.a0), channel_id=1, source_target_pairs={{0,64},{4,68},{8,72},{12,76},{16,80},{20,84},{24,88},{28,92},{32,9... | collective-permute-start | bytes 98312 | tf_op jit(solution)/shard_map/ppermute | solution.py:42
  71.5 8.3 %collective-permute-start.19 = (bf16[64,256]{1,0:T(8,128)(2,1)}, bf16[64,256]{1,0:T(8,128)(2,1)S(1)}, u32[]{:S(2)}, u32[]{:S(2)}) collective-permute-start(bf16[64,256]{1,0:T(8,128)(2,1)} %get-tuple-element.40.a0), channel_id=1, source_target_pairs={{0,128},{4,132},{8,136},{12,140},{16,144},{20,148},{24,152},{28,15... | collective-permute-start | bytes 98312 | tf_op jit(solution)/shard_map/ppermute | solution.py:42
  98.8 6.1 %collective-permute-start.21 = (bf16[8,48,256]{2,1,0:T(8,128)(2,1)S(1)}, bf16[8,48,256]{2,1,0:T(8,128)(2,1)S(1)}, u32[]{:S(2)}, u32[]{:S(2)}) collective-permute-start(bf16[8,48,256]{2,1,0:T(8,128)(2,1)S(1)} %all_to_all.10.refs_0_.refs_2_), channel_id=1, source_target_pairs={{0,8},{4,12},{8,16},{12,20},{16,24},{20,28},{24,0},{28,4},{32,40},... | collective-permute-start | bytes 589832 | tf_op jit(solution)/shard_map/ppermute | solution.py:42
  100.1 7.3 %collective-permute-start.22 = (bf16[8,48,256]{2,1,0:T(8,128)(2,1)S(1)}, bf16[8,48,256]{2,1,0:T(8,128)(2,1)S(1)}, u32[]{:S(2)}, u32[]{:S(2)}) collective-permute-start(bf16[8,48,256]{2,1,0:T(8,128)(2,1)S(1)} %all_to_all.10.refs_0_.refs_2_), channel_id=1, source_target_pairs={{0,16},{4,20},{8,24},{12,28},{16,0},{20,4},{24,8},{28,12},{32,48},... | collective-permute-start | bytes 589832 | tf_op jit(solution)/shard_map/ppermute | solution.py:42
  101.8 7.6 %collective-permute-start.23 = (bf16[8,48,256]{2,1,0:T(8,128)(2,1)S(1)}, bf16[8,48,256]{2,1,0:T(8,128)(2,1)S(1)}, u32[]{:S(2)}, u32[]{:S(2)}) collective-permute-start(bf16[8,48,256]{2,1,0:T(8,128)(2,1)S(1)} %all_to_all.10.refs_0_.refs_2_), channel_id=1, source_target_pairs={{0,24},{4,28},{8,0},{12,4},{16,8},{20,12},{24,16},{28,20},{32,56},... | collective-permute-start | bytes 589832 | tf_op jit(solution)/shard_map/ppermute | solution.py:42
  103.4 6.6 %collective-permute-start.24 = (bf16[8,48,256]{2,1,0:T(8,128)(2,1)S(1)}, bf16[8,48,256]{2,1,0:T(8,128)(2,1)S(1)}, u32[]{:S(2)}, u32[]{:S(2)}) collective-permute-start(bf16[8,48,256]{2,1,0:T(8,128)(2,1)S(1)} %all_to_all.10.refs_0_.refs_2_), channel_id=1, source_target_pairs={{0,4},{4,0},{8,12},{12,8},{16,20},{20,16},{24,28},{28,24},{32,36},... | collective-permute-start | bytes 589832 | tf_op jit(solution)/shard_map/ppermute | solution.py:42
  (30 other events, 169.8 us)

commit v2 on v1

v2 whole, which is shorter than its diff:
```python
import jax
import jax.numpy as jnp
from jax import lax
from jax.experimental import pallas as pl
from jax.experimental.pallas import tpu as pltpu
from jax.sharding import PartitionSpec as P


Z, X, C = 8, 4, 2
CLUSTERS = Z * X * C
ROWS = 42
PART = 48
EARLY = 6
BF, F32 = jnp.bfloat16, jnp.float32


def place(z, x, c):
    return (z * X + x) * C + c


def shifted(dz=0, dx=0, dc=0):
    return [
        (place(z, x, c), place((z + dz) % Z, (x + dx) % X, c ^ dc))
        for z in range(Z)
        for x in range(X)
        for c in range(C)
    ]


def pair_shifted(dx, dp):
    return [
        (place(z, x, c), place(z ^ dp, (x + dx) % X, c))
        for z in range(Z)
        for x in range(X)
        for c in range(C)
    ]


Z_RINGS = [[place(z, x, c) for z in range(Z)] for x in range(X) for c in range(C)]
SLOTS = ((0, 0), (1, 0), (3, 0), (0, 1), (2, 0), (1, 1), (3, 1), (2, 1))


def moved(value, pairs):
    return lax.ppermute(value, "cluster", pairs)


def dot(a, b):
    return jnp.dot(a, b, preferred_element_type=F32)


def complex_square(x, y):
    top = jnp.concatenate([x, y], axis=1)
    return top, jnp.concatenate([top, jnp.concatenate([-y, x], axis=1)], axis=0)


def pack_kernel(here_ref, mant_ref, expo_ref, chan_ref, inv_ref, *outs):
    x, pair, c = here_ref[0], here_ref[1], here_ref[2]
    row = lax.broadcasted_iota(jnp.int32, (168, 14), 0)
    first = lax.broadcasted_iota(jnp.int32, (168, 14), 1) * 12
    inside = ((row >= first) & (row < first + 12)).astype(F32).astype(BF)
    scales = dot(inside, jnp.exp2(expo_ref[...].astype(F32)).astype(BF))
    lane = lax.broadcasted_iota(jnp.int32, (168, 16), 1)
    for out, (dx, dp) in zip(outs, SLOTS):
        for k, side in enumerate((c, 1 - c)):
            r = side * 8 + lax.rem(x + dx, X) * 2 + (1 - pair if dp else pair)
            out[k, 0:256, :] = inv_ref[r]
            out[k, 256:384, :] = chan_ref[r]
            scale = jnp.sum(jnp.where(lane == r, scales, 0.0), axis=1, keepdims=True)
            out[k, 384:552, :] = (mant_ref[r].astype(F32) * scale).astype(BF)


def packed(here, mant, expo, chan, inv):
    vmem = pl.BlockSpec(memory_space=pltpu.VMEM)
    return pl.pallas_call(
        pack_kernel,
        in_specs=[pl.BlockSpec(memory_space=pltpu.SMEM)] + [vmem] * 4,
        out_specs=[vmem] * 8,
        out_shape=[jax.ShapeDtypeStruct((2, 552, 128), BF)] * 8,
        cost_estimate=pl.CostEstimate(flops=6000000, bytes_accessed=5000000, transcendentals=0),
    )(here, mant, expo, chan, inv)


def square_of(raw):
    return complex_square(raw[0:128, :].T, raw[128:256, :].T)


def add_means(raws, av):
    for raw in raws:
        top, square = square_of(raw)
        av[0:128, :] += top.astype(F32)
        av[128:256, :] += dot(top, square)


def add_estimates(raws, p, d, t, av=None):
    sums = None
    for raw in raws:
        top, square = square_of(raw)
        cr, ci = raw[256:320, :], raw[320:384, :]
        match = jnp.concatenate(
            [jnp.concatenate([cr, -ci], axis=1), jnp.concatenate([ci, cr], axis=1)], axis=0
        )
        m = dot(raw[384:552, :], match).astype(BF)
        t1 = dot(m, square)
        t2 = dot(t1.astype(BF), square)
        t3 = dot(t2.astype(BF), square)
        new = (t1, t2, t3) + ((top.astype(F32), dot(top, square)) if av is not None else ())
        sums = new if sums is None else tuple(u + v for u, v in zip(sums, new))
    t1, t2, t3 = sums[:3]
    p[0:168, :] += t1
    d[0:168, :] += t2 - 2.0 * t1
    t[0:168, :] += 3.0 * t1 - 1.5 * t2 + 0.25 * t3
    if av is not None:
        av[0:128, :] += sums[3]
        av[128:256, :] += sums[4]


def early_kernel(*refs):
    raws, (p, d, t, av), held = refs[: 2 * EARLY], refs[2 * EARLY : -1], refs[-1]
    for k, raw in enumerate(raws):
        held[k] = raw[0]
    for ref in (p, d, t, av):
        ref[...] = jnp.zeros_like(ref)

    def two(k, carry):
        add_estimates((held[2 * k], held[2 * k + 1]), p, d, t, av)
        return carry

    lax.fori_loop(0, EARLY, two, 0)


def mean_kernel(*refs):
    raws, before, out, av = refs[:-3], refs[-3], refs[-2], refs[-1]
    av[...] = before[...]
    add_means([raw[0, 0:256, :] for raw in raws], av)
    ones = (
        lax.broadcasted_iota(jnp.int32, (128, 256), 0) == lax.broadcasted_iota(jnp.int32, (128, 256), 1)
    ).astype(F32) * 16.0
    first = av[0:128, :]
    out[0:128, :] = (first - ones).astype(BF)
    out[128:256, :] = (av[128:256, :] - 2.0 * first + ones).astype(BF)


def late_kernel(q_ref, *refs):
    n = 2 * (8 - EARLY)
    raws, before, outs = refs[:n], refs[n : n + 3], refs[n + 3 : n + 7]
    sums, shares = refs[n + 7 : n + 10], refs[n + 10]
    for ref, old in zip(sums, before):
        ref[...] = old[...]
    for k in range(0, n, 2):
        add_estimates((raws[k][0], raws[k + 1][0]), *sums)
    shares[...] = jnp.zeros_like(shares)
    for k, ref in enumerate(sums):
        for part in range(4):
            shares[part, k * PART : k * PART + ROWS, :] = ref[part * ROWS : part * ROWS + ROWS, :]
    for away, out in enumerate(outs):
        out[...] = shares[lax.rem(q_ref[0] + away, 4)].astype(BF)


SUM = (168, 256)
SUMS = (SUM, SUM, SUM, (256, 256))
COST = pl.CostEstimate(flops=2000000000, bytes_accessed=3000000, transcendentals=0)


def cluster_specs(slots):
    own = pl.BlockSpec((1, 552, 128), lambda i, *_: (0, 0, 0))
    other = pl.BlockSpec((1, 552, 128), lambda i, *_: (1, 0, 0))
    return [own, other] * slots


def full(shape):
    return pl.BlockSpec(shape, lambda i, *_: (0,) * len(shape))


def early_sums(raws):
    return pl.pallas_call(
        early_kernel,
        grid=(1,),
        in_specs=cluster_specs(EARLY),
        out_specs=[full(shape) for shape in SUMS],
        out_shape=[jax.ShapeDtypeStruct(shape, F32) for shape in SUMS],
        scratch_shapes=[pltpu.VMEM((2 * EARLY, 552, 128), BF)],
        cost_estimate=COST,
    )(*raws)


def mean_sums(raws, before):
    return pl.pallas_call(
        mean_kernel,
        grid=(1,),
        in_specs=cluster_specs(8 - EARLY) + [full((256, 256))],
        out_specs=full((256, 256)),
        out_shape=jax.ShapeDtypeStruct((256, 256), BF),
        scratch_shapes=[pltpu.VMEM((256, 256), F32)],
        cost_estimate=COST,
    )(*raws, before)


def late_sums(q, raws, before):
    return pl.pallas_call(
        late_kernel,
        grid_spec=pltpu.PrefetchScalarGridSpec(
            num_scalar_prefetch=1,
            grid=(1,),
            in_specs=cluster_specs(8 - EARLY) + [full(SUM)] * 3,
            out_specs=[full((144, 256))] * 4,
            scratch_shapes=[pltpu.VMEM(SUM, F32)] * 3 + [pltpu.VMEM((4, 144, 256), F32)],
        ),
        out_shape=[jax.ShapeDtypeStruct((144, 256), BF)] * 4,
        cost_estimate=COST,
    )(q, *raws, *before)


def dot_wide(a, b):
    high = a.astype(BF)
    low = (a - high.astype(F32)).astype(BF)
    return dot(high, b) + dot(low, b)


def mean_of(parts):
    total = parts[0][...].astype(F32)
    for part in parts[1:]:
        total += part[...].astype(F32)
    return total * (1.0 / CLUSTERS)


def solve_kernel(*refs):
    sums, means, share_ref, power_ref = refs[:4], refs[4:8], refs[8], refs[9]
    total, mean = mean_of(sums), mean_of(means).astype(BF)
    _, first = complex_square(mean[0:128, 0:128], mean[0:128, 128:256])
    _, second = complex_square(mean[128:256, 0:128], mean[128:256, 128:256])
    z1, d, t = total[0:48, :], total[48:96, :], total[96:144, :]
    g = dot_wide(z1, first)
    z3 = t + 1.5 * g - 0.5 * dot_wide(z1, second) + dot_wide(g - 0.5 * d, first)
    share_ref[...] = z3.astype(BF)
    kept = z3.astype(BF).astype(F32)
    power = jnp.sum(kept * kept, axis=0, keepdims=True)
    power_ref[...] = power[:, 0:128] + power[:, 128:256]


def whole(kernel, ins, outs, scratch=()):
    vmem = pl.BlockSpec(memory_space=pltpu.VMEM)
    return pl.pallas_call(
        kernel,
        in_specs=[
            pl.BlockSpec(memory_space=pltpu.SMEM) if value.dtype == jnp.int32 else vmem for value in ins
        ],
        out_specs=jax.tree.map(lambda _: vmem, outs),
        out_shape=outs,
        scratch_shapes=scratch,
    )(*ins)


def solved(sums, means):
    outs = (jax.ShapeDtypeStruct((PART, 256), BF), jax.ShapeDtypeStruct((1, 128), F32))
    return whole(solve_kernel, (*sums, *means), outs)


def copies_kernel(share_ref, p0, p1, p2, p3, out_ref):
    power = p0[...] + p1[...] + p2[...] + p3[...]
    value = share_ref[...].astype(F32)
    row = lax.broadcasted_iota(jnp.int32, (PART, 256), 0)
    for k in range(3):
        term = power.astype(BF).astype(F32)
        power = power - term
        wide = jnp.concatenate([term, jnp.zeros_like(term)], axis=1)
        value = jnp.where(row == ROWS + k, wide, value)
    value = value.astype(BF)
    for k in range(Z):
        out_ref[k] = value


def finish_kernel(vectors, order_ref, *refs):
    parts, out_ref, rows, block = refs[:8], refs[8], refs[9], refs[10]
    for k, part in enumerate(parts):
        power = jnp.zeros((1, 256), F32)
        for zz in range(Z):
            tail = part[zz, 40:48, :].astype(F32)
            power += tail[2:3, :] + tail[3:4, :] + tail[4:5, :]
        rows[order_ref[k]] = power[:, 0:128]
    power = rows[0]
    for k in range(1, 8):
        power += rows[k]
    factor = lax.rsqrt(power * (1.0 / vectors) + 1e-06)
    factor = jnp.concatenate([factor, factor], axis=1)
    for k, part in enumerate(parts):
        for pair in range(2):
            for q in range(4):
                value = part[2 * q + pair].astype(F32) * factor
                block[pair, q * ROWS : q * ROWS + ROWS, :] = value[0:ROWS, :]
            out_ref[order_ref[k], pair] = block[pair].astype(BF)


def finished(order, parts, vectors):
    return whole(
        lambda *refs: finish_kernel(vectors, *refs),
        (order, *parts),
        jax.ShapeDtypeStruct((8, 2, 168, 256), BF),
        (pltpu.VMEM((8, 1, 128), F32), pltpu.VMEM((2, 168, 256), F32)),
    )


def per_device(mantissas, exponents, channel, inverses):
    place_here = lax.axis_index("cluster")
    c = place_here % C
    x = place_here // C % X
    z = place_here // (C * X)
    mant, expo = mantissas[0], exponents[0].T
    blocks, vectors, _ = mant.shape
    here = jnp.stack([x, z % 2, c]).astype(jnp.int32)
    sent = packed(
        here, mant, expo, channel[0].reshape(blocks, 128, 128), inverses[0].reshape(blocks, 256, 128)
    )
    raws = [sent[0]]
    for k in range(1, 8):
        raws.append(moved(sent[k], pair_shifted(*SLOTS[k])))
    swapped = []
    for k in range(8):
        swapped.append(moved(raws[k], shifted(dc=1)))
    q = (z // 2).reshape(1).astype(jnp.int32)
    slots = [part for pair in zip(raws, swapped) for part in pair]
    before = early_sums(slots[: 2 * EARLY])
    means = mean_sums(slots[2 * EARLY :], before[3])
    means = [means, means, means, means]
    for d in (2, 1, 3):
        means[d] = moved(means[0], shifted(dz=2 * d))
    sums = late_sums(q, slots[2 * EARLY :], before[:3])
    sums = [sums[0]] + [moved(sums[d], shifted(dz=2 * d)) for d in (2, 1, 3)]
    share, power = solved(sums, means)
    powers = [power] + [
        lax.ppermute(power, "sub", [(y, (y + d) % 4) for y in range(4)]) for d in (2, 1, 3)
    ]
    copies = whole(copies_kernel, (share, *powers), jax.ShapeDtypeStruct((Z, PART, 256), BF))
    mine = lax.all_to_all(copies, "cluster", 0, 0, tiled=True, axis_index_groups=Z_RINGS)
    same = [mine] + [moved(mine, shifted(dx=d)) for d in (1, 2, 3)]
    other = [moved(value, shifted(dc=1)) for value in same]
    order = jnp.stack(
        [side * X + (x + X - d) % X for side in (c, 1 - c) for d in range(X)]
    ).astype(jnp.int32)
    total = blocks * lax.axis_size("sub") * vectors
    return finished(order, same + other, total).reshape(blocks, vectors, 256)


def solution(mesh):
    placed = (
        P("cluster", "sub", None, None),
        P("cluster", "sub", None),
        P("cluster", "sub", None, None, None),
        P("cluster", "sub", None, None, None),
    )
    return jax.shard_map(
        per_device, mesh=mesh, in_specs=placed, out_specs=P("sub", None, None), check_vma=False
    )
```

time: 127 us -> 124 us (0.976); the launches traced: 127 us -> 122 us
  blocking collectives: 23.6 us -> 13.1 us
  waiting for transfers between devices: 28.1 us -> 37.5 us
  local copies, waits for them, and re-layouts: 6.69 us -> 4.73 us
  starting transfers between devices: 44.7 us -> 43.4 us
    all_to_all x1 -> x0, blocking collectives: 9.49 us -> none  [per_device(): lax.all_to_all(jnp.broadcast_to(power, (4, 1, 128)), 'sub', 0, 0, tiled=T...]
    ppermute x28, starting transfers between devices: 44.7 us -> 37 us  [moved(): return lax.ppermute(value, 'cluster', pairs)]
    ppermute x28, waiting for transfers between devices: 28.1 us -> 35.8 us  [moved(): return lax.ppermute(value, 'cluster', pairs)]
    ppermute x0 -> x3, starting transfers between devices: none -> 6.43 us  [per_device(): lax.ppermute(power, 'sub', [(y, (y + d) % 4) for y in range(4)])]
    ppermute x0 -> x3, waiting for transfers between devices: none -> 1.75 us  [per_device(): lax.ppermute(power, 'sub', [(y, (y + d) % 4) for y in range(4)])]
    broadcast_in_dim x2 -> x0, local copies, waits for them, and re-layouts: 1.41 us -> none  [the longest x1 0.75 us: per_device(): copies = jnp.broadcast_to(share, (Z, PART, 256))]
    unnamed x53 -> x61, local copies, waits for them, and re-layouts: 4.66 us -> 4.06 us
  transfers between devices with their start and end apart: 28 -> 31, of which waited for: 12 -> 13; matrix products, arithmetic and copies ran while one was open for 0% -> 1% of each run, Pallas kernels for 4% -> 7%
where the time goes in v2:
time: 124 us; the launch traced here: 122 us
  starting transfers between devices  43.4 us (35%)
  waiting for transfers between devices  37.5 us (30%)
  Pallas kernels  22.7 us (18%)
  blocking collectives  13.1 us (11%)
  local copies, waits for them, and re-layouts  4.73 us (4%)
    ppermute x28, starting transfers between devices, moved(): return lax.ppermute(value, 'cluster', pairs)  37 us
    ppermute x28, waiting for transfers between devices, moved(): return lax.ppermute(value, 'cluster', pairs)  35.8 us
    all_to_all x1, blocking collectives, per_device(): lax.all_to_all(copies, 'cluster', 0, 0, tiled=True, axis_index_groups=Z_R...  13.1 us
    pallas_call x1, Pallas kernels, early_sums(): pl.pallas_call(early_kernel, grid=(1,), in_specs=cluster_specs(EARLY), ou...  6.84 us
    pallas_call x3, Pallas kernels, whole(): pl.pallas_call(kernel, in_specs=[pl.BlockSpec(memory_space=pltpu.SMEM) if...  6.64 us
    ppermute x3, starting transfers between devices, per_device(): lax.ppermute(power, 'sub', [(y, (y + d) % 4) for y in range(4)])  6.43 us
    unnamed x61, local copies, waits for them, and re-layouts  4.06 us
    pallas_call x1, Pallas kernels, packed(): pl.pallas_call(pack_kernel, in_specs=[pl.BlockSpec(memory_space=pltpu.SME...  3.7 us
  transfers between devices with their start and end apart: 31, of which 13 were waited for; matrix products, arithmetic and copies ran while one was open for 1% of the time, Pallas kernels for 7%

profile of v2, /device:TPU:2, one launch (start us, length us, event | category | flops | bytes accessed | tf_op | source)
XLA Modules:
  0.0 122.2 jit_solution(3671592420697220360)
XLA Ops:
  1.8 3.7 %shard_map.46 = (bf16[2,552,128]{2,1,0:T(8,128)(2,1)}, bf16[2,552,128]{2,1,0:T(8,128)(2,1)}, bf16[2,552,128]{2,1,0:T(8,128)(2,1)}, bf16[2,552,128]{2,1,0:T(8,128...) custom-call(s32[3]{0:T(128)} %pad_add_fusion.here_ref, ...), custom_call_target="tpu_custom_call" | custom-call | flops 6000000 | bytes 5000000 | tf_op jit(solution)/shard_map/pallas_call | solution.py:74
  7.5 2.1 %collective-permute-start.11 = (bf16[2,552,128]{2,1,0:T(8,128)(2,1)}, bf16[2,552,128]{2,1,0:T(8,128)(2,1)S(1)}, u32[]{:S(2)}, u32[]{:S(2)}) collective-permute-start(bf16[2,552,128]{2,1,0:T(8,128)(2,1)} %get-tuple-element.29), channel_id=1, source_target_pairs={{0,16},{4,20},{8,24},{12,28},{16,0},{20,4},{24,8},{28,12},{32,48},... | collective-permute-start | bytes 847880 | tf_op jit(solution)/shard_map/ppermute | solution.py:44
  12.7 2.6 %collective-permute-done.9.refs_6_ = bf16[2,552,128]{2,1,0:T(8,128)(2,1)S(1)} collective-permute-done((bf16[2,552,128]{2,1,0:T(8,128)(2,1)}, bf16[2,552,128]{2,1,0:T(8,128)(2,1)S(1)}, u32[]{:S(2)}, u32[]{:S(2)}) %collective-permute-start.9) | collective-permute-done | bytes 282656 | tf_op jit(solution)/shard_map/ppermute | solution.py:44
  15.4 3.5 %collective-permute-done.11.refs_8_ = bf16[2,552,128]{2,1,0:T(8,128)(2,1)S(1)} collective-permute-done((bf16[2,552,128]{2,1,0:T(8,128)(2,1)}, bf16[2,552,128]{2,1,0:T(8,128)(2,1)S(1)}, u32[]{:S(2)}, u32[]{:S(2)}) %collective-permute-start.11) | collective-permute-done | bytes 282656 | tf_op jit(solution)/shard_map/ppermute | solution.py:44
  18.8 6.2 %collective-permute-start = (bf16[2,552,128]{2,1,0:T(8,128)(2,1)}, bf16[2,552,128]{2,1,0:T(8,128)(2,1)S(1)}, u32[]{:S(2)}, u32[]{:S(2)}) collective-permute-start(bf16[2,552,128]{2,1,0:T(8,128)(2,1)} %get-tuple-element.23), channel_id=1, source_target_pairs={{0,56},{4,60},{8,32},{12,36},{16,40},{20,44},{24,48},{28,52},{32,2... | collective-permute-start | bytes 847880 | tf_op jit(solution)/shard_map/ppermute | solution.py:44
  25.1 4.0 %collective-permute-start.2 = (bf16[2,552,128]{2,1,0:T(8,128)(2,1)}, bf16[2,552,128]{2,1,0:T(8,128)(2,1)S(1)}, u32[]{:S(2)}, u32[]{:S(2)}) collective-permute-start(bf16[2,552,128]{2,1,0:T(8,128)(2,1)} %get-tuple-element.24), channel_id=1, source_target_pairs={{0,48},{4,52},{8,56},{12,60},{16,32},{20,36},{24,40},{28,44},{32,1... | collective-permute-start | bytes 847880 | tf_op jit(solution)/shard_map/ppermute | solution.py:44
  29.0 2.8 %collective-permute-done.5.refs_2_ = bf16[2,552,128]{2,1,0:T(8,128)(2,1)S(1)} collective-permute-done((bf16[2,552,128]{2,1,0:T(8,128)(2,1)}, bf16[2,552,128]{2,1,0:T(8,128)(2,1)S(1)}, u32[]{:S(2)}, u32[]{:S(2)}) %collective-permute-start.5) | collective-permute-done | bytes 282656 | tf_op jit(solution)/shard_map/ppermute | solution.py:44
  33.9 5.4 %collective-permute-done.2.refs_2_ = bf16[2,552,128]{2,1,0:T(8,128)(2,1)S(1)} collective-permute-done((bf16[2,552,128]{2,1,0:T(8,128)(2,1)}, bf16[2,552,128]{2,1,0:T(8,128)(2,1)S(1)}, u32[]{:S(2)}, u32[]{:S(2)}) %collective-permute-start.2) | collective-permute-done | bytes 282656 | tf_op jit(solution)/shard_map/ppermute | solution.py:44
  41.1 6.8 %shard_map.47 = (f32[168,256]{1,0:T(8,128)}, f32[168,256]{1,0:T(8,128)}, f32[168,256]{1,0:T(8,128)}, f32[256,256]{1,0:T(8,128)}) custom-call(bf16[2,552,128]{2,1,0:T(8,128)(2,1)} %get-tuple-element.25.refs_0_, bf16[2,552,128]{2,1,0:T(8,128)(2,1)} %copy-done.24, bf16[2,552,128]{2,1,0:T(8,128)(2,1)} %copy-done.22, ...), custom_call_target="tpu_custom_call" | custom-call | flops 2000000000 | bytes 3000000 | tf_op jit(solution)/shard_map/pallas_call | solution.py:175
  48.7 3.3 %shard_map.48 = (bf16[144,256]{1,0:T(8,128)(2,1)}, bf16[144,256]{1,0:T(8,128)(2,1)}, bf16[144,256]{1,0:T(8,128)(2,1)}, bf16[144,256]{1,0:T(8,128)(2,1)}) custom-call(s32[1]{0:T(128)} %bitcast.8.q_ref, bf16[2,552,128]{2,1,0:T(8,128)(2,1)} %copy-done.18, bf16[2,552,128]{2,1,0:T(8,128)(2,1)} %copy-done.27, bf16[2,552,128]{2,1,0:T(8,128)(2,1)} %copy-done.21, ...), custom_call_target="tpu_custom_call" | custom-call | flops 2000000000 | bytes 3000000 | tf_op jit(solution)/shard_map/pallas_call | solution.py:199
  52.0 5.8 %collective-permute-start.15 = (bf16[144,256]{1,0:T(8,128)(2,1)}, bf16[144,256]{1,0:T(8,128)(2,1)S(1)}, u32[]{:S(2)}, u32[]{:S(2)}) collective-permute-start(bf16[144,256]{1,0:T(8,128)(2,1)} %get-tuple-element.35), channel_id=1, source_target_pairs={{0,128},{4,132},{8,136},{12,140},{16,144},{20,148},{24,152},{28,15... | collective-permute-start | bytes 221192 | tf_op jit(solution)/shard_map/ppermute | solution.py:44
  57.8 2.2 %shard_map.49.refs_4_ = bf16[256,256]{1,0:T(8,128)(2,1)} custom-call(bf16[2,552,128]{2,1,0:T(8,128)(2,1)} %copy-done.18, bf16[2,552,128]{2,1,0:T(8,128)(2,1)} %copy-done.27, bf16[2,552,128]{2,1,0:T(8,128)(2,1)} %copy-done.21, bf16[2,552,128]{2,1,0:T(8,128)(2,1)} %collective-permute-done.3.refs_3_, f32[256,256]{1,0:T(8,128)} %get-tuple-element.38.refs_4_), custom_call_target="tpu_custom_call" | custom-call | flops 2000000000 | bytes 3000000 | tf_op jit(solution)/shard_map/pallas_call | solution.py:187
  63.0 2.1 %collective-permute-start.20 = (bf16[256,256]{1,0:T(8,128)(2,1)}, bf16[256,256]{1,0:T(8,128)(2,1)S(1)}, u32[]{:S(2)}, u32[]{:S(2)}) collective-permute-start(bf16[256,256]{1,0:T(8,128)(2,1)} %shard_map.49.refs_4_), channel_id=1, source_target_pairs={{0,192},{4,196},{8,200},{12,204},{16,208},{20,212},{24,216},{28,22... | collective-permute-start | bytes 393224 | tf_op jit(solution)/shard_map/ppermute | solution.py:44
  66.5 2.8 %collective-permute-start.17 = (bf16[144,256]{1,0:T(8,128)(2,1)S(1)}, bf16[144,256]{1,0:T(8,128)(2,1)S(1)}, u32[]{:S(2)}, u32[]{:S(2)}) collective-permute-start(bf16[144,256]{1,0:T(8,128)(2,1)S(1)} %copy-done.28), channel_id=1, source_target_pairs={{0,192},{4,196},{8,200},{12,204},{16,208},{20,212},{24,216},{28,22... | collective-permute-start | bytes 221192 | tf_op jit(solution)/shard_map/ppermute | solution.py:44
  69.3 7.7 %collective-permute-done.16.refs_2_ = bf16[144,256]{1,0:T(8,128)(2,1)S(1)} collective-permute-done((bf16[144,256]{1,0:T(8,128)(2,1)S(1)}, bf16[144,256]{1,0:T(8,128)(2,1)S(1)}, u32[]{:S(2)}, u32[]{:S(2)}) %collective-permute-start.16) | collective-permute-done | bytes 73760 | tf_op jit(solution)/shard_map/ppermute | solution.py:44
  77.0 4.4 %collective-permute-done.17.refs_3_ = bf16[144,256]{1,0:T(8,128)(2,1)S(1)} collective-permute-done((bf16[144,256]{1,0:T(8,128)(2,1)S(1)}, bf16[144,256]{1,0:T(8,128)(2,1)S(1)}, u32[]{:S(2)}, u32[]{:S(2)}) %collective-permute-start.17) | collective-permute-done | bytes 73760 | tf_op jit(solution)/shard_map/ppermute | solution.py:44
  82.1 2.2 %shard_map.50 = (bf16[48,256]{1,0:T(8,128)(2,1)}, f32[1,128]{1,0:T(1,128)}) custom-call(bf16[144,256]{1,0:T(8,128)(2,1)} %get-tuple-element.34.refs_0_, bf16[144,256]{1,0:T(8,128)(2,1)} %copy-done.11, bf16[144,256]{1,0:T(8,128)(2,1)} %copy-done.12, bf16[144,256]{1,0:T(8,128)(2,1)} %copy-done.13, bf16[256,256]{1,0:T(8,128)(2,1)} %shard_map.49.refs_4_, ...), custom_call_target="tpu_custom_call" | custom-call | tf_op jit(solution)/shard_map/pallas_call | solution.py:242
  84.3 3.2 %collective-permute-start.21 = (f32[1,128]{1,0:T(1,128)}, f32[1,128]{1,0:T(1,128)S(1)}, u32[]{:S(2)}, u32[]{:S(2)}) collective-permute-start(f32[1,128]{1,0:T(1,128)} %get-tuple-element.40.p0), channel_id=1, source_target_pairs={{0,2},{1,3},{2,0},{3,1},{4,6},{5,7},{6,4},{7,5},{8,10},{9,11},{10,... | collective-permute-start | bytes 1544 | tf_op jit(solution)/shard_map/ppermute | solution.py:330
  88.1 2.6 %collective-permute-start.23 = (f32[1,128]{1,0:T(1,128)}, f32[1,128]{1,0:T(1,128)S(1)}, u32[]{:S(2)}, u32[]{:S(2)}) collective-permute-start(f32[1,128]{1,0:T(1,128)} %get-tuple-element.40.p0), channel_id=1, source_target_pairs={{0,3},{1,0},{2,1},{3,2},{4,7},{5,4},{6,5},{7,6},{8,11},{9,8},{10,9... | collective-permute-start | bytes 1544 | tf_op jit(solution)/shard_map/ppermute | solution.py:330
  94.5 13.1 %all_to_all.5.refs_1_ = bf16[8,48,256]{2,1,0:T(8,128)(2,1)S(1)} all-to-all(bf16[8,48,256]{2,1,0:T(8,128)(2,1)} %shard_map.51), channel_id=1, replica_groups={{0,32,64,96,128,160,192,224},{4,36,68,100,132,164,196,228},{8,40,72,104..., dimensions={0} | all-to-all | bytes 393216 | tf_op jit(solution)/shard_map/all_to_all | solution.py:333
  107.6 2.5 %collective-permute-start.25 = (bf16[8,48,256]{2,1,0:T(8,128)(2,1)S(1)}, bf16[8,48,256]{2,1,0:T(8,128)(2,1)S(1)}, u32[]{:S(2)}, u32[]{:S(2)}) collective-permute-start(bf16[8,48,256]{2,1,0:T(8,128)(2,1)S(1)} %all_to_all.5.refs_1_), channel_id=1, source_target_pairs={{0,16},{4,20},{8,24},{12,28},{16,0},{20,4},{24,8},{28,12},{32,48},... | collective-permute-start | bytes 589832 | tf_op jit(solution)/shard_map/ppermute | solution.py:44
  110.9 2.5 %collective-permute-done.24.refs_2_ = bf16[8,48,256]{2,1,0:T(8,128)(2,1)S(1)} collective-permute-done((bf16[8,48,256]{2,1,0:T(8,128)(2,1)S(1)}, bf16[8,48,256]{2,1,0:T(8,128)(2,1)S(1)}, u32[]{:S(2)}, u32[]{:S(2)}) %collective-permute-start.24) | collective-permute-done | bytes 196640 | tf_op jit(solution)/shard_map/ppermute | solution.py:44
  115.0 2.0 %collective-permute-done.26.refs_4_ = bf16[8,48,256]{2,1,0:T(8,128)(2,1)S(1)} collective-permute-done((bf16[8,48,256]{2,1,0:T(8,128)(2,1)S(1)}, bf16[8,48,256]{2,1,0:T(8,128)(2,1)S(1)}, u32[]{:S(2)}, u32[]{:S(2)}) %collective-permute-start.26) | collective-permute-done | bytes 196640 | tf_op jit(solution)/shard_map/ppermute | solution.py:44
  119.2 3.0 %shard_map.52 = bf16[8,2,168,256]{3,2,1,0:T(8,128)(2,1)} custom-call(s32[8]{0:T(128)} %stack.47.refs_0_, bf16[8,48,256]{2,1,0:T(8,128)(2,1)} %copy-done, bf16[8,48,256]{2,1,0:T(8,128)(2,1)} %copy-done.1, bf16[8,48,256]{2,1,0:T(8,128)(2,1)} %copy-done.2, bf16[8,48,256]{2,1,0:T(8,128)(2,1)} %copy-done.3, bf16[8,48,256]{2,1,0:T(8,128)(2,1)} %copy-done.4, ...), custom_call_target="tpu_custom_call" | custom-call | tf_op jit(solution)/shard_map/pallas_call | solution.py:242
  (109 shorter events, 25.6 us)
Async XLA Ops:
  5.5 9.8 %collective-permute-start.9 = (bf16[2,552,128]{2,1,0:T(8,128)(2,1)}, bf16[2,552,128]{2,1,0:T(8,128)(2,1)S(1)}, u32[]{:S(2)}, u32[]{:S(2)}) collective-permute-start(bf16[2,552,128]{2,1,0:T(8,128)(2,1)} %get-tuple-element.28), channel_id=1, source_target_pairs={{0,32},{4,36},{8,40},{12,44},{16,48},{20,52},{24,56},{28,60},{32,0... | collective-permute-start | bytes 847880 | tf_op jit(solution)/shard_map/ppermute | solution.py:44
  7.5 11.4 %collective-permute-start.11 = (bf16[2,552,128]{2,1,0:T(8,128)(2,1)}, bf16[2,552,128]{2,1,0:T(8,128)(2,1)S(1)}, u32[]{:S(2)}, u32[]{:S(2)}) collective-permute-start(bf16[2,552,128]{2,1,0:T(8,128)(2,1)} %get-tuple-element.29), channel_id=1, source_target_pairs={{0,16},{4,20},{8,24},{12,28},{16,0},{20,4},{24,8},{28,12},{32,48},... | collective-permute-start | bytes 847880 | tf_op jit(solution)/shard_map/ppermute | solution.py:44
  9.6 15.5 %collective-permute-start.13 = (bf16[2,552,128]{2,1,0:T(8,128)(2,1)}, bf16[2,552,128]{2,1,0:T(8,128)(2,1)S(1)}, u32[]{:S(2)}, u32[]{:S(2)}) collective-permute-start(bf16[2,552,128]{2,1,0:T(8,128)(2,1)} %get-tuple-element.30), channel_id=1, source_target_pairs={{0,40},{4,44},{8,48},{12,52},{16,56},{20,60},{24,32},{28,36},{32,8... | collective-permute-start | bytes 847880 | tf_op jit(solution)/shard_map/ppermute | solution.py:44
  10.7 21.1 %collective-permute-start.5 = (bf16[2,552,128]{2,1,0:T(8,128)(2,1)}, bf16[2,552,128]{2,1,0:T(8,128)(2,1)S(1)}, u32[]{:S(2)}, u32[]{:S(2)}) collective-permute-start(bf16[2,552,128]{2,1,0:T(8,128)(2,1)} %get-tuple-element.26), channel_id=1, source_target_pairs={{0,8},{4,12},{8,16},{12,20},{16,24},{20,28},{24,0},{28,4},{32,40},... | collective-permute-start | bytes 847880 | tf_op jit(solution)/shard_map/ppermute | solution.py:44
  11.1 20.7 %collective-permute-start.7 = (bf16[2,552,128]{2,1,0:T(8,128)(2,1)}, bf16[2,552,128]{2,1,0:T(8,128)(2,1)S(1)}, u32[]{:S(2)}, u32[]{:S(2)}) collective-permute-start(bf16[2,552,128]{2,1,0:T(8,128)(2,1)} %get-tuple-element.27), channel_id=1, source_target_pairs={{0,24},{4,28},{8,0},{12,4},{16,8},{20,12},{24,16},{28,20},{32,56},... | collective-permute-start | bytes 847880 | tf_op jit(solution)/shard_map/ppermute | solution.py:44
  15.4 16.9 %collective-permute-start.4 = (bf16[2,552,128]{2,1,0:T(8,128)(2,1)}, bf16[2,552,128]{2,1,0:T(8,128)(2,1)S(1)}, u32[]{:S(2)}, u32[]{:S(2)}) collective-permute-start(bf16[2,552,128]{2,1,0:T(8,128)(2,1)} %get-tuple-element.25.refs_0_), channel_id=1, source_target_pairs={{0,4},{4,0},{8,12},{12,8},{16,20},{20,16},{24,28},{28,24},{32,36},... | collective-permute-start | bytes 847880 | tf_op jit(solution)/shard_map/ppermute | solution.py:44
  18.8 15.1 %collective-permute-start = (bf16[2,552,128]{2,1,0:T(8,128)(2,1)}, bf16[2,552,128]{2,1,0:T(8,128)(2,1)S(1)}, u32[]{:S(2)}, u32[]{:S(2)}) collective-permute-start(bf16[2,552,128]{2,1,0:T(8,128)(2,1)} %get-tuple-element.23), channel_id=1, source_target_pairs={{0,56},{4,60},{8,32},{12,36},{16,40},{20,44},{24,48},{28,52},{32,2... | collective-permute-start | bytes 847880 | tf_op jit(solution)/shard_map/ppermute | solution.py:44
  25.1 14.3 %collective-permute-start.2 = (bf16[2,552,128]{2,1,0:T(8,128)(2,1)}, bf16[2,552,128]{2,1,0:T(8,128)(2,1)S(1)}, u32[]{:S(2)}, u32[]{:S(2)}) collective-permute-start(bf16[2,552,128]{2,1,0:T(8,128)(2,1)} %get-tuple-element.24), channel_id=1, source_target_pairs={{0,48},{4,52},{8,56},{12,60},{16,32},{20,36},{24,40},{28,44},{32,1... | collective-permute-start | bytes 847880 | tf_op jit(solution)/shard_map/ppermute | solution.py:44
  31.8 7.6 %collective-permute-start.10 = (bf16[2,552,128]{2,1,0:T(8,128)(2,1)S(1)}, bf16[2,552,128]{2,1,0:T(8,128)(2,1)S(1)}, u32[]{:S(2)}, u32[]{:S(2)}) collective-permute-start(bf16[2,552,128]{2,1,0:T(8,128)(2,1)S(1)} %collective-permute-done.9.refs_6_), channel_id=1, source_target_pairs={{0,4},{4,0},{8,12},{12,8},{16,20},{20,16},{24,28},{28,24},{32,36},... | collective-permute-start | bytes 847880 | tf_op jit(solution)/shard_map/ppermute | solution.py:44
  31.8 8.1 %collective-permute-start.12 = (bf16[2,552,128]{2,1,0:T(8,128)(2,1)S(1)}, bf16[2,552,128]{2,1,0:T(8,128)(2,1)S(1)}, u32[]{:S(2)}, u32[]{:S(2)}) collective-permute-start(bf16[2,552,128]{2,1,0:T(8,128)(2,1)S(1)} %collective-permute-done.11.refs_8_), channel_id=1, source_target_pairs={{0,4},{4,0},{8,12},{12,8},{16,20},{20,16},{24,28},{28,24},{32,36},... | collective-permute-start | bytes 847880 | tf_op jit(solution)/shard_map/ppermute | solution.py:44
  32.3 7.7 %collective-permute-start.14 = (bf16[2,552,128]{2,1,0:T(8,128)(2,1)S(1)}, bf16[2,552,128]{2,1,0:T(8,128)(2,1)}, u32[]{:S(2)}, u32[]{:S(2)}) collective-permute-start(bf16[2,552,128]{2,1,0:T(8,128)(2,1)S(1)} %collective-permute-done.13.refs_10_), channel_id=1, source_target_pairs={{0,4},{4,0},{8,12},{12,8},{16,20},{20,16},{24,28},{28,24},{32,36},... | collective-permute-start | bytes 847880 | tf_op jit(solution)/shard_map/ppermute | solution.py:44
  33.9 6.1 %collective-permute-start.6 = (bf16[2,552,128]{2,1,0:T(8,128)(2,1)S(1)}, bf16[2,552,128]{2,1,0:T(8,128)(2,1)}, u32[]{:S(2)}, u32[]{:S(2)}) collective-permute-start(bf16[2,552,128]{2,1,0:T(8,128)(2,1)S(1)} %collective-permute-done.5.refs_2_), channel_id=1, source_target_pairs={{0,4},{4,0},{8,12},{12,8},{16,20},{20,16},{24,28},{28,24},{32,36},... | collective-permute-start | bytes 847880 | tf_op jit(solution)/shard_map/ppermute | solution.py:44
  39.4 8.6 %collective-permute-start.1 = (bf16[2,552,128]{2,1,0:T(8,128)(2,1)S(1)}, bf16[2,552,128]{2,1,0:T(8,128)(2,1)S(1)}, u32[]{:S(2)}, u32[]{:S(2)}) collective-permute-start(bf16[2,552,128]{2,1,0:T(8,128)(2,1)S(1)} %collective-permute-done.refs_0_), channel_id=1, source_target_pairs={{0,4},{4,0},{8,12},{12,8},{16,20},{20,16},{24,28},{28,24},{32,36},... | collective-permute-start | bytes 847880 | tf_op jit(solution)/shard_map/ppermute | solution.py:44
  39.9 8.1 %collective-permute-start.3 = (bf16[2,552,128]{2,1,0:T(8,128)(2,1)S(1)}, bf16[2,552,128]{2,1,0:T(8,128)(2,1)}, u32[]{:S(2)}, u32[]{:S(2)}) collective-permute-start(bf16[2,552,128]{2,1,0:T(8,128)(2,1)S(1)} %collective-permute-done.2.refs_2_), channel_id=1, source_target_pairs={{0,4},{4,0},{8,12},{12,8},{16,20},{20,16},{24,28},{28,24},{32,36},... | collective-permute-start | bytes 847880 | tf_op jit(solution)/shard_map/ppermute | solution.py:44
  52.0 14.5 %collective-permute-start.15 = (bf16[144,256]{1,0:T(8,128)(2,1)}, bf16[144,256]{1,0:T(8,128)(2,1)S(1)}, u32[]{:S(2)}, u32[]{:S(2)}) collective-permute-start(bf16[144,256]{1,0:T(8,128)(2,1)} %get-tuple-element.35), channel_id=1, source_target_pairs={{0,128},{4,132},{8,136},{12,140},{16,144},{20,148},{24,152},{28,15... | collective-permute-start | bytes 221192 | tf_op jit(solution)/shard_map/ppermute | solution.py:44
  60.0 21.3 %collective-permute-start.18 = (bf16[256,256]{1,0:T(8,128)(2,1)}, bf16[256,256]{1,0:T(8,128)(2,1)S(1)}, u32[]{:S(2)}, u32[]{:S(2)}) collective-permute-start(bf16[256,256]{1,0:T(8,128)(2,1)} %shard_map.49.refs_4_), channel_id=1, source_target_pairs={{0,64},{4,68},{8,72},{12,76},{16,80},{20,84},{24,88},{28,92},{32,9... | collective-permute-start | bytes 393224 | tf_op jit(solution)/shard_map/ppermute | solution.py:44
  61.5 19.8 %collective-permute-start.19 = (bf16[256,256]{1,0:T(8,128)(2,1)}, bf16[256,256]{1,0:T(8,128)(2,1)S(1)}, u32[]{:S(2)}, u32[]{:S(2)}) collective-permute-start(bf16[256,256]{1,0:T(8,128)(2,1)} %shard_map.49.refs_4_), channel_id=1, source_target_pairs={{0,128},{4,132},{8,136},{12,140},{16,144},{20,148},{24,152},{28,15... | collective-permute-start | bytes 393224 | tf_op jit(solution)/shard_map/ppermute | solution.py:44
  63.0 18.4 %collective-permute-start.20 = (bf16[256,256]{1,0:T(8,128)(2,1)}, bf16[256,256]{1,0:T(8,128)(2,1)S(1)}, u32[]{:S(2)}, u32[]{:S(2)}) collective-permute-start(bf16[256,256]{1,0:T(8,128)(2,1)} %shard_map.49.refs_4_), channel_id=1, source_target_pairs={{0,192},{4,196},{8,200},{12,204},{16,208},{20,212},{24,216},{28,22... | collective-permute-start | bytes 393224 | tf_op jit(solution)/shard_map/ppermute | solution.py:44
  65.1 11.9 %collective-permute-start.16 = (bf16[144,256]{1,0:T(8,128)(2,1)S(1)}, bf16[144,256]{1,0:T(8,128)(2,1)S(1)}, u32[]{:S(2)}, u32[]{:S(2)}) collective-permute-start(bf16[144,256]{1,0:T(8,128)(2,1)S(1)} %copy-done.29), channel_id=1, source_target_pairs={{0,64},{4,68},{8,72},{12,76},{16,80},{20,84},{24,88},{28,92},{32,9... | collective-permute-start | bytes 221192 | tf_op jit(solution)/shard_map/ppermute | solution.py:44
  66.5 14.8 %collective-permute-start.17 = (bf16[144,256]{1,0:T(8,128)(2,1)S(1)}, bf16[144,256]{1,0:T(8,128)(2,1)S(1)}, u32[]{:S(2)}, u32[]{:S(2)}) collective-permute-start(bf16[144,256]{1,0:T(8,128)(2,1)S(1)} %copy-done.28), channel_id=1, source_target_pairs={{0,192},{4,196},{8,200},{12,204},{16,208},{20,212},{24,216},{28,22... | collective-permute-start | bytes 221192 | tf_op jit(solution)/shard_map/ppermute | solution.py:44
  84.3 6.4 %collective-permute-start.21 = (f32[1,128]{1,0:T(1,128)}, f32[1,128]{1,0:T(1,128)S(1)}, u32[]{:S(2)}, u32[]{:S(2)}) collective-permute-start(f32[1,128]{1,0:T(1,128)} %get-tuple-element.40.p0), channel_id=1, source_target_pairs={{0,2},{1,3},{2,0},{3,1},{4,6},{5,7},{6,4},{7,5},{8,10},{9,11},{10,... | collective-permute-start | bytes 1544 | tf_op jit(solution)/shard_map/ppermute | solution.py:330
  107.6 7.4 %collective-permute-start.25 = (bf16[8,48,256]{2,1,0:T(8,128)(2,1)S(1)}, bf16[8,48,256]{2,1,0:T(8,128)(2,1)S(1)}, u32[]{:S(2)}, u32[]{:S(2)}) collective-permute-start(bf16[8,48,256]{2,1,0:T(8,128)(2,1)S(1)} %all_to_all.5.refs_1_), channel_id=1, source_target_pairs={{0,16},{4,20},{8,24},{12,28},{16,0},{20,4},{24,8},{28,12},{32,48},... | collective-permute-start | bytes 589832 | tf_op jit(solution)/shard_map/ppermute | solution.py:44
  110.1 6.9 %collective-permute-start.26 = (bf16[8,48,256]{2,1,0:T(8,128)(2,1)S(1)}, bf16[8,48,256]{2,1,0:T(8,128)(2,1)S(1)}, u32[]{:S(2)}, u32[]{:S(2)}) collective-permute-start(bf16[8,48,256]{2,1,0:T(8,128)(2,1)S(1)} %all_to_all.5.refs_1_), channel_id=1, source_target_pairs={{0,24},{4,28},{8,0},{12,4},{16,8},{20,12},{24,16},{28,20},{32,56},... | collective-permute-start | bytes 589832 | tf_op jit(solution)/shard_map/ppermute | solution.py:44
  110.9 6.8 %collective-permute-start.27 = (bf16[8,48,256]{2,1,0:T(8,128)(2,1)S(1)}, bf16[8,48,256]{2,1,0:T(8,128)(2,1)S(1)}, u32[]{:S(2)}, u32[]{:S(2)}) collective-permute-start(bf16[8,48,256]{2,1,0:T(8,128)(2,1)S(1)} %all_to_all.5.refs_1_), channel_id=1, source_target_pairs={{0,4},{4,0},{8,12},{12,8},{16,20},{20,16},{24,28},{28,24},{32,36},... | collective-permute-start | bytes 589832 | tf_op jit(solution)/shard_map/ppermute | solution.py:44
  (37 other events, 207.9 us)

commit v3 on v2

v3 whole, which is shorter than its diff:
```python
import jax
import jax.numpy as jnp
from jax import lax
from jax.experimental import pallas as pl
from jax.experimental.pallas import tpu as pltpu
from jax.sharding import PartitionSpec as P


Z, X, C = 8, 4, 2
CLUSTERS = Z * X * C
ROWS = 176
EARLY = 6
BF, F32 = jnp.bfloat16, jnp.float32


def place(z, x, c):
    return (z * X + x) * C + c


def shifted(dz=0, dx=0, dc=0):
    return [
        (place(z, x, c), place((z + dz) % Z, (x + dx) % X, c ^ dc))
        for z in range(Z)
        for x in range(X)
        for c in range(C)
    ]


def pair_shifted(dx, dp):
    return [
        (place(z, x, c), place(z ^ dp, (x + dx) % X, c))
        for z in range(Z)
        for x in range(X)
        for c in range(C)
    ]


SLOTS = ((0, 0), (1, 0), (3, 0), (0, 1), (2, 0), (1, 1), (3, 1), (2, 1))


def moved(value, pairs):
    return lax.ppermute(value, "cluster", pairs)


def dot(a, b):
    return jnp.dot(a, b, preferred_element_type=F32)


def complex_square(x, y):
    top = jnp.concatenate([x, y], axis=1)
    return top, jnp.concatenate([top, jnp.concatenate([-y, x], axis=1)], axis=0)


def pack_kernel(x_ref, pair_ref, c_ref, mant_ref, expo_ref, chan_ref, inv_ref, *outs):
    x, pair, c = x_ref[0], pair_ref[0], c_ref[0]
    row = lax.broadcasted_iota(jnp.int32, (168, 14), 0)
    first = lax.broadcasted_iota(jnp.int32, (168, 14), 1) * 12
    inside = ((row >= first) & (row < first + 12)).astype(F32).astype(BF)
    expo = jnp.concatenate([expo_ref[t] for t in range(14)], axis=0)
    scales = dot(inside, jnp.exp2(expo.astype(F32)).astype(BF))
    lane = lax.broadcasted_iota(jnp.int32, (168, 16), 1)
    for out, (dx, dp) in zip(outs, SLOTS):
        for k, side in enumerate((c, 1 - c)):
            r = side * 8 + lax.rem(x + dx, X) * 2 + (1 - pair if dp else pair)
            out[k, 0:256, :] = inv_ref[r]
            out[k, 256:384, :] = chan_ref[r]
            scale = jnp.sum(jnp.where(lane == r, scales, 0.0), axis=1, keepdims=True)
            out[k, 384:552, :] = (mant_ref[r].astype(F32) * scale).astype(BF)


def whole(kernel, ins, outs, scratch=(), cost=None):
    vmem = pl.BlockSpec(memory_space=pltpu.VMEM)
    return pl.pallas_call(
        kernel,
        in_specs=[pl.BlockSpec(memory_space=pltpu.SMEM) if value.shape == (1,) else vmem for value in ins],
        out_specs=jax.tree.map(lambda _: vmem, outs),
        out_shape=outs,
        scratch_shapes=scratch,
        cost_estimate=cost,
    )(*ins)


def packed(*ins):
    cost = pl.CostEstimate(flops=6000000, bytes_accessed=5000000, transcendentals=0)
    return whole(pack_kernel, ins, [jax.ShapeDtypeStruct((2, 552, 128), BF)] * 8, cost=cost)


def square_of(raw):
    return complex_square(raw[0:128, :].T, raw[128:256, :].T)


def add_means(raws, av):
    for raw in raws:
        top, square = square_of(raw)
        av[0:128, :] += top.astype(F32)
        av[128:256, :] += dot(top, square)


def add_estimates(raws, p, d, t, av=None):
    sums = None
    for raw in raws:
        top, square = square_of(raw)
        cr, ci = raw[256:320, :], raw[320:384, :]
        match = jnp.concatenate(
            [jnp.concatenate([cr, -ci], axis=1), jnp.concatenate([ci, cr], axis=1)], axis=0
        )
        m = dot(raw[384:552, :], match).astype(BF)
        t1 = dot(m, square)
        t2 = dot(t1.astype(BF), square)
        t3 = dot(t2.astype(BF), square)
        new = (t1, t2, t3) + ((top.astype(F32), dot(top, square)) if av is not None else ())
        sums = new if sums is None else tuple(u + v for u, v in zip(sums, new))
    t1, t2, t3 = sums[:3]
    p[0:168, :] += t1
    d[0:168, :] += t2 - 2.0 * t1
    t[0:168, :] += 3.0 * t1 - 1.5 * t2 + 0.25 * t3
    if av is not None:
        av[0:128, :] += sums[3]
        av[128:256, :] += sums[4]


def early_kernel(*refs):
    raws, (p, d, t, av), held = refs[: 2 * EARLY], refs[2 * EARLY : -1], refs[-1]
    for k, raw in enumerate(raws):
        held[k] = raw[0]
    for ref in (p, d, t, av):
        ref[...] = jnp.zeros_like(ref)

    def two(k, carry):
        add_estimates((held[2 * k], held[2 * k + 1]), p, d, t, av)
        return carry

    lax.fori_loop(0, EARLY, two, 0)


def mean_kernel(*refs):
    raws, before, out, av = refs[:-3], refs[-3], refs[-2], refs[-1]
    av[...] = before[...]
    add_means([raw[0, 0:256, :] for raw in raws], av)
    ones = (
        lax.broadcasted_iota(jnp.int32, (128, 256), 0) == lax.broadcasted_iota(jnp.int32, (128, 256), 1)
    ).astype(F32) * 16.0
    first = av[0:128, :]
    out[0:128, :] = (first - ones).astype(BF)
    out[128:256, :] = (av[128:256, :] - 2.0 * first + ones).astype(BF)


def late_kernel(*refs):
    n = 2 * (8 - EARLY)
    raws, before, sums = refs[:n], refs[n : n + 3], refs[n + 3 :]
    for ref, old in zip(sums, before):
        ref[...] = old[...]
    for k in range(0, n, 2):
        add_estimates((raws[k][0], raws[k + 1][0]), *sums)


SUM = (168, 256)
SUMS = (SUM, SUM, SUM, (256, 256))
COST = pl.CostEstimate(flops=2000000000, bytes_accessed=3000000, transcendentals=0)


def cluster_specs(slots):
    own = pl.BlockSpec((1, 552, 128), lambda i, *_: (0, 0, 0))
    other = pl.BlockSpec((1, 552, 128), lambda i, *_: (1, 0, 0))
    return [own, other] * slots


def full(shape):
    return pl.BlockSpec(shape, lambda i, *_: (0,) * len(shape))


def early_sums(raws):
    return pl.pallas_call(
        early_kernel,
        grid=(1,),
        in_specs=cluster_specs(EARLY),
        out_specs=[full(shape) for shape in SUMS],
        out_shape=[jax.ShapeDtypeStruct(shape, F32) for shape in SUMS],
        scratch_shapes=[pltpu.VMEM((2 * EARLY, 552, 128), BF)],
        cost_estimate=COST,
    )(*raws)


def mean_sums(raws, before):
    return pl.pallas_call(
        mean_kernel,
        grid=(1,),
        in_specs=cluster_specs(8 - EARLY) + [full((256, 256))],
        out_specs=full((256, 256)),
        out_shape=jax.ShapeDtypeStruct((256, 256), BF),
        scratch_shapes=[pltpu.VMEM((256, 256), F32)],
        cost_estimate=COST,
    )(*raws, before)


def late_sums(raws, before):
    return pl.pallas_call(
        late_kernel,
        grid=(1,),
        in_specs=cluster_specs(8 - EARLY) + [full(SUM)] * 3,
        out_specs=[full(SUM)] * 3,
        out_shape=[jax.ShapeDtypeStruct(SUM, F32)] * 3,
        cost_estimate=COST,
    )(*raws, *before)


def dot_wide(a, b):
    high = a.astype(BF)
    low = (a - high.astype(F32)).astype(BF)
    return dot(high, b) + dot(low, b)


def share_kernel(p_ref, d_ref, t_ref, *refs):
    means, out_ref = refs[:4], refs[4]
    mean = means[0][...].astype(F32)
    for part in means[1:]:
        mean += part[...].astype(F32)
    mean = (mean * (1.0 / CLUSTERS)).astype(BF)
    _, first = complex_square(mean[0:128, 0:128], mean[0:128, 128:256])
    _, second = complex_square(mean[128:256, 0:128], mean[128:256, 128:256])
    p = p_ref[...]
    g = dot_wide(p, first)
    share = t_ref[...] + 1.5 * g - 0.5 * dot_wide(p, second) + dot_wide(g - 0.5 * d_ref[...], first)
    out_ref[...] = (share * (1.0 / CLUSTERS)).astype(BF)


def consensus_kernel(s0, s1, s2, s3, out_ref, power_ref):
    even = s0[...].astype(F32) + s2[...].astype(F32)
    odd = s1[...].astype(F32) + s3[...].astype(F32)
    value = (even + odd).astype(BF)
    out_ref[...] = value
    kept = value.astype(F32)
    power = jnp.sum(kept * kept, axis=0, keepdims=True)
    power_ref[...] = power[:, 0:128] + power[:, 128:256]


def tail_kernel(value_ref, p0, p1, p2, p3, out_ref):
    power = (p0[...] + p2[...]) + (p1[...] + p3[...])
    row = lax.broadcasted_iota(jnp.int32, (8, 256), 0)
    tail = jnp.zeros((8, 256), F32)
    for k in range(3):
        term = power.astype(BF).astype(F32)
        power = power - term
        tail = jnp.where(row == k, jnp.concatenate([term, jnp.zeros_like(term)], axis=1), tail)
    out_ref[0:168, :] = value_ref[...]
    out_ref[168:176, :] = tail.astype(BF)


def finish_kernel(vectors, x_ref, pair_ref, c_ref, *refs):
    parts, out_ref, rows = refs[:8], refs[8], refs[9]
    x, pair, c = x_ref[0], pair_ref[0], c_ref[0]
    blocks = [
        side * 8 + lax.rem(x + X - d, X) * 2 + parity
        for side in (c, 1 - c)
        for d in range(X)
        for parity in (pair, 1 - pair)
    ]
    for k in range(16):
        tail = parts[k // 2][k % 2, 168:176, :].astype(F32)
        power = (tail[0:1, :] + tail[1:2, :]) + tail[2:3, :]
        rows[blocks[k]] = power[:, 0:128]
    power = rows[0]
    for k in range(1, 16):
        power += rows[k]
    factor = lax.rsqrt(power * (1.0 / vectors) + 1e-06)
    factor = jnp.concatenate([factor, factor], axis=1)
    for k in range(16):
        value = parts[k // 2][k % 2, 0:168, :].astype(F32) * factor
        out_ref[blocks[k]] = value.astype(BF)


def per_device(mantissas, exponents, channel, inverses):
    place_here = lax.axis_index("cluster")
    c = place_here % C
    x = place_here // C % X
    z = place_here // (C * X)
    mant, expo = mantissas[0], exponents.transpose(2, 0, 1)
    blocks, vectors, _ = mant.shape
    here = tuple(v.reshape(1).astype(jnp.int32) for v in (x, z % 2, c))
    sent = packed(
        *here, mant, expo, channel[0].reshape(blocks, 128, 128), inverses[0].reshape(blocks, 256, 128)
    )
    raws = [sent[0]]
    for k in range(1, 8):
        raws.append(moved(sent[k], pair_shifted(*SLOTS[k])))
    swapped = []
    for k in range(8):
        swapped.append(moved(raws[k], shifted(dc=1)))
    slots = [part for pair in zip(raws, swapped) for part in pair]
    before = early_sums(slots[: 2 * EARLY])
    means = mean_sums(slots[2 * EARLY :], before[3])
    means = [means, means, means, means]
    for d in (2, 1, 3):
        means[d] = moved(means[0], shifted(dz=2 * d))
    sums = late_sums(slots[2 * EARLY :], before[:3])
    share = whole(share_kernel, (*sums, *means), jax.ShapeDtypeStruct(SUM, BF))
    shares = [share, share, share, share]
    for d in (2, 1, 3):
        shares[d] = moved(share, shifted(dz=2 * d))
    value, power = whole(
        consensus_kernel, shares, (jax.ShapeDtypeStruct(SUM, BF), jax.ShapeDtypeStruct((1, 128), F32))
    )
    powers = [power, power, power, power]
    for d in (2, 1, 3):
        powers[d] = lax.ppermute(power, "sub", [(y, (y + d) % 4) for y in range(4)])
    mine = whole(tail_kernel, (value, *powers), jax.ShapeDtypeStruct((ROWS, 256), BF))
    both = jnp.stack([mine, moved(mine, pair_shifted(0, 1))])
    same = [both] + [moved(both, shifted(dx=d)) for d in (1, 2, 3)]
    other = [moved(part, shifted(dc=1)) for part in same]
    total = blocks * lax.axis_size("sub") * vectors
    return whole(
        lambda *refs: finish_kernel(total, *refs),
        (*here, *same, *other),
        jax.ShapeDtypeStruct((blocks, vectors, 256), BF),
        (pltpu.VMEM((16, 1, 128), F32),),
    )


def solution(mesh):
    placed = (
        P("cluster", "sub", None, None),
        P("cluster", "sub", None),
        P("cluster", "sub", None, None, None),
        P("cluster", "sub", None, None, None),
    )
    return jax.shard_map(
        per_device, mesh=mesh, in_specs=placed, out_specs=P("sub", None, None), check_vma=False
    )
```

time: 124 us -> 120 us (0.968)
  blocking collectives: 13.1 us -> 0 us
  waiting for transfers between devices: 37.5 us -> 40.8 us
  starting transfers between devices: 43.4 us -> 46.6 us
  Pallas kernels: 22.7 us -> 24.3 us
    all_to_all x1 -> x0, blocking collectives: 13.1 us -> none  [per_device(): lax.all_to_all(copies, 'cluster', 0, 0, tiled=True, axis_index_groups=Z_R...]
    pallas_call x3 -> x5, Pallas kernels: 6.64 us -> 12.1 us  [whole(): pl.pallas_call(kernel, in_specs=[pl.BlockSpec(memory_space=pltpu.SMEM) if...]
    ppermute x28 -> x29, starting transfers between devices: 37 us -> 40.8 us  [moved(): return lax.ppermute(value, 'cluster', pairs)]
    pallas_call x2 -> x1, Pallas kernels: 6.96 us -> 3.14 us  [late_sums(): pl.pallas_call(late_kernel, grid=(1,), in_specs=cluster_specs(8 - EARLY)...]
    ppermute x28 -> x29, waiting for transfers between devices: 35.8 us -> 38.5 us  [moved(): return lax.ppermute(value, 'cluster', pairs)]
    unnamed x61 -> x62, local copies, waits for them, and re-layouts: 4.06 us -> 5.37 us
  transfers between devices with their start and end apart: 31 -> 32, of which waited for: 13 -> 14; matrix products, arithmetic and copies ran while one was open for 1% -> 0% of each run, Pallas kernels for 7% -> 8%
where the time goes in v3:
time: 120 us; the launch traced here: 118 us
  starting transfers between devices  46.6 us (39%)
  waiting for transfers between devices  40.8 us (34%)
  Pallas kernels  24.3 us (20%)
  local copies, waits for them, and re-layouts  5.37 us (4%)
    ppermute x29, starting transfers between devices, moved(): return lax.ppermute(value, 'cluster', pairs)  40.8 us
    ppermute x29, waiting for transfers between devices, moved(): return lax.ppermute(value, 'cluster', pairs)  38.5 us
    pallas_call x5, Pallas kernels, whole(): pl.pallas_call(kernel, in_specs=[pl.BlockSpec(memory_space=pltpu.SMEM) if...  12.1 us
    pallas_call x1, Pallas kernels, early_sums(): pl.pallas_call(early_kernel, grid=(1,), in_specs=cluster_specs(EARLY), ou...  6.88 us
    ppermute x3, starting transfers between devices, per_device(): powers[d] = lax.ppermute(power, 'sub', [(y, (y + d) % 4) for y in range(4)])  5.81 us
    unnamed x62, local copies, waits for them, and re-layouts  5.37 us
    pallas_call x1, Pallas kernels, late_sums(): pl.pallas_call(late_kernel, grid=(1,), in_specs=cluster_specs(8 - EARLY)...  3.14 us
  transfers between devices with their start and end apart: 32, of which 14 were waited for; matrix products, arithmetic and copies ran while one was open for 0% of the time, Pallas kernels for 8%

profile of v3, /device:TPU:2, one launch (start us, length us, event | category | flops | bytes accessed | tf_op | source)
XLA Modules:
  0.0 118.2 jit_solution(6959022364988382343)
XLA Ops:
  0.0 3.7 %shard_map.46 = (bf16[2,552,128]{2,1,0:T(8,128)(2,1)}, bf16[2,552,128]{2,1,0:T(8,128)(2,1)}, bf16[2,552,128]{2,1,0:T(8,128)(2,1)}, bf16[2,552,128]{2,1,0:T(8,128...) custom-call(s32[1]{0:T(128)} %bitcast.x_ref.refs_0_, ...), custom_call_target="tpu_custom_call" | custom-call | flops 6000000 | bytes 5000000 | tf_op jit(solution)/shard_map/pallas_call | solution.py:73
  10.9 2.6 %collective-permute-done.9.refs_6_ = bf16[2,552,128]{2,1,0:T(8,128)(2,1)S(1)} collective-permute-done((bf16[2,552,128]{2,1,0:T(8,128)(2,1)}, bf16[2,552,128]{2,1,0:T(8,128)(2,1)S(1)}, u32[]{:S(2)}, u32[]{:S(2)}) %collective-permute-start.9) | collective-permute-done | bytes 282656 | tf_op jit(solution)/shard_map/ppermute | solution.py:42
  13.5 3.5 %collective-permute-done.11.refs_8_ = bf16[2,552,128]{2,1,0:T(8,128)(2,1)S(1)} collective-permute-done((bf16[2,552,128]{2,1,0:T(8,128)(2,1)}, bf16[2,552,128]{2,1,0:T(8,128)(2,1)S(1)}, u32[]{:S(2)}, u32[]{:S(2)}) %collective-permute-start.11) | collective-permute-done | bytes 282656 | tf_op jit(solution)/shard_map/ppermute | solution.py:42
  17.0 6.1 %collective-permute-start = (bf16[2,552,128]{2,1,0:T(8,128)(2,1)}, bf16[2,552,128]{2,1,0:T(8,128)(2,1)S(1)}, u32[]{:S(2)}, u32[]{:S(2)}) collective-permute-start(bf16[2,552,128]{2,1,0:T(8,128)(2,1)} %get-tuple-element.22), channel_id=1, source_target_pairs={{0,56},{4,60},{8,32},{12,36},{16,40},{20,44},{24,48},{28,52},{32,2... | collective-permute-start | bytes 847880 | tf_op jit(solution)/shard_map/ppermute | solution.py:42
  23.1 4.0 %collective-permute-start.2 = (bf16[2,552,128]{2,1,0:T(8,128)(2,1)}, bf16[2,552,128]{2,1,0:T(8,128)(2,1)S(1)}, u32[]{:S(2)}, u32[]{:S(2)}) collective-permute-start(bf16[2,552,128]{2,1,0:T(8,128)(2,1)} %get-tuple-element.23), channel_id=1, source_target_pairs={{0,48},{4,52},{8,56},{12,60},{16,32},{20,36},{24,40},{28,44},{32,1... | collective-permute-start | bytes 847880 | tf_op jit(solution)/shard_map/ppermute | solution.py:42
  27.2 7.0 %collective-permute-done.5.refs_2_ = bf16[2,552,128]{2,1,0:T(8,128)(2,1)S(1)} collective-permute-done((bf16[2,552,128]{2,1,0:T(8,128)(2,1)}, bf16[2,552,128]{2,1,0:T(8,128)(2,1)S(1)}, u32[]{:S(2)}, u32[]{:S(2)}) %collective-permute-start.5) | collective-permute-done | bytes 282656 | tf_op jit(solution)/shard_map/ppermute | solution.py:42
  35.2 2.4 %collective-permute-done.2.refs_2_ = bf16[2,552,128]{2,1,0:T(8,128)(2,1)S(1)} collective-permute-done((bf16[2,552,128]{2,1,0:T(8,128)(2,1)}, bf16[2,552,128]{2,1,0:T(8,128)(2,1)S(1)}, u32[]{:S(2)}, u32[]{:S(2)}) %collective-permute-start.2) | collective-permute-done | bytes 282656 | tf_op jit(solution)/shard_map/ppermute | solution.py:42
  39.7 6.9 %shard_map.47 = (f32[168,256]{1,0:T(8,128)}, f32[168,256]{1,0:T(8,128)}, f32[168,256]{1,0:T(8,128)}, f32[256,256]{1,0:T(8,128)}) custom-call(bf16[2,552,128]{2,1,0:T(8,128)(2,1)} %get-tuple-element.24.refs_0_, bf16[2,552,128]{2,1,0:T(8,128)(2,1)} %copy-done.24, bf16[2,552,128]{2,1,0:T(8,128)(2,1)} %copy-done.22, bf16[2,552,128]{2,1,0:T(8,128)(2,1)} %copy-done.30, ...), custom_call_target="tpu_custom_call" | custom-call | flops 2000000000 | bytes 3000000 | tf_op jit(solution)/shard_map/pallas_call | solution.py:173
  47.4 2.2 %shard_map.49.refs_0_ = bf16[256,256]{1,0:T(8,128)(2,1)} custom-call(bf16[2,552,128]{2,1,0:T(8,128)(2,1)} %copy-done.17, bf16[2,552,128]{2,1,0:T(8,128)(2,1)} %copy-done.26, bf16[2,552,128]{2,1,0:T(8,128)(2,1)} %copy-done.20, bf16[2,552,128]{2,1,0:T(8,128)(2,1)} %copy-done.28, f32[256,256]{1,0:T(8,128)} %get-tuple-element.36.refs_4_), custom_call_target="tpu_custom_call" | custom-call | flops 2000000000 | bytes 3000000 | tf_op jit(solution)/shard_map/pallas_call | solution.py:185
  49.6 2.8 %collective-permute-start.15 = (bf16[256,256]{1,0:T(8,128)(2,1)}, bf16[256,256]{1,0:T(8,128)(2,1)S(1)}, u32[]{:S(2)}, u32[]{:S(2)}) collective-permute-start(bf16[256,256]{1,0:T(8,128)(2,1)} %shard_map.49.refs_0_), channel_id=1, source_target_pairs={{0,64},{4,68},{8,72},{12,76},{16,80},{20,84},{24,88},{28,92},{32,9... | collective-permute-start | bytes 393224 | tf_op jit(solution)/shard_map/ppermute | solution.py:42
  52.4 4.5 %collective-permute-start.16 = (bf16[256,256]{1,0:T(8,128)(2,1)}, bf16[256,256]{1,0:T(8,128)(2,1)S(1)}, u32[]{:S(2)}, u32[]{:S(2)}) collective-permute-start(bf16[256,256]{1,0:T(8,128)(2,1)} %shard_map.49.refs_0_), channel_id=1, source_target_pairs={{0,128},{4,132},{8,136},{12,140},{16,144},{20,148},{24,152},{28,15... | collective-permute-start | bytes 393224 | tf_op jit(solution)/shard_map/ppermute | solution.py:42
  56.8 2.7 %collective-permute-start.17 = (bf16[256,256]{1,0:T(8,128)(2,1)}, bf16[256,256]{1,0:T(8,128)(2,1)S(1)}, u32[]{:S(2)}, u32[]{:S(2)}) collective-permute-start(bf16[256,256]{1,0:T(8,128)(2,1)} %shard_map.49.refs_0_), channel_id=1, source_target_pairs={{0,192},{4,196},{8,200},{12,204},{16,208},{20,212},{24,216},{28,22... | collective-permute-start | bytes 393224 | tf_op jit(solution)/shard_map/ppermute | solution.py:42
  59.5 3.1 %shard_map.48 = (f32[168,256]{1,0:T(8,128)}, f32[168,256]{1,0:T(8,128)}, f32[168,256]{1,0:T(8,128)}) custom-call(bf16[2,552,128]{2,1,0:T(8,128)(2,1)} %copy-done.17, bf16[2,552,128]{2,1,0:T(8,128)(2,1)} %copy-done.26, bf16[2,552,128]{2,1,0:T(8,128)(2,1)} %copy-done.20, bf16[2,552,128]{2,1,0:T(8,128)(2,1)} %copy-done.28, ...), custom_call_target="tpu_custom_call" | custom-call | flops 2000000000 | bytes 3000000 | tf_op jit(solution)/shard_map/pallas_call | solution.py:197
  62.7 4.0 %collective-permute-done.16.refs_2_ = bf16[256,256]{1,0:T(8,128)(2,1)S(1)} collective-permute-done((bf16[256,256]{1,0:T(8,128)(2,1)}, bf16[256,256]{1,0:T(8,128)(2,1)S(1)}, u32[]{:S(2)}, u32[]{:S(2)}) %collective-permute-start.16) | collective-permute-done | bytes 131104 | tf_op jit(solution)/shard_map/ppermute | solution.py:42
  66.6 3.1 %collective-permute-done.17.refs_3_ = bf16[256,256]{1,0:T(8,128)(2,1)S(1)} collective-permute-done((bf16[256,256]{1,0:T(8,128)(2,1)}, bf16[256,256]{1,0:T(8,128)(2,1)S(1)}, u32[]{:S(2)}, u32[]{:S(2)}) %collective-permute-start.17) | collective-permute-done | bytes 131104 | tf_op jit(solution)/shard_map/ppermute | solution.py:42
  70.4 2.3 %shard_map.50.s0 = bf16[168,256]{1,0:T(8,128)(2,1)} custom-call(f32[168,256]{1,0:T(8,128)} %get-tuple-element.33.p_ref, f32[168,256]{1,0:T(8,128)} %get-tuple-element.34.d_ref, f32[168,256]{1,0:T(8,128)} %get-tuple-element.35.t_ref, bf16[256,256]{1,0:T(8,128)(2,1)} %shard_map.49.refs_0_, bf16[256,256]{1,0:T(8,128)(2,1)} %copy-done.8, ...), custom_call_target="tpu_custom_call" | custom-call | tf_op jit(solution)/shard_map/pallas_call | solution.py:73
  73.9 4.7 %collective-permute-start.19 = (bf16[168,256]{1,0:T(8,128)(2,1)}, bf16[168,256]{1,0:T(8,128)(2,1)S(1)}, u32[]{:S(2)}, u32[]{:S(2)}) collective-permute-start(bf16[168,256]{1,0:T(8,128)(2,1)} %shard_map.50.s0), channel_id=1, source_target_pairs={{0,128},{4,132},{8,136},{12,140},{16,144},{20,148},{24,152},{28,15... | collective-permute-start | bytes 258056 | tf_op jit(solution)/shard_map/ppermute | solution.py:42
  78.7 2.5 %collective-permute-start.20 = (bf16[168,256]{1,0:T(8,128)(2,1)}, bf16[168,256]{1,0:T(8,128)(2,1)S(1)}, u32[]{:S(2)}, u32[]{:S(2)}) collective-permute-start(bf16[168,256]{1,0:T(8,128)(2,1)} %shard_map.50.s0), channel_id=1, source_target_pairs={{0,192},{4,196},{8,200},{12,204},{16,208},{20,212},{24,216},{28,22... | collective-permute-start | bytes 258056 | tf_op jit(solution)/shard_map/ppermute | solution.py:42
  81.2 4.2 %collective-permute-done.19.s2 = bf16[168,256]{1,0:T(8,128)(2,1)S(1)} collective-permute-done((bf16[168,256]{1,0:T(8,128)(2,1)}, bf16[168,256]{1,0:T(8,128)(2,1)S(1)}, u32[]{:S(2)}, u32[]{:S(2)}) %collective-permute-start.19) | collective-permute-done | bytes 86048 | tf_op jit(solution)/shard_map/ppermute | solution.py:42
  89.9 2.9 %collective-permute-start.22 = (f32[1,128]{1,0:T(1,128)}, f32[1,128]{1,0:T(1,128)S(1)}, u32[]{:S(2)}, u32[]{:S(2)}) collective-permute-start(f32[1,128]{1,0:T(1,128)} %get-tuple-element.38.p0), channel_id=1, source_target_pairs={{0,2},{1,3},{2,0},{3,1},{4,6},{5,7},{6,4},{7,5},{8,10},{9,11},{10,... | collective-permute-start | bytes 1544 | tf_op jit(solution)/shard_map/ppermute | solution.py:305
  98.5 4.7 %collective-permute-done.24 = bf16[176,256]{1,0:T(8,128)(2,1)S(1)} collective-permute-done((bf16[176,256]{1,0:T(8,128)(2,1)}, bf16[176,256]{1,0:T(8,128)(2,1)S(1)}, u32[]{:S(2)}, u32[]{:S(2)}) %collective-permute-start.24) | collective-permute-done | bytes 90144 | tf_op jit(solution)/shard_map/ppermute | solution.py:42
  104.3 2.5 %collective-permute-start.26 = (bf16[2,176,256]{2,1,0:T(8,128)(2,1)S(1)}, bf16[2,176,256]{2,1,0:T(8,128)(2,1)S(1)}, u32[]{:S(2)}, u32[]{:S(2)}) collective-permute-start(bf16[2,176,256]{2,1,0:T(8,128)(2,1)S(1)} %pad_maximum_fusion.refs_3_), channel_id=1, source_target_pairs={{0,16},{4,20},{8,24},{12,28},{16,0},{20,4},{24,8},{28,12},{32,48},... | collective-permute-start | bytes 540680 | tf_op jit(solution)/shard_map/ppermute | solution.py:42
  107.6 2.1 %collective-permute-done.25.refs_4_ = bf16[2,176,256]{2,1,0:T(8,128)(2,1)S(1)} collective-permute-done((bf16[2,176,256]{2,1,0:T(8,128)(2,1)S(1)}, bf16[2,176,256]{2,1,0:T(8,128)(2,1)S(1)}, u32[]{:S(2)}, u32[]{:S(2)}) %collective-permute-start.25) | collective-permute-done | bytes 180256 | tf_op jit(solution)/shard_map/ppermute | solution.py:42
  115.4 2.8 %shard_map.53 = bf16[16,168,256]{2,1,0:T(8,128)(2,1)} custom-call(s32[1]{0:T(128)} %bitcast.x_ref.refs_0_, s32[1]{0:T(128)} %bitcast.1.pair_ref.refs_1_, s32[1]{0:T(128)} %bitcast.2.c_ref.refs_2_, bf16[2,176,256]{2,1,0:T(8,128)(2,1)} %copy-done, bf16[2,176,256]{2,1,0:T(8,128)(2,1)} %copy-done.1, bf16[2,176,256]{2,1,0:T(8,128)(2,1)} %copy-done.2, ...), custom_call_target="tpu_custom_call" | custom-call | tf_op jit(solution)/shard_map/pallas_call | solution.py:73
  (111 shorter events, 30.6 us)
Async XLA Ops:
  3.7 9.8 %collective-permute-start.9 = (bf16[2,552,128]{2,1,0:T(8,128)(2,1)}, bf16[2,552,128]{2,1,0:T(8,128)(2,1)S(1)}, u32[]{:S(2)}, u32[]{:S(2)}) collective-permute-start(bf16[2,552,128]{2,1,0:T(8,128)(2,1)} %get-tuple-element.27), channel_id=1, source_target_pairs={{0,32},{4,36},{8,40},{12,44},{16,48},{20,52},{24,56},{28,60},{32,0... | collective-permute-start | bytes 847880 | tf_op jit(solution)/shard_map/ppermute | solution.py:42
  5.6 11.4 %collective-permute-start.11 = (bf16[2,552,128]{2,1,0:T(8,128)(2,1)}, bf16[2,552,128]{2,1,0:T(8,128)(2,1)S(1)}, u32[]{:S(2)}, u32[]{:S(2)}) collective-permute-start(bf16[2,552,128]{2,1,0:T(8,128)(2,1)} %get-tuple-element.28), channel_id=1, source_target_pairs={{0,16},{4,20},{8,24},{12,28},{16,0},{20,4},{24,8},{28,12},{32,48},... | collective-permute-start | bytes 847880 | tf_op jit(solution)/shard_map/ppermute | solution.py:42
  7.7 15.4 %collective-permute-start.13 = (bf16[2,552,128]{2,1,0:T(8,128)(2,1)}, bf16[2,552,128]{2,1,0:T(8,128)(2,1)S(1)}, u32[]{:S(2)}, u32[]{:S(2)}) collective-permute-start(bf16[2,552,128]{2,1,0:T(8,128)(2,1)} %get-tuple-element.29), channel_id=1, source_target_pairs={{0,40},{4,44},{8,48},{12,52},{16,56},{20,60},{24,32},{28,36},{32,8... | collective-permute-start | bytes 847880 | tf_op jit(solution)/shard_map/ppermute | solution.py:42
  8.9 25.3 %collective-permute-start.5 = (bf16[2,552,128]{2,1,0:T(8,128)(2,1)}, bf16[2,552,128]{2,1,0:T(8,128)(2,1)S(1)}, u32[]{:S(2)}, u32[]{:S(2)}) collective-permute-start(bf16[2,552,128]{2,1,0:T(8,128)(2,1)} %get-tuple-element.25), channel_id=1, source_target_pairs={{0,8},{4,12},{8,16},{12,20},{16,24},{20,28},{24,0},{28,4},{32,40},... | collective-permute-start | bytes 847880 | tf_op jit(solution)/shard_map/ppermute | solution.py:42
  9.3 24.9 %collective-permute-start.7 = (bf16[2,552,128]{2,1,0:T(8,128)(2,1)}, bf16[2,552,128]{2,1,0:T(8,128)(2,1)S(1)}, u32[]{:S(2)}, u32[]{:S(2)}) collective-permute-start(bf16[2,552,128]{2,1,0:T(8,128)(2,1)} %get-tuple-element.26), channel_id=1, source_target_pairs={{0,24},{4,28},{8,0},{12,4},{16,8},{20,12},{24,16},{28,20},{32,56},... | collective-permute-start | bytes 847880 | tf_op jit(solution)/shard_map/ppermute | solution.py:42
  13.5 21.1 %collective-permute-start.4 = (bf16[2,552,128]{2,1,0:T(8,128)(2,1)}, bf16[2,552,128]{2,1,0:T(8,128)(2,1)S(1)}, u32[]{:S(2)}, u32[]{:S(2)}) collective-permute-start(bf16[2,552,128]{2,1,0:T(8,128)(2,1)} %get-tuple-element.24.refs_0_), channel_id=1, source_target_pairs={{0,4},{4,0},{8,12},{12,8},{16,20},{20,16},{24,28},{28,24},{32,36},... | collective-permute-start | bytes 847880 | tf_op jit(solution)/shard_map/ppermute | solution.py:42
  17.0 17.8 %collective-permute-start = (bf16[2,552,128]{2,1,0:T(8,128)(2,1)}, bf16[2,552,128]{2,1,0:T(8,128)(2,1)S(1)}, u32[]{:S(2)}, u32[]{:S(2)}) collective-permute-start(bf16[2,552,128]{2,1,0:T(8,128)(2,1)} %get-tuple-element.22), channel_id=1, source_target_pairs={{0,56},{4,60},{8,32},{12,36},{16,40},{20,44},{24,48},{28,52},{32,2... | collective-permute-start | bytes 847880 | tf_op jit(solution)/shard_map/ppermute | solution.py:42
  23.1 14.4 %collective-permute-start.2 = (bf16[2,552,128]{2,1,0:T(8,128)(2,1)}, bf16[2,552,128]{2,1,0:T(8,128)(2,1)S(1)}, u32[]{:S(2)}, u32[]{:S(2)}) collective-permute-start(bf16[2,552,128]{2,1,0:T(8,128)(2,1)} %get-tuple-element.23), channel_id=1, source_target_pairs={{0,48},{4,52},{8,56},{12,60},{16,32},{20,36},{24,40},{28,44},{32,1... | collective-permute-start | bytes 847880 | tf_op jit(solution)/shard_map/ppermute | solution.py:42
  34.1 3.9 %collective-permute-start.12 = (bf16[2,552,128]{2,1,0:T(8,128)(2,1)S(1)}, bf16[2,552,128]{2,1,0:T(8,128)(2,1)S(1)}, u32[]{:S(2)}, u32[]{:S(2)}) collective-permute-start(bf16[2,552,128]{2,1,0:T(8,128)(2,1)S(1)} %collective-permute-done.11.refs_8_), channel_id=1, source_target_pairs={{0,4},{4,0},{8,12},{12,8},{16,20},{20,16},{24,28},{28,24},{32,36},... | collective-permute-start | bytes 847880 | tf_op jit(solution)/shard_map/ppermute | solution.py:42
  37.5 9.0 %collective-permute-start.1 = (bf16[2,552,128]{2,1,0:T(8,128)(2,1)S(1)}, bf16[2,552,128]{2,1,0:T(8,128)(2,1)S(1)}, u32[]{:S(2)}, u32[]{:S(2)}) collective-permute-start(bf16[2,552,128]{2,1,0:T(8,128)(2,1)S(1)} %collective-permute-done.refs_0_), channel_id=1, source_target_pairs={{0,4},{4,0},{8,12},{12,8},{16,20},{20,16},{24,28},{28,24},{32,36},... | collective-permute-start | bytes 847880 | tf_op jit(solution)/shard_map/ppermute | solution.py:42
  38.0 8.5 %collective-permute-start.3 = (bf16[2,552,128]{2,1,0:T(8,128)(2,1)S(1)}, bf16[2,552,128]{2,1,0:T(8,128)(2,1)S(1)}, u32[]{:S(2)}, u32[]{:S(2)}) collective-permute-start(bf16[2,552,128]{2,1,0:T(8,128)(2,1)S(1)} %collective-permute-done.2.refs_2_), channel_id=1, source_target_pairs={{0,4},{4,0},{8,12},{12,8},{16,20},{20,16},{24,28},{28,24},{32,36},... | collective-permute-start | bytes 847880 | tf_op jit(solution)/shard_map/ppermute | solution.py:42
  49.6 13.1 %collective-permute-start.15 = (bf16[256,256]{1,0:T(8,128)(2,1)}, bf16[256,256]{1,0:T(8,128)(2,1)S(1)}, u32[]{:S(2)}, u32[]{:S(2)}) collective-permute-start(bf16[256,256]{1,0:T(8,128)(2,1)} %shard_map.49.refs_0_), channel_id=1, source_target_pairs={{0,64},{4,68},{8,72},{12,76},{16,80},{20,84},{24,88},{28,92},{32,9... | collective-permute-start | bytes 393224 | tf_op jit(solution)/shard_map/ppermute | solution.py:42
  52.4 14.2 %collective-permute-start.16 = (bf16[256,256]{1,0:T(8,128)(2,1)}, bf16[256,256]{1,0:T(8,128)(2,1)S(1)}, u32[]{:S(2)}, u32[]{:S(2)}) collective-permute-start(bf16[256,256]{1,0:T(8,128)(2,1)} %shard_map.49.refs_0_), channel_id=1, source_target_pairs={{0,128},{4,132},{8,136},{12,140},{16,144},{20,148},{24,152},{28,15... | collective-permute-start | bytes 393224 | tf_op jit(solution)/shard_map/ppermute | solution.py:42
  56.8 12.9 %collective-permute-start.17 = (bf16[256,256]{1,0:T(8,128)(2,1)}, bf16[256,256]{1,0:T(8,128)(2,1)S(1)}, u32[]{:S(2)}, u32[]{:S(2)}) collective-permute-start(bf16[256,256]{1,0:T(8,128)(2,1)} %shard_map.49.refs_0_), channel_id=1, source_target_pairs={{0,192},{4,196},{8,200},{12,204},{16,208},{20,212},{24,216},{28,22... | collective-permute-start | bytes 393224 | tf_op jit(solution)/shard_map/ppermute | solution.py:42
  72.7 8.5 %collective-permute-start.18 = (bf16[168,256]{1,0:T(8,128)(2,1)}, bf16[168,256]{1,0:T(8,128)(2,1)S(1)}, u32[]{:S(2)}, u32[]{:S(2)}) collective-permute-start(bf16[168,256]{1,0:T(8,128)(2,1)} %shard_map.50.s0), channel_id=1, source_target_pairs={{0,64},{4,68},{8,72},{12,76},{16,80},{20,84},{24,88},{28,92},{32,9... | collective-permute-start | bytes 258056 | tf_op jit(solution)/shard_map/ppermute | solution.py:42
  73.9 11.4 %collective-permute-start.19 = (bf16[168,256]{1,0:T(8,128)(2,1)}, bf16[168,256]{1,0:T(8,128)(2,1)S(1)}, u32[]{:S(2)}, u32[]{:S(2)}) collective-permute-start(bf16[168,256]{1,0:T(8,128)(2,1)} %shard_map.50.s0), channel_id=1, source_target_pairs={{0,128},{4,132},{8,136},{12,140},{16,144},{20,148},{24,152},{28,15... | collective-permute-start | bytes 258056 | tf_op jit(solution)/shard_map/ppermute | solution.py:42
  78.7 6.7 %collective-permute-start.20 = (bf16[168,256]{1,0:T(8,128)(2,1)}, bf16[168,256]{1,0:T(8,128)(2,1)S(1)}, u32[]{:S(2)}, u32[]{:S(2)}) collective-permute-start(bf16[168,256]{1,0:T(8,128)(2,1)} %shard_map.50.s0), channel_id=1, source_target_pairs={{0,192},{4,196},{8,200},{12,204},{16,208},{20,212},{24,216},{28,22... | collective-permute-start | bytes 258056 | tf_op jit(solution)/shard_map/ppermute | solution.py:42
  88.4 5.8 %collective-permute-start.21 = (f32[1,128]{1,0:T(1,128)}, f32[1,128]{1,0:T(1,128)S(1)}, u32[]{:S(2)}, u32[]{:S(2)}) collective-permute-start(f32[1,128]{1,0:T(1,128)} %get-tuple-element.38.p0), channel_id=1, source_target_pairs={{0,1},{1,2},{2,3},{3,0},{4,5},{5,6},{6,7},{7,4},{8,9},{9,10},{10,1... | collective-permute-start | bytes 1544 | tf_op jit(solution)/shard_map/ppermute | solution.py:305
  89.9 5.1 %collective-permute-start.22 = (f32[1,128]{1,0:T(1,128)}, f32[1,128]{1,0:T(1,128)S(1)}, u32[]{:S(2)}, u32[]{:S(2)}) collective-permute-start(f32[1,128]{1,0:T(1,128)} %get-tuple-element.38.p0), channel_id=1, source_target_pairs={{0,2},{1,3},{2,0},{3,1},{4,6},{5,7},{6,4},{7,5},{8,10},{9,11},{10,... | collective-permute-start | bytes 1544 | tf_op jit(solution)/shard_map/ppermute | solution.py:305
  98.5 4.7 %collective-permute-start.24 = (bf16[176,256]{1,0:T(8,128)(2,1)}, bf16[176,256]{1,0:T(8,128)(2,1)S(1)}, u32[]{:S(2)}, u32[]{:S(2)}) collective-permute-start(bf16[176,256]{1,0:T(8,128)(2,1)} %shard_map.52), channel_id=1, source_target_pairs={{0,32},{4,36},{8,40},{12,44},{16,48},{20,52},{24,56},{28,60},{32,0... | collective-permute-start | bytes 270344 | tf_op jit(solution)/shard_map/ppermute | solution.py:42
  104.2 5.6 %collective-permute-start.25 = (bf16[2,176,256]{2,1,0:T(8,128)(2,1)S(1)}, bf16[2,176,256]{2,1,0:T(8,128)(2,1)S(1)}, u32[]{:S(2)}, u32[]{:S(2)}) collective-permute-start(bf16[2,176,256]{2,1,0:T(8,128)(2,1)S(1)} %pad_maximum_fusion.refs_3_), channel_id=1, source_target_pairs={{0,8},{4,12},{8,16},{12,20},{16,24},{20,28},{24,0},{28,4},{32,40},... | collective-permute-start | bytes 540680 | tf_op jit(solution)/shard_map/ppermute | solution.py:42
  104.3 7.2 %collective-permute-start.26 = (bf16[2,176,256]{2,1,0:T(8,128)(2,1)S(1)}, bf16[2,176,256]{2,1,0:T(8,128)(2,1)S(1)}, u32[]{:S(2)}, u32[]{:S(2)}) collective-permute-start(bf16[2,176,256]{2,1,0:T(8,128)(2,1)S(1)} %pad_maximum_fusion.refs_3_), channel_id=1, source_target_pairs={{0,16},{4,20},{8,24},{12,28},{16,0},{20,4},{24,8},{28,12},{32,48},... | collective-permute-start | bytes 540680 | tf_op jit(solution)/shard_map/ppermute | solution.py:42
  106.8 6.5 %collective-permute-start.27 = (bf16[2,176,256]{2,1,0:T(8,128)(2,1)S(1)}, bf16[2,176,256]{2,1,0:T(8,128)(2,1)S(1)}, u32[]{:S(2)}, u32[]{:S(2)}) collective-permute-start(bf16[2,176,256]{2,1,0:T(8,128)(2,1)S(1)} %pad_maximum_fusion.refs_3_), channel_id=1, source_target_pairs={{0,24},{4,28},{8,0},{12,4},{16,8},{20,12},{24,16},{28,20},{32,56},... | collective-permute-start | bytes 540680 | tf_op jit(solution)/shard_map/ppermute | solution.py:42
  107.6 5.7 %collective-permute-start.28 = (bf16[2,176,256]{2,1,0:T(8,128)(2,1)S(1)}, bf16[2,176,256]{2,1,0:T(8,128)(2,1)S(1)}, u32[]{:S(2)}, u32[]{:S(2)}) collective-permute-start(bf16[2,176,256]{2,1,0:T(8,128)(2,1)S(1)} %pad_maximum_fusion.refs_3_), channel_id=1, source_target_pairs={{0,4},{4,0},{8,12},{12,8},{16,20},{20,16},{24,28},{28,24},{32,36},... | collective-permute-start | bytes 540680 | tf_op jit(solution)/shard_map/ppermute | solution.py:42
  (39 other events, 177.1 us)

commit v4 on v3

--- a/solution.py
+++ b/solution.py
@@ -10,6 +10,7 @@
 CLUSTERS = Z * X * C
 ROWS = 176
 EARLY = 6
+ROOM = 16 * 1024 * 1024
 BF, F32 = jnp.bfloat16, jnp.float32
 
 
@@ -68,21 +69,32 @@
             out[k, 384:552, :] = (mant_ref[r].astype(F32) * scale).astype(BF)
 
 
-def whole(kernel, ins, outs, scratch=(), cost=None):
+def near(shape, dtype):
+    return pltpu.VMEM(shape, dtype)
+
+
+def whole(kernel, ins, outs, scratch=(), cost=None, fetched=False):
     vmem = pl.BlockSpec(memory_space=pltpu.VMEM)
+    scalar = [value.shape == (1,) for value in ins]
+    if not fetched:
+        ins = [
+            value if small else pltpu.with_memory_space_constraint(value, pltpu.VMEM)
+            for value, small in zip(ins, scalar)
+        ]
     return pl.pallas_call(
         kernel,
-        in_specs=[pl.BlockSpec(memory_space=pltpu.SMEM) if value.shape == (1,) else vmem for value in ins],
-        out_specs=jax.tree.map(lambda _: vmem, outs),
+        in_specs=[pl.BlockSpec(memory_space=pltpu.SMEM) if small else vmem for small in scalar],
+        out_specs=[vmem] * len(outs) if isinstance(outs, list) else vmem,
         out_shape=outs,
         scratch_shapes=scratch,
         cost_estimate=cost,
+        compiler_params=pltpu.CompilerParams(vmem_limit_bytes=ROOM),
     )(*ins)
 
 
 def packed(*ins):
     cost = pl.CostEstimate(flops=6000000, bytes_accessed=5000000, transcendentals=0)
-    return whole(pack_kernel, ins, [jax.ShapeDtypeStruct((2, 552, 128), BF)] * 8, cost=cost)
+    return whole(pack_kernel, ins, [near((2, 552, 128), BF)] * 8, cost=cost, fetched=True)
 
 
 def square_of(raw):
@@ -122,7 +134,7 @@
 def early_kernel(*refs):
     raws, (p, d, t, av), held = refs[: 2 * EARLY], refs[2 * EARLY : -1], refs[-1]
     for k, raw in enumerate(raws):
-        held[k] = raw[0]
+        held[k] = raw[k % 2]
     for ref in (p, d, t, av):
         ref[...] = jnp.zeros_like(ref)
 
@@ -136,7 +148,7 @@
 def mean_kernel(*refs):
     raws, before, out, av = refs[:-3], refs[-3], refs[-2], refs[-1]
     av[...] = before[...]
-    add_means([raw[0, 0:256, :] for raw in raws], av)
+    add_means([raw[k % 2, 0:256, :] for k, raw in enumerate(raws)], av)
     ones = (
         lax.broadcasted_iota(jnp.int32, (128, 256), 0) == lax.broadcasted_iota(jnp.int32, (128, 256), 1)
     ).astype(F32) * 16.0
@@ -151,7 +163,7 @@
     for ref, old in zip(sums, before):
         ref[...] = old[...]
     for k in range(0, n, 2):
-        add_estimates((raws[k][0], raws[k + 1][0]), *sums)
+        add_estimates((raws[k][0], raws[k + 1][1]), *sums)
 
 
 SUM = (168, 256)
@@ -159,49 +171,18 @@
 COST = pl.CostEstimate(flops=2000000000, bytes_accessed=3000000, transcendentals=0)
 
 
-def cluster_specs(slots):
-    own = pl.BlockSpec((1, 552, 128), lambda i, *_: (0, 0, 0))
-    other = pl.BlockSpec((1, 552, 128), lambda i, *_: (1, 0, 0))
-    return [own, other] * slots
-
-
-def full(shape):
-    return pl.BlockSpec(shape, lambda i, *_: (0,) * len(shape))
-
-
 def early_sums(raws):
-    return pl.pallas_call(
-        early_kernel,
-        grid=(1,),
-        in_specs=cluster_specs(EARLY),
-        out_specs=[full(shape) for shape in SUMS],
-        out_shape=[jax.ShapeDtypeStruct(shape, F32) for shape in SUMS],
-        scratch_shapes=[pltpu.VMEM((2 * EARLY, 552, 128), BF)],
-        cost_estimate=COST,
-    )(*raws)
+    scratch = [pltpu.VMEM((2 * EARLY, 552, 128), BF)]
+    return whole(early_kernel, raws, [near(shape, F32) for shape in SUMS], scratch, COST)
 
 
 def mean_sums(raws, before):
-    return pl.pallas_call(
-        mean_kernel,
-        grid=(1,),
-        in_specs=cluster_specs(8 - EARLY) + [full((256, 256))],
-        out_specs=full((256, 256)),
-        out_shape=jax.ShapeDtypeStruct((256, 256), BF),
-        scratch_shapes=[pltpu.VMEM((256, 256), F32)],
-        cost_estimate=COST,
-    )(*raws, before)
+    scratch = [pltpu.VMEM((256, 256), F32)]
+    return whole(mean_kernel, [*raws, before], near((256, 256), BF), scratch, COST)
 
 
 def late_sums(raws, before):
-    return pl.pallas_call(
-        late_kernel,
-        grid=(1,),
-        in_specs=cluster_specs(8 - EARLY) + [full(SUM)] * 3,
-        out_specs=[full(SUM)] * 3,
-        out_shape=[jax.ShapeDtypeStruct(SUM, F32)] * 3,
-        cost_estimate=COST,
-    )(*raws, *before)
+    return whole(late_kernel, [*raws, *before], [near(SUM, F32)] * 3, cost=COST)
 
 
 def dot_wide(a, b):
@@ -293,17 +274,15 @@
     for d in (2, 1, 3):
         means[d] = moved(means[0], shifted(dz=2 * d))
     sums = late_sums(slots[2 * EARLY :], before[:3])
-    share = whole(share_kernel, (*sums, *means), jax.ShapeDtypeStruct(SUM, BF))
+    share = whole(share_kernel, (*sums, *means), near(SUM, BF))
     shares = [share, share, share, share]
     for d in (2, 1, 3):
         shares[d] = moved(share, shifted(dz=2 * d))
-    value, power = whole(
-        consensus_kernel, shares, (jax.ShapeDtypeStruct(SUM, BF), jax.ShapeDtypeStruct((1, 128), F32))
-    )
+    value, power = whole(consensus_kernel, shares, [near(SUM, BF), near((1, 128), F32)])
     powers = [power, power, power, power]
     for d in (2, 1, 3):
         powers[d] = lax.ppermute(power, "sub", [(y, (y + d) % 4) for y in range(4)])
-    mine = whole(tail_kernel, (value, *powers), jax.ShapeDtypeStruct((ROWS, 256), BF))
+    mine = whole(tail_kernel, (value, *powers), near((ROWS, 256), BF))
     both = jnp.stack([mine, moved(mine, pair_shifted(0, 1))])
     same = [both] + [moved(both, shifted(dx=d)) for d in (1, 2, 3)]
     other = [moved(part, shifted(dc=1)) for part in same]

time: 120 us -> 104 us (0.87)
  Pallas kernels: 24.3 us -> 8.57 us
  waiting for transfers between devices: 40.8 us -> 42.7 us
    pallas_call x3 -> x0, Pallas kernels: 12.2 us -> none  [the longest x1 6.88 us: early_sums(): pl.pallas_call(early_kernel, grid=(1,), in_specs=cluster_specs(EARLY), ou...]
    pallas_call x5 -> x8, Pallas kernels: 12.1 us -> 8.57 us  [whole(): pl.pallas_call(kernel, in_specs=[pl.BlockSpec(memory_space=pltpu.SMEM) if...]
    ppermute x29, waiting for transfers between devices: 38.5 us -> 40.5 us  [moved(): return lax.ppermute(value, 'cluster', pairs)]
    unnamed x62 -> x8, local copies, waits for them, and re-layouts: 5.37 us -> 4.3 us
  transfers between devices with their start and end apart: 32 -> 32, of which waited for: 14 -> 15; matrix products, arithmetic and copies ran while one was open for 0% -> 0% of each run, Pallas kernels for 8% -> 6%
where the time goes in v4:
time: 104 us; the launch traced here: 103 us
  starting transfers between devices  46.9 us (45%)
  waiting for transfers between devices  42.7 us (41%)
  Pallas kernels  8.57 us (8%)
  local copies, waits for them, and re-layouts  4.3 us (4%)
    ppermute x29, starting transfers between devices, moved(): return lax.ppermute(value, 'cluster', pairs)  41 us
    ppermute x29, waiting for transfers between devices, moved(): return lax.ppermute(value, 'cluster', pairs)  40.5 us
    pallas_call x8, Pallas kernels, whole(): pl.pallas_call(kernel, in_specs=[pl.BlockSpec(memory_space=pltpu.SMEM) if...  8.57 us
    ppermute x3, starting transfers between devices, per_device(): powers[d] = lax.ppermute(power, 'sub', [(y, (y + d) % 4) for y in range(4)])  5.9 us
    unnamed x8, local copies, waits for them, and re-layouts  4.3 us
    ppermute x3, waiting for transfers between devices, per_device(): powers[d] = lax.ppermute(power, 'sub', [(y, (y + d) % 4) for y in range(4)])  2.22 us
  transfers between devices with their start and end apart: 32, of which 15 were waited for; matrix products, arithmetic and copies ran while one was open for 0% of the time, Pallas kernels for 6%

profile of v4, /device:TPU:2, one launch (start us, length us, event | category | flops | bytes accessed | tf_op | source)
XLA Modules:
  0.0 102.6 jit_solution(7505819593728832876)
XLA Ops:
  4.9 2.0 %collective-permute-start.9 = (bf16[2,552,128]{2,1,0:T(8,128)(2,1)S(1)}, bf16[2,552,128]{2,1,0:T(8,128)(2,1)S(1)}, u32[]{:S(2)}, u32[]{:S(2)}) collective-permute-start(bf16[2,552,128]{2,1,0:T(8,128)(2,1)S(1)} %get-tuple-element.27), channel_id=1, source_target_pairs={{0,32},{4,36},{8,40},{12,44},{16,48},{20,52},{24,56},{28,60},{32,0... | collective-permute-start | bytes 847880 | tf_op jit(solution)/shard_map/ppermute | solution.py:43
  6.9 2.1 %collective-permute-start.11 = (bf16[2,552,128]{2,1,0:T(8,128)(2,1)S(1)}, bf16[2,552,128]{2,1,0:T(8,128)(2,1)S(1)}, u32[]{:S(2)}, u32[]{:S(2)}) collective-permute-start(bf16[2,552,128]{2,1,0:T(8,128)(2,1)S(1)} %get-tuple-element.28), channel_id=1, source_target_pairs={{0,16},{4,20},{8,24},{12,28},{16,0},{20,4},{24,8},{28,12},{32,48},... | collective-permute-start | bytes 847880 | tf_op jit(solution)/shard_map/ppermute | solution.py:43
  12.2 2.4 %collective-permute-done.9.refs_6_ = bf16[2,552,128]{2,1,0:T(8,128)(2,1)S(1)} collective-permute-done((bf16[2,552,128]{2,1,0:T(8,128)(2,1)S(1)}, bf16[2,552,128]{2,1,0:T(8,128)(2,1)S(1)}, u32[]{:S(2)}, u32[]{:S(2)}) %collective-permute-start.9) | collective-permute-done | bytes 282656 | tf_op jit(solution)/shard_map/ppermute | solution.py:43
  14.6 3.5 %collective-permute-done.11.refs_8_ = bf16[2,552,128]{2,1,0:T(8,128)(2,1)S(1)} collective-permute-done((bf16[2,552,128]{2,1,0:T(8,128)(2,1)S(1)}, bf16[2,552,128]{2,1,0:T(8,128)(2,1)S(1)}, u32[]{:S(2)}, u32[]{:S(2)}) %collective-permute-start.11) | collective-permute-done | bytes 282656 | tf_op jit(solution)/shard_map/ppermute | solution.py:43
  18.1 6.3 %collective-permute-start = (bf16[2,552,128]{2,1,0:T(8,128)(2,1)S(1)}, bf16[2,552,128]{2,1,0:T(8,128)(2,1)S(1)}, u32[]{:S(2)}, u32[]{:S(2)}) collective-permute-start(bf16[2,552,128]{2,1,0:T(8,128)(2,1)S(1)} %get-tuple-element.22), channel_id=1, source_target_pairs={{0,56},{4,60},{8,32},{12,36},{16,40},{20,44},{24,48},{28,52},{32,2... | collective-permute-start | bytes 847880 | tf_op jit(solution)/shard_map/ppermute | solution.py:43
  24.3 3.9 %collective-permute-start.2 = (bf16[2,552,128]{2,1,0:T(8,128)(2,1)S(1)}, bf16[2,552,128]{2,1,0:T(8,128)(2,1)S(1)}, u32[]{:S(2)}, u32[]{:S(2)}) collective-permute-start(bf16[2,552,128]{2,1,0:T(8,128)(2,1)S(1)} %get-tuple-element.23), channel_id=1, source_target_pairs={{0,48},{4,52},{8,56},{12,60},{16,32},{20,36},{24,40},{28,44},{32,1... | collective-permute-start | bytes 847880 | tf_op jit(solution)/shard_map/ppermute | solution.py:43
  28.2 7.0 %collective-permute-done.5.refs_2_ = bf16[2,552,128]{2,1,0:T(8,128)(2,1)S(1)} collective-permute-done((bf16[2,552,128]{2,1,0:T(8,128)(2,1)S(1)}, bf16[2,552,128]{2,1,0:T(8,128)(2,1)S(1)}, u32[]{:S(2)}, u32[]{:S(2)}) %collective-permute-start.5) | collective-permute-done | bytes 282656 | tf_op jit(solution)/shard_map/ppermute | solution.py:43
  36.2 2.2 %collective-permute-done.2.refs_2_ = bf16[2,552,128]{2,1,0:T(8,128)(2,1)S(1)} collective-permute-done((bf16[2,552,128]{2,1,0:T(8,128)(2,1)S(1)}, bf16[2,552,128]{2,1,0:T(8,128)(2,1)S(1)}, u32[]{:S(2)}, u32[]{:S(2)}) %collective-permute-start.2) | collective-permute-done | bytes 282656 | tf_op jit(solution)/shard_map/ppermute | solution.py:43
  39.9 4.7 %shard_map.47 = (f32[168,256]{1,0:T(8,128)S(1)}, f32[168,256]{1,0:T(8,128)S(1)}, f32[168,256]{1,0:T(8,128)S(1)}, f32[256,256]{1,0:T(8,128)S(1)}) custom-call(bf16[2,552,128]{2,1,0:T(8,128)(2,1)S(1)} %get-tuple-element.24.refs_0_, bf16[2,552,128]{2,1,0:T(8,128)(2,1)S(1)} %collective-permute-done.4.refs_1_, ...), custom_call_target="tpu_custom_call" | custom-call | flops 2000000000 | bytes 3000000 | tf_op jit(solution)/shard_map/pallas_call | solution.py:84
  44.9 2.9 %collective-permute-start.15 = (bf16[256,256]{1,0:T(8,128)(2,1)S(1)}, bf16[256,256]{1,0:T(8,128)(2,1)S(1)}, u32[]{:S(2)}, u32[]{:S(2)}) collective-permute-start(bf16[256,256]{1,0:T(8,128)(2,1)S(1)} %shard_map.49.refs_0_), channel_id=1, source_target_pairs={{0,64},{4,68},{8,72},{12,76},{16,80},{20,84},{24,88},{28,92},{32,9... | collective-permute-start | bytes 393224 | tf_op jit(solution)/shard_map/ppermute | solution.py:43
  47.8 4.5 %collective-permute-start.16 = (bf16[256,256]{1,0:T(8,128)(2,1)S(1)}, bf16[256,256]{1,0:T(8,128)(2,1)S(1)}, u32[]{:S(2)}, u32[]{:S(2)}) collective-permute-start(bf16[256,256]{1,0:T(8,128)(2,1)S(1)} %shard_map.49.refs_0_), channel_id=1, source_target_pairs={{0,128},{4,132},{8,136},{12,140},{16,144},{20,148},{24,152},{28,15... | collective-permute-start | bytes 393224 | tf_op jit(solution)/shard_map/ppermute | solution.py:43
  52.3 2.7 %collective-permute-start.17 = (bf16[256,256]{1,0:T(8,128)(2,1)S(1)}, bf16[256,256]{1,0:T(8,128)(2,1)S(1)}, u32[]{:S(2)}, u32[]{:S(2)}) collective-permute-start(bf16[256,256]{1,0:T(8,128)(2,1)S(1)} %shard_map.49.refs_0_), channel_id=1, source_target_pairs={{0,192},{4,196},{8,200},{12,204},{16,208},{20,212},{24,216},{28,22... | collective-permute-start | bytes 393224 | tf_op jit(solution)/shard_map/ppermute | solution.py:43
  56.2 5.2 %collective-permute-done.16.refs_2_ = bf16[256,256]{1,0:T(8,128)(2,1)S(1)} collective-permute-done((bf16[256,256]{1,0:T(8,128)(2,1)S(1)}, bf16[256,256]{1,0:T(8,128)(2,1)S(1)}, u32[]{:S(2)}, u32[]{:S(2)}) %collective-permute-start.16) | collective-permute-done | bytes 131104 | tf_op jit(solution)/shard_map/ppermute | solution.py:43
  61.4 3.4 %collective-permute-done.17.refs_3_ = bf16[256,256]{1,0:T(8,128)(2,1)S(1)} collective-permute-done((bf16[256,256]{1,0:T(8,128)(2,1)S(1)}, bf16[256,256]{1,0:T(8,128)(2,1)S(1)}, u32[]{:S(2)}, u32[]{:S(2)}) %collective-permute-start.17) | collective-permute-done | bytes 131104 | tf_op jit(solution)/shard_map/ppermute | solution.py:43
  66.6 4.7 %collective-permute-start.19 = (bf16[168,256]{1,0:T(8,128)(2,1)S(1)}, bf16[168,256]{1,0:T(8,128)(2,1)S(1)}, u32[]{:S(2)}, u32[]{:S(2)}) collective-permute-start(bf16[168,256]{1,0:T(8,128)(2,1)S(1)} %shard_map.50.s0), channel_id=1, source_target_pairs={{0,128},{4,132},{8,136},{12,140},{16,144},{20,148},{24,152},{28,15... | collective-permute-start | bytes 258056 | tf_op jit(solution)/shard_map/ppermute | solution.py:43
  71.2 2.4 %collective-permute-start.20 = (bf16[168,256]{1,0:T(8,128)(2,1)S(1)}, bf16[168,256]{1,0:T(8,128)(2,1)S(1)}, u32[]{:S(2)}, u32[]{:S(2)}) collective-permute-start(bf16[168,256]{1,0:T(8,128)(2,1)S(1)} %shard_map.50.s0), channel_id=1, source_target_pairs={{0,192},{4,196},{8,200},{12,204},{16,208},{20,212},{24,216},{28,22... | collective-permute-start | bytes 258056 | tf_op jit(solution)/shard_map/ppermute | solution.py:43
  73.7 4.2 %collective-permute-done.19.s2 = bf16[168,256]{1,0:T(8,128)(2,1)S(1)} collective-permute-done((bf16[168,256]{1,0:T(8,128)(2,1)S(1)}, bf16[168,256]{1,0:T(8,128)(2,1)S(1)}, u32[]{:S(2)}, u32[]{:S(2)}) %collective-permute-start.19) | collective-permute-done | bytes 86048 | tf_op jit(solution)/shard_map/ppermute | solution.py:43
  78.0 1.6 %collective-permute-start.21 = (f32[1,128]{1,0:T(1,128)S(1)}, f32[1,128]{1,0:T(1,128)S(1)}, u32[]{:S(2)}, u32[]{:S(2)}) collective-permute-start(f32[1,128]{1,0:T(1,128)S(1)} %get-tuple-element.38.p0), channel_id=1, source_target_pairs={{0,1},{1,2},{2,3},{3,0},{4,5},{5,6},{6,7},{7,4},{8,9},{9,10},{10,1... | collective-permute-start | bytes 1544 | tf_op jit(solution)/shard_map/ppermute | solution.py:284
  79.6 2.9 %collective-permute-start.22 = (f32[1,128]{1,0:T(1,128)S(1)}, f32[1,128]{1,0:T(1,128)S(1)}, u32[]{:S(2)}, u32[]{:S(2)}) collective-permute-start(f32[1,128]{1,0:T(1,128)S(1)} %get-tuple-element.38.p0), channel_id=1, source_target_pairs={{0,2},{1,3},{2,0},{3,1},{4,6},{5,7},{6,4},{7,5},{8,10},{9,11},{10,... | collective-permute-start | bytes 1544 | tf_op jit(solution)/shard_map/ppermute | solution.py:284
  86.2 4.5 %collective-permute-done.24 = bf16[176,256]{1,0:T(8,128)(2,1)S(1)} collective-permute-done((bf16[176,256]{1,0:T(8,128)(2,1)S(1)}, bf16[176,256]{1,0:T(8,128)(2,1)S(1)}, u32[]{:S(2)}, u32[]{:S(2)}) %collective-permute-start.24) | collective-permute-done | bytes 90144 | tf_op jit(solution)/shard_map/ppermute | solution.py:43
  90.8 2.5 %collective-permute-start.26 = (bf16[2,176,256]{2,1,0:T(8,128)(2,1)S(1)}, bf16[2,176,256]{2,1,0:T(8,128)(2,1)S(1)}, u32[]{:S(2)}, u32[]{:S(2)}) collective-permute-start(bf16[2,176,256]{2,1,0:T(8,128)(2,1)S(1)} %pad_maximum_fusion.refs_3_), channel_id=1, source_target_pairs={{0,16},{4,20},{8,24},{12,28},{16,0},{20,4},{24,8},{28,12},{32,48},... | collective-permute-start | bytes 540680 | tf_op jit(solution)/shard_map/ppermute | solution.py:43
  94.1 2.2 %collective-permute-done.25.refs_4_ = bf16[2,176,256]{2,1,0:T(8,128)(2,1)S(1)} collective-permute-done((bf16[2,176,256]{2,1,0:T(8,128)(2,1)S(1)}, bf16[2,176,256]{2,1,0:T(8,128)(2,1)S(1)}, u32[]{:S(2)}, u32[]{:S(2)}) %collective-permute-start.25) | collective-permute-done | bytes 180256 | tf_op jit(solution)/shard_map/ppermute | solution.py:43
  96.3 1.7 %collective-permute-done.26.refs_5_ = bf16[2,176,256]{2,1,0:T(8,128)(2,1)S(1)} collective-permute-done((bf16[2,176,256]{2,1,0:T(8,128)(2,1)S(1)}, bf16[2,176,256]{2,1,0:T(8,128)(2,1)S(1)}, u32[]{:S(2)}, u32[]{:S(2)}) %collective-permute-start.26) | collective-permute-done | bytes 180256 | tf_op jit(solution)/shard_map/ppermute | solution.py:43
  98.0 1.8 %collective-permute-done.27.refs_6_ = bf16[2,176,256]{2,1,0:T(8,128)(2,1)S(1)} collective-permute-done((bf16[2,176,256]{2,1,0:T(8,128)(2,1)S(1)}, bf16[2,176,256]{2,1,0:T(8,128)(2,1)S(1)}, u32[]{:S(2)}, u32[]{:S(2)}) %collective-permute-start.27) | collective-permute-done | bytes 180256 | tf_op jit(solution)/shard_map/ppermute | solution.py:43
  (57 shorter events, 21.2 us)
Async XLA Ops:
  4.9 9.7 %collective-permute-start.9 = (bf16[2,552,128]{2,1,0:T(8,128)(2,1)S(1)}, bf16[2,552,128]{2,1,0:T(8,128)(2,1)S(1)}, u32[]{:S(2)}, u32[]{:S(2)}) collective-permute-start(bf16[2,552,128]{2,1,0:T(8,128)(2,1)S(1)} %get-tuple-element.27), channel_id=1, source_target_pairs={{0,32},{4,36},{8,40},{12,44},{16,48},{20,52},{24,56},{28,60},{32,0... | collective-permute-start | bytes 847880 | tf_op jit(solution)/shard_map/ppermute | solution.py:43
  6.9 11.2 %collective-permute-start.11 = (bf16[2,552,128]{2,1,0:T(8,128)(2,1)S(1)}, bf16[2,552,128]{2,1,0:T(8,128)(2,1)S(1)}, u32[]{:S(2)}, u32[]{:S(2)}) collective-permute-start(bf16[2,552,128]{2,1,0:T(8,128)(2,1)S(1)} %get-tuple-element.28), channel_id=1, source_target_pairs={{0,16},{4,20},{8,24},{12,28},{16,0},{20,4},{24,8},{28,12},{32,48},... | collective-permute-start | bytes 847880 | tf_op jit(solution)/shard_map/ppermute | solution.py:43
  9.0 15.3 %collective-permute-start.13 = (bf16[2,552,128]{2,1,0:T(8,128)(2,1)S(1)}, bf16[2,552,128]{2,1,0:T(8,128)(2,1)S(1)}, u32[]{:S(2)}, u32[]{:S(2)}) collective-permute-start(bf16[2,552,128]{2,1,0:T(8,128)(2,1)S(1)} %get-tuple-element.29), channel_id=1, source_target_pairs={{0,40},{4,44},{8,48},{12,52},{16,56},{20,60},{24,32},{28,36},{32,8... | collective-permute-start | bytes 847880 | tf_op jit(solution)/shard_map/ppermute | solution.py:43
  10.1 25.1 %collective-permute-start.5 = (bf16[2,552,128]{2,1,0:T(8,128)(2,1)S(1)}, bf16[2,552,128]{2,1,0:T(8,128)(2,1)S(1)}, u32[]{:S(2)}, u32[]{:S(2)}) collective-permute-start(bf16[2,552,128]{2,1,0:T(8,128)(2,1)S(1)} %get-tuple-element.25), channel_id=1, source_target_pairs={{0,8},{4,12},{8,16},{12,20},{16,24},{20,28},{24,0},{28,4},{32,40},... | collective-permute-start | bytes 847880 | tf_op jit(solution)/shard_map/ppermute | solution.py:43
  10.5 24.7 %collective-permute-start.7 = (bf16[2,552,128]{2,1,0:T(8,128)(2,1)S(1)}, bf16[2,552,128]{2,1,0:T(8,128)(2,1)S(1)}, u32[]{:S(2)}, u32[]{:S(2)}) collective-permute-start(bf16[2,552,128]{2,1,0:T(8,128)(2,1)S(1)} %get-tuple-element.26), channel_id=1, source_target_pairs={{0,24},{4,28},{8,0},{12,4},{16,8},{20,12},{24,16},{28,20},{32,56},... | collective-permute-start | bytes 847880 | tf_op jit(solution)/shard_map/ppermute | solution.py:43
  14.6 21.1 %collective-permute-start.4 = (bf16[2,552,128]{2,1,0:T(8,128)(2,1)S(1)}, bf16[2,552,128]{2,1,0:T(8,128)(2,1)S(1)}, u32[]{:S(2)}, u32[]{:S(2)}) collective-permute-start(bf16[2,552,128]{2,1,0:T(8,128)(2,1)S(1)} %get-tuple-element.24.refs_0_), channel_id=1, source_target_pairs={{0,4},{4,0},{8,12},{12,8},{16,20},{20,16},{24,28},{28,24},{32,36},... | collective-permute-start | bytes 847880 | tf_op jit(solution)/shard_map/ppermute | solution.py:43
  18.1 17.7 %collective-permute-start = (bf16[2,552,128]{2,1,0:T(8,128)(2,1)S(1)}, bf16[2,552,128]{2,1,0:T(8,128)(2,1)S(1)}, u32[]{:S(2)}, u32[]{:S(2)}) collective-permute-start(bf16[2,552,128]{2,1,0:T(8,128)(2,1)S(1)} %get-tuple-element.22), channel_id=1, source_target_pairs={{0,56},{4,60},{8,32},{12,36},{16,40},{20,44},{24,48},{28,52},{32,2... | collective-permute-start | bytes 847880 | tf_op jit(solution)/shard_map/ppermute | solution.py:43
  24.3 14.0 %collective-permute-start.2 = (bf16[2,552,128]{2,1,0:T(8,128)(2,1)S(1)}, bf16[2,552,128]{2,1,0:T(8,128)(2,1)S(1)}, u32[]{:S(2)}, u32[]{:S(2)}) collective-permute-start(bf16[2,552,128]{2,1,0:T(8,128)(2,1)S(1)} %get-tuple-element.23), channel_id=1, source_target_pairs={{0,48},{4,52},{8,56},{12,60},{16,32},{20,36},{24,40},{28,44},{32,1... | collective-permute-start | bytes 847880 | tf_op jit(solution)/shard_map/ppermute | solution.py:43
  35.2 3.7 %collective-permute-start.12 = (bf16[2,552,128]{2,1,0:T(8,128)(2,1)S(1)}, bf16[2,552,128]{2,1,0:T(8,128)(2,1)S(1)}, u32[]{:S(2)}, u32[]{:S(2)}) collective-permute-start(bf16[2,552,128]{2,1,0:T(8,128)(2,1)S(1)} %collective-permute-done.11.refs_8_), channel_id=1, source_target_pairs={{0,4},{4,0},{8,12},{12,8},{16,20},{20,16},{24,28},{28,24},{32,36},... | collective-permute-start | bytes 847880 | tf_op jit(solution)/shard_map/ppermute | solution.py:43
  38.4 6.2 %collective-permute-start.1 = (bf16[2,552,128]{2,1,0:T(8,128)(2,1)S(1)}, bf16[2,552,128]{2,1,0:T(8,128)(2,1)S(1)}, u32[]{:S(2)}, u32[]{:S(2)}) collective-permute-start(bf16[2,552,128]{2,1,0:T(8,128)(2,1)S(1)} %collective-permute-done.refs_0_), channel_id=1, source_target_pairs={{0,4},{4,0},{8,12},{12,8},{16,20},{20,16},{24,28},{28,24},{32,36},... | collective-permute-start | bytes 847880 | tf_op jit(solution)/shard_map/ppermute | solution.py:43
  38.9 5.7 %collective-permute-start.3 = (bf16[2,552,128]{2,1,0:T(8,128)(2,1)S(1)}, bf16[2,552,128]{2,1,0:T(8,128)(2,1)S(1)}, u32[]{:S(2)}, u32[]{:S(2)}) collective-permute-start(bf16[2,552,128]{2,1,0:T(8,128)(2,1)S(1)} %collective-permute-done.2.refs_2_), channel_id=1, source_target_pairs={{0,4},{4,0},{8,12},{12,8},{16,20},{20,16},{24,28},{28,24},{32,36},... | collective-permute-start | bytes 847880 | tf_op jit(solution)/shard_map/ppermute | solution.py:43
  44.9 11.2 %collective-permute-start.15 = (bf16[256,256]{1,0:T(8,128)(2,1)S(1)}, bf16[256,256]{1,0:T(8,128)(2,1)S(1)}, u32[]{:S(2)}, u32[]{:S(2)}) collective-permute-start(bf16[256,256]{1,0:T(8,128)(2,1)S(1)} %shard_map.49.refs_0_), channel_id=1, source_target_pairs={{0,64},{4,68},{8,72},{12,76},{16,80},{20,84},{24,88},{28,92},{32,9... | collective-permute-start | bytes 393224 | tf_op jit(solution)/shard_map/ppermute | solution.py:43
  47.8 13.6 %collective-permute-start.16 = (bf16[256,256]{1,0:T(8,128)(2,1)S(1)}, bf16[256,256]{1,0:T(8,128)(2,1)S(1)}, u32[]{:S(2)}, u32[]{:S(2)}) collective-permute-start(bf16[256,256]{1,0:T(8,128)(2,1)S(1)} %shard_map.49.refs_0_), channel_id=1, source_target_pairs={{0,128},{4,132},{8,136},{12,140},{16,144},{20,148},{24,152},{28,15... | collective-permute-start | bytes 393224 | tf_op jit(solution)/shard_map/ppermute | solution.py:43
  52.3 12.5 %collective-permute-start.17 = (bf16[256,256]{1,0:T(8,128)(2,1)S(1)}, bf16[256,256]{1,0:T(8,128)(2,1)S(1)}, u32[]{:S(2)}, u32[]{:S(2)}) collective-permute-start(bf16[256,256]{1,0:T(8,128)(2,1)S(1)} %shard_map.49.refs_0_), channel_id=1, source_target_pairs={{0,192},{4,196},{8,200},{12,204},{16,208},{20,212},{24,216},{28,22... | collective-permute-start | bytes 393224 | tf_op jit(solution)/shard_map/ppermute | solution.py:43
  65.2 8.4 %collective-permute-start.18 = (bf16[168,256]{1,0:T(8,128)(2,1)S(1)}, bf16[168,256]{1,0:T(8,128)(2,1)S(1)}, u32[]{:S(2)}, u32[]{:S(2)}) collective-permute-start(bf16[168,256]{1,0:T(8,128)(2,1)S(1)} %shard_map.50.s0), channel_id=1, source_target_pairs={{0,64},{4,68},{8,72},{12,76},{16,80},{20,84},{24,88},{28,92},{32,9... | collective-permute-start | bytes 258056 | tf_op jit(solution)/shard_map/ppermute | solution.py:43
  66.6 11.3 %collective-permute-start.19 = (bf16[168,256]{1,0:T(8,128)(2,1)S(1)}, bf16[168,256]{1,0:T(8,128)(2,1)S(1)}, u32[]{:S(2)}, u32[]{:S(2)}) collective-permute-start(bf16[168,256]{1,0:T(8,128)(2,1)S(1)} %shard_map.50.s0), channel_id=1, source_target_pairs={{0,128},{4,132},{8,136},{12,140},{16,144},{20,148},{24,152},{28,15... | collective-permute-start | bytes 258056 | tf_op jit(solution)/shard_map/ppermute | solution.py:43
  71.2 6.6 %collective-permute-start.20 = (bf16[168,256]{1,0:T(8,128)(2,1)S(1)}, bf16[168,256]{1,0:T(8,128)(2,1)S(1)}, u32[]{:S(2)}, u32[]{:S(2)}) collective-permute-start(bf16[168,256]{1,0:T(8,128)(2,1)S(1)} %shard_map.50.s0), channel_id=1, source_target_pairs={{0,192},{4,196},{8,200},{12,204},{16,208},{20,212},{24,216},{28,22... | collective-permute-start | bytes 258056 | tf_op jit(solution)/shard_map/ppermute | solution.py:43
  78.0 5.9 %collective-permute-start.21 = (f32[1,128]{1,0:T(1,128)S(1)}, f32[1,128]{1,0:T(1,128)S(1)}, u32[]{:S(2)}, u32[]{:S(2)}) collective-permute-start(f32[1,128]{1,0:T(1,128)S(1)} %get-tuple-element.38.p0), channel_id=1, source_target_pairs={{0,1},{1,2},{2,3},{3,0},{4,5},{5,6},{6,7},{7,4},{8,9},{9,10},{10,1... | collective-permute-start | bytes 1544 | tf_op jit(solution)/shard_map/ppermute | solution.py:284
  79.6 5.1 %collective-permute-start.22 = (f32[1,128]{1,0:T(1,128)S(1)}, f32[1,128]{1,0:T(1,128)S(1)}, u32[]{:S(2)}, u32[]{:S(2)}) collective-permute-start(f32[1,128]{1,0:T(1,128)S(1)} %get-tuple-element.38.p0), channel_id=1, source_target_pairs={{0,2},{1,3},{2,0},{3,1},{4,6},{5,7},{6,4},{7,5},{8,10},{9,11},{10,... | collective-permute-start | bytes 1544 | tf_op jit(solution)/shard_map/ppermute | solution.py:284
  86.1 4.6 %collective-permute-start.24 = (bf16[176,256]{1,0:T(8,128)(2,1)S(1)}, bf16[176,256]{1,0:T(8,128)(2,1)S(1)}, u32[]{:S(2)}, u32[]{:S(2)}) collective-permute-start(bf16[176,256]{1,0:T(8,128)(2,1)S(1)} %shard_map.52), channel_id=1, source_target_pairs={{0,32},{4,36},{8,40},{12,44},{16,48},{20,52},{24,56},{28,60},{32,0... | collective-permute-start | bytes 270344 | tf_op jit(solution)/shard_map/ppermute | solution.py:43
  90.7 5.6 %collective-permute-start.25 = (bf16[2,176,256]{2,1,0:T(8,128)(2,1)S(1)}, bf16[2,176,256]{2,1,0:T(8,128)(2,1)S(1)}, u32[]{:S(2)}, u32[]{:S(2)}) collective-permute-start(bf16[2,176,256]{2,1,0:T(8,128)(2,1)S(1)} %pad_maximum_fusion.refs_3_), channel_id=1, source_target_pairs={{0,8},{4,12},{8,16},{12,20},{16,24},{20,28},{24,0},{28,4},{32,40},... | collective-permute-start | bytes 540680 | tf_op jit(solution)/shard_map/ppermute | solution.py:43
  90.8 7.2 %collective-permute-start.26 = (bf16[2,176,256]{2,1,0:T(8,128)(2,1)S(1)}, bf16[2,176,256]{2,1,0:T(8,128)(2,1)S(1)}, u32[]{:S(2)}, u32[]{:S(2)}) collective-permute-start(bf16[2,176,256]{2,1,0:T(8,128)(2,1)S(1)} %pad_maximum_fusion.refs_3_), channel_id=1, source_target_pairs={{0,16},{4,20},{8,24},{12,28},{16,0},{20,4},{24,8},{28,12},{32,48},... | collective-permute-start | bytes 540680 | tf_op jit(solution)/shard_map/ppermute | solution.py:43
  93.4 6.5 %collective-permute-start.27 = (bf16[2,176,256]{2,1,0:T(8,128)(2,1)S(1)}, bf16[2,176,256]{2,1,0:T(8,128)(2,1)S(1)}, u32[]{:S(2)}, u32[]{:S(2)}) collective-permute-start(bf16[2,176,256]{2,1,0:T(8,128)(2,1)S(1)} %pad_maximum_fusion.refs_3_), channel_id=1, source_target_pairs={{0,24},{4,28},{8,0},{12,4},{16,8},{20,12},{24,16},{28,20},{32,56},... | collective-permute-start | bytes 540680 | tf_op jit(solution)/shard_map/ppermute | solution.py:43
  94.1 5.7 %collective-permute-start.28 = (bf16[2,176,256]{2,1,0:T(8,128)(2,1)S(1)}, bf16[2,176,256]{2,1,0:T(8,128)(2,1)S(1)}, u32[]{:S(2)}, u32[]{:S(2)}) collective-permute-start(bf16[2,176,256]{2,1,0:T(8,128)(2,1)S(1)} %pad_maximum_fusion.refs_3_), channel_id=1, source_target_pairs={{0,4},{4,0},{8,12},{12,8},{16,20},{20,16},{24,28},{28,24},{32,36},... | collective-permute-start | bytes 540680 | tf_op jit(solution)/shard_map/ppermute | solution.py:43
  (12 other events, 25.9 us)

commit v5 on v4

--- a/solution.py
+++ b/solution.py
@@ -36,7 +36,20 @@
     ]
 
 
-SLOTS = ((0, 0), (1, 0), (3, 0), (0, 1), (2, 0), (1, 1), (3, 1), (2, 1))
+SLOTS = ((0, 0), (2, 1), (1, 0), (1, 1), (3, 0), (3, 1), (2, 0), (0, 1))
+
+
+def ring_step(turn, count, spread):
+    first = {k: (k ^ 1 if turn == 0 else (k - 1) % 4 if k % 2 == 0 else (k + 1) % 4) for k in range(4)}
+    return [(spread(k, n), spread(first[k], n)) for k in range(4) for n in range(count)]
+
+
+def on_z_ring(turn):
+    return ring_step(turn, 2 * X * C, lambda q, n: place(2 * q + n // (X * C), n // C % X, n % C))
+
+
+def on_sub_ring(turn):
+    return ring_step(turn, 1, lambda y, n: y)
 
 
 def moved(value, pairs):
@@ -52,38 +65,50 @@
     return top, jnp.concatenate([top, jnp.concatenate([-y, x], axis=1)], axis=0)
 
 
-def pack_kernel(x_ref, pair_ref, c_ref, mant_ref, expo_ref, chan_ref, inv_ref, *outs):
+def pack_kernel(x_ref, pair_ref, c_ref, *refs):
+    far, outs, near, sems = refs[:4], refs[4:12], refs[12:16], refs[16]
+    loads = [pltpu.make_async_copy(a, b, sems.at[k]) for k, (a, b) in enumerate(zip(far, near))]
+    for load in loads:
+        load.start()
+    expo_ref, inv_ref, chan_ref, mant_ref = near
     x, pair, c = x_ref[0], pair_ref[0], c_ref[0]
+    loads[0].wait()
     row = lax.broadcasted_iota(jnp.int32, (168, 14), 0)
     first = lax.broadcasted_iota(jnp.int32, (168, 14), 1) * 12
     inside = ((row >= first) & (row < first + 12)).astype(F32).astype(BF)
     expo = jnp.concatenate([expo_ref[t] for t in range(14)], axis=0)
     scales = dot(inside, jnp.exp2(expo.astype(F32)).astype(BF))
     lane = lax.broadcasted_iota(jnp.int32, (168, 16), 1)
-    for out, (dx, dp) in zip(outs, SLOTS):
-        for k, side in enumerate((c, 1 - c)):
-            r = side * 8 + lax.rem(x + dx, X) * 2 + (1 - pair if dp else pair)
-            out[k, 0:256, :] = inv_ref[r]
-            out[k, 256:384, :] = chan_ref[r]
-            scale = jnp.sum(jnp.where(lane == r, scales, 0.0), axis=1, keepdims=True)
-            out[k, 384:552, :] = (mant_ref[r].astype(F32) * scale).astype(BF)
+    places = [
+        (out, k, side * 8 + lax.rem(x + dx, X) * 2 + (1 - pair if dp else pair))
+        for out, (dx, dp) in zip(outs, SLOTS)
+        for k, side in enumerate((c, 1 - c))
+    ]
+    loads[1].wait()
+    loads[2].wait()
+    for out, k, r in places:
+        out[k, 0:256, :] = inv_ref[r]
+        out[k, 256:384, :] = chan_ref[r]
+    loads[3].wait()
+    for out, k, r in places:
+        scale = jnp.sum(jnp.where(lane == r, scales, 0.0), axis=1, keepdims=True)
+        out[k, 384:552, :] = (mant_ref[r].astype(F32) * scale).astype(BF)
 
 
 def near(shape, dtype):
     return pltpu.VMEM(shape, dtype)
 
 
-def whole(kernel, ins, outs, scratch=(), cost=None, fetched=False):
-    vmem = pl.BlockSpec(memory_space=pltpu.VMEM)
+def whole(kernel, ins, outs, scratch=(), cost=None, space=pltpu.VMEM, out_space=pltpu.VMEM):
+    vmem = pl.BlockSpec(memory_space=out_space)
     scalar = [value.shape == (1,) for value in ins]
-    if not fetched:
-        ins = [
-            value if small else pltpu.with_memory_space_constraint(value, pltpu.VMEM)
-            for value, small in zip(ins, scalar)
-        ]
+    ins = [
+        value if small else pltpu.with_memory_space_constraint(value, space)
+        for value, small in zip(ins, scalar)
+    ]
     return pl.pallas_call(
         kernel,
-        in_specs=[pl.BlockSpec(memory_space=pltpu.SMEM) if small else vmem for small in scalar],
+        in_specs=[pl.BlockSpec(memory_space=pltpu.SMEM if small else space) for small in scalar],
         out_specs=[vmem] * len(outs) if isinstance(outs, list) else vmem,
         out_shape=outs,
         scratch_shapes=scratch,
@@ -94,7 +119,8 @@
 
 def packed(*ins):
     cost = pl.CostEstimate(flops=6000000, bytes_accessed=5000000, transcendentals=0)
-    return whole(pack_kernel, ins, [near((2, 552, 128), BF)] * 8, cost=cost, fetched=True)
+    scratch = [pltpu.VMEM(value.shape, value.dtype) for value in ins[3:]] + [pltpu.SemaphoreType.DMA((4,))]
+    return whole(pack_kernel, ins, [near((2, 552, 128), BF)] * 8, scratch, cost, pltpu.HBM)
 
 
 def square_of(raw):
@@ -146,15 +172,21 @@
 
 
 def mean_kernel(*refs):
-    raws, before, out, av = refs[:-3], refs[-3], refs[-2], refs[-1]
+    raws, before, first_ref, second_ref, av = refs[:-4], *refs[-4:]
     av[...] = before[...]
     add_means([raw[k % 2, 0:256, :] for k, raw in enumerate(raws)], av)
     ones = (
         lax.broadcasted_iota(jnp.int32, (128, 256), 0) == lax.broadcasted_iota(jnp.int32, (128, 256), 1)
     ).astype(F32) * 16.0
     first = av[0:128, :]
-    out[0:128, :] = (first - ones).astype(BF)
-    out[128:256, :] = (av[128:256, :] - 2.0 * first + ones).astype(BF)
+    first_ref[...] = (first - ones).astype(BF)
+    second_ref[...] = (av[128:256, :] - 2.0 * first + ones).astype(BF)
+
+
+def pair_kernel(*refs):
+    n = len(refs) // 3
+    for a, b, out in zip(refs[:n], refs[n : 2 * n], refs[2 * n :]):
+        out[...] = (a[...].astype(F32) + b[...].astype(F32)).astype(out.dtype)
 
 
 def late_kernel(*refs):
@@ -178,7 +210,7 @@
 
 def mean_sums(raws, before):
     scratch = [pltpu.VMEM((256, 256), F32)]
-    return whole(mean_kernel, [*raws, before], near((256, 256), BF), scratch, COST)
+    return whole(mean_kernel, [*raws, before], [near((128, 256), BF)] * 2, scratch, COST)
 
 
 def late_sums(raws, before):
@@ -192,13 +224,11 @@
 
 
 def share_kernel(p_ref, d_ref, t_ref, *refs):
-    means, out_ref = refs[:4], refs[4]
-    mean = means[0][...].astype(F32)
-    for part in means[1:]:
-        mean += part[...].astype(F32)
-    mean = (mean * (1.0 / CLUSTERS)).astype(BF)
-    _, first = complex_square(mean[0:128, 0:128], mean[0:128, 128:256])
-    _, second = complex_square(mean[128:256, 0:128], mean[128:256, 128:256])
+    g0, g1, s0, s1, out_ref = refs
+    first = ((g0[...].astype(F32) + g1[...].astype(F32)) * (1.0 / CLUSTERS)).astype(BF)
+    second = ((s0[...].astype(F32) + s1[...].astype(F32)) * (1.0 / CLUSTERS)).astype(BF)
+    _, first = complex_square(first[:, 0:128], first[:, 128:256])
+    _, second = complex_square(second[:, 0:128], second[:, 128:256])
     p = p_ref[...]
     g = dot_wide(p, first)
     share = t_ref[...] + 1.5 * g - 0.5 * dot_wide(p, second) + dot_wide(g - 0.5 * d_ref[...], first)
@@ -215,8 +245,8 @@
     power_ref[...] = power[:, 0:128] + power[:, 128:256]
 
 
-def tail_kernel(value_ref, p0, p1, p2, p3, out_ref):
-    power = (p0[...] + p2[...]) + (p1[...] + p3[...])
+def tail_kernel(value_ref, p0, p1, out_ref):
+    power = p0[...] + p1[...]
     row = lax.broadcasted_iota(jnp.int32, (8, 256), 0)
     tail = jnp.zeros((8, 256), F32)
     for k in range(3):
@@ -228,7 +258,7 @@
 
 
 def finish_kernel(vectors, x_ref, pair_ref, c_ref, *refs):
-    parts, out_ref, rows = refs[:8], refs[8], refs[9]
+    parts, out_ref, rows, held, sems = refs[:8], refs[8], refs[9], refs[10], refs[11]
     x, pair, c = x_ref[0], pair_ref[0], c_ref[0]
     blocks = [
         side * 8 + lax.rem(x + X - d, X) * 2 + parity
@@ -245,9 +275,14 @@
         power += rows[k]
     factor = lax.rsqrt(power * (1.0 / vectors) + 1e-06)
     factor = jnp.concatenate([factor, factor], axis=1)
+    stores = []
     for k in range(16):
         value = parts[k // 2][k % 2, 0:168, :].astype(F32) * factor
-        out_ref[blocks[k]] = value.astype(BF)
+        held[k] = value.astype(BF)
+        stores.append(pltpu.make_async_copy(held.at[k], out_ref.at[blocks[k]], sems.at[k]))
+        stores[k].start()
+    for store in stores:
+        store.wait()
 
 
 def per_device(mantissas, exponents, channel, inverses):
@@ -259,7 +294,7 @@
     blocks, vectors, _ = mant.shape
     here = tuple(v.reshape(1).astype(jnp.int32) for v in (x, z % 2, c))
     sent = packed(
-        *here, mant, expo, channel[0].reshape(blocks, 128, 128), inverses[0].reshape(blocks, 256, 128)
+        *here, expo, inverses[0].reshape(blocks, 256, 128), channel[0].reshape(blocks, 128, 128), mant
     )
     raws = [sent[0]]
     for k in range(1, 8):
@@ -270,19 +305,22 @@
     slots = [part for pair in zip(raws, swapped) for part in pair]
     before = early_sums(slots[: 2 * EARLY])
     means = mean_sums(slots[2 * EARLY :], before[3])
-    means = [means, means, means, means]
-    for d in (2, 1, 3):
-        means[d] = moved(means[0], shifted(dz=2 * d))
+    first = moved(means[0], on_z_ring(0))
+    second = moved(means[1], on_z_ring(1))
+    means = whole(pair_kernel, (*means, first, second), [near((128, 256), BF)] * 2)
+    first = moved(means[0], on_z_ring(1))
+    second = moved(means[1], on_z_ring(0))
+    means = (means[0], first, means[1], second)
     sums = late_sums(slots[2 * EARLY :], before[:3])
     share = whole(share_kernel, (*sums, *means), near(SUM, BF))
     shares = [share, share, share, share]
     for d in (2, 1, 3):
         shares[d] = moved(share, shifted(dz=2 * d))
     value, power = whole(consensus_kernel, shares, [near(SUM, BF), near((1, 128), F32)])
-    powers = [power, power, power, power]
-    for d in (2, 1, 3):
-        powers[d] = lax.ppermute(power, "sub", [(y, (y + d) % 4) for y in range(4)])
-    mine = whole(tail_kernel, (value, *powers), near((ROWS, 256), BF))
+    near_power = lax.ppermute(power, "sub", on_sub_ring(0))
+    power = whole(pair_kernel, (power, near_power), near((1, 128), F32))
+    far_power = lax.ppermute(power, "sub", on_sub_ring(1))
+    mine = whole(tail_kernel, (value, power, far_power), near((ROWS, 256), BF))
     both = jnp.stack([mine, moved(mine, pair_shifted(0, 1))])
     same = [both] + [moved(both, shifted(dx=d)) for d in (1, 2, 3)]
     other = [moved(part, shifted(dc=1)) for part in same]
@@ -291,7 +329,12 @@
         lambda *refs: finish_kernel(total, *refs),
         (*here, *same, *other),
         jax.ShapeDtypeStruct((blocks, vectors, 256), BF),
-        (pltpu.VMEM((16, 1, 128), F32),),
+        (
+            pltpu.VMEM((16, 1, 128), F32),
+            pltpu.VMEM((16, vectors, 256), BF),
+            pltpu.SemaphoreType.DMA((16,)),
+        ),
+        out_space=pltpu.HBM,
     )
 
 

time: 104 us -> 102 us (0.981)
  the two profiles are of different devices: /device:TPU:2 before, /device:TPU:1 now
where the time goes in v5:
time: 102 us
  starting transfers between devices  63.6 us (62%)
  waiting for transfers between devices  28.2 us (28%)
  Pallas kernels  10.3 us (10%)
    ppermute x30, starting transfers between devices, moved(): return lax.ppermute(value, 'cluster', pairs)  59.4 us
    ppermute x30, waiting for transfers between devices, moved(): return lax.ppermute(value, 'cluster', pairs)  26.1 us
    pallas_call x10, Pallas kernels, whole(): pl.pallas_call(kernel, in_specs=[pl.BlockSpec(memory_space=pltpu.SMEM if...  10.3 us
    ppermute x1, starting transfers between devices, per_device(): far_power = lax.ppermute(power, 'sub', on_sub_ring(1))  2.83 us
  transfers between devices with their start and end apart: 32, of which 17 were waited for; matrix products, arithmetic and copies ran while one was open for 0% of the time, Pallas kernels for 6%

profile of v5, /device:TPU:1, one launch (start us, length us, event | category | flops | bytes accessed | tf_op | source)
XLA Modules:
  0.0 102.4 jit_solution(539661167044731369)
XLA Ops:
  0.0 2.3 %shard_map.46 = (bf16[2,552,128]{2,1,0:T(8,128)(2,1)S(1)}, bf16[2,552,128]{2,1,0:T(8,128)(2,1)S(1)}, bf16[2,552,128]{2,1,0:T(8,128)(2,1)S(1)}, bf16[2,552,128]{2...) custom-call(s32[1]{0:T(128)} %bitcast.x_ref.refs_0_, ...), custom_call_target="tpu_custom_call" | custom-call | flops 6000000 | bytes 5000000 | tf_op jit(solution)/shard_map/pallas_call | solution.py:109
  2.3 3.5 %collective-permute-start.9 = (bf16[2,552,128]{2,1,0:T(8,128)(2,1)S(1)}, bf16[2,552,128]{2,1,0:T(8,128)(2,1)S(1)}, u32[]{:S(2)}, u32[]{:S(2)}) collective-permute-start(bf16[2,552,128]{2,1,0:T(8,128)(2,1)S(1)} %get-tuple-element.31), channel_id=1, source_target_pairs={{0,40},{4,44},{8,48},{12,52},{16,56},{20,60},{24,32},{28,36},{32,8... | collective-permute-start | bytes 847880 | tf_op jit(solution)/shard_map/ppermute | solution.py:56
  8.0 1.9 %collective-permute-start.5 = (bf16[2,552,128]{2,1,0:T(8,128)(2,1)S(1)}, bf16[2,552,128]{2,1,0:T(8,128)(2,1)S(1)}, u32[]{:S(2)}, u32[]{:S(2)}) collective-permute-start(bf16[2,552,128]{2,1,0:T(8,128)(2,1)S(1)} %get-tuple-element.29), channel_id=1, source_target_pairs={{0,48},{4,52},{8,56},{12,60},{16,32},{20,36},{24,40},{28,44},{32,1... | collective-permute-start | bytes 847880 | tf_op jit(solution)/shard_map/ppermute | solution.py:56
  11.7 5.6 %collective-permute-start.4 = (bf16[2,552,128]{2,1,0:T(8,128)(2,1)S(1)}, bf16[2,552,128]{2,1,0:T(8,128)(2,1)S(1)}, u32[]{:S(2)}, u32[]{:S(2)}) collective-permute-start(bf16[2,552,128]{2,1,0:T(8,128)(2,1)S(1)} %get-tuple-element.28.refs_0_), channel_id=1, source_target_pairs={{0,4},{4,0},{8,12},{12,8},{16,20},{20,16},{24,28},{28,24},{32,36},... | collective-permute-start | bytes 847880 | tf_op jit(solution)/shard_map/ppermute | solution.py:56
  20.4 5.9 %collective-permute-done.5.refs_2_ = bf16[2,552,128]{2,1,0:T(8,128)(2,1)S(1)} collective-permute-done((bf16[2,552,128]{2,1,0:T(8,128)(2,1)S(1)}, bf16[2,552,128]{2,1,0:T(8,128)(2,1)S(1)}, u32[]{:S(2)}, u32[]{:S(2)}) %collective-permute-start.5) | collective-permute-done | bytes 282656 | tf_op jit(solution)/shard_map/ppermute | solution.py:56
  26.3 4.9 %collective-permute-start.10 = (bf16[2,552,128]{2,1,0:T(8,128)(2,1)S(1)}, bf16[2,552,128]{2,1,0:T(8,128)(2,1)S(1)}, u32[]{:S(2)}, u32[]{:S(2)}) collective-permute-start(bf16[2,552,128]{2,1,0:T(8,128)(2,1)S(1)} %collective-permute-done.9.refs_6_), channel_id=1, source_target_pairs={{0,4},{4,0},{8,12},{12,8},{16,20},{20,16},{24,28},{28,24},{32,36},... | collective-permute-start | bytes 847880 | tf_op jit(solution)/shard_map/ppermute | solution.py:56
  31.7 5.7 %collective-permute-start.6 = (bf16[2,552,128]{2,1,0:T(8,128)(2,1)S(1)}, bf16[2,552,128]{2,1,0:T(8,128)(2,1)S(1)}, u32[]{:S(2)}, u32[]{:S(2)}) collective-permute-start(bf16[2,552,128]{2,1,0:T(8,128)(2,1)S(1)} %collective-permute-done.5.refs_2_), channel_id=1, source_target_pairs={{0,4},{4,0},{8,12},{12,8},{16,20},{20,16},{24,28},{28,24},{32,36},... | collective-permute-start | bytes 847880 | tf_op jit(solution)/shard_map/ppermute | solution.py:56
  39.1 4.7 %shard_map.47 = (f32[168,256]{1,0:T(8,128)S(1)}, f32[168,256]{1,0:T(8,128)S(1)}, f32[168,256]{1,0:T(8,128)S(1)}, f32[256,256]{1,0:T(8,128)S(1)}) custom-call(bf16[2,552,128]{2,1,0:T(8,128)(2,1)S(1)} %get-tuple-element.28.refs_0_, bf16[2,552,128]{2,1,0:T(8,128)(2,1)S(1)} %collective-permute-done.4.refs_1_, ...), custom_call_target="tpu_custom_call" | custom-call | flops 2000000000 | bytes 3000000 | tf_op jit(solution)/shard_map/pallas_call | solution.py:109
  44.1 3.1 %collective-permute-start.15 = (bf16[128,256]{1,0:T(8,128)(2,1)S(1)}, bf16[128,256]{1,0:T(8,128)(2,1)S(1)}, u32[]{:S(2)}, u32[]{:S(2)}) collective-permute-start(bf16[128,256]{1,0:T(8,128)(2,1)S(1)} %get-tuple-element.41.refs_0_), channel_id=1, source_target_pairs={{0,64},{4,68},{8,72},{12,76},{16,80},{20,84},{24,88},{28,92},{32,9... | collective-permute-start | bytes 196616 | tf_op jit(solution)/shard_map/ppermute | solution.py:56
  47.2 2.6 %collective-permute-start.16 = (bf16[128,256]{1,0:T(8,128)(2,1)S(1)}, bf16[128,256]{1,0:T(8,128)(2,1)S(1)}, u32[]{:S(2)}, u32[]{:S(2)}) collective-permute-start(bf16[128,256]{1,0:T(8,128)(2,1)S(1)} %get-tuple-element.42.refs_1_), channel_id=1, source_target_pairs={{0,192},{4,196},{8,200},{12,204},{16,208},{20,212},{24,216},{28,22... | collective-permute-start | bytes 196616 | tf_op jit(solution)/shard_map/ppermute | solution.py:56
  50.5 2.0 %collective-permute-done.16.refs_3_ = bf16[128,256]{1,0:T(8,128)(2,1)S(1)} collective-permute-done((bf16[128,256]{1,0:T(8,128)(2,1)S(1)}, bf16[128,256]{1,0:T(8,128)(2,1)S(1)}, u32[]{:S(2)}, u32[]{:S(2)}) %collective-permute-start.16) | collective-permute-done | bytes 65568 | tf_op jit(solution)/shard_map/ppermute | solution.py:56
  52.5 4.6 %collective-permute-start.17 = (bf16[128,256]{1,0:T(8,128)(2,1)S(1)}, bf16[128,256]{1,0:T(8,128)(2,1)S(1)}, u32[]{:S(2)}, u32[]{:S(2)}) collective-permute-start(bf16[128,256]{1,0:T(8,128)(2,1)S(1)} %get-tuple-element.43.refs_0_), channel_id=1, source_target_pairs={{0,192},{4,196},{8,200},{12,204},{16,208},{20,212},{24,216},{28,22... | collective-permute-start | bytes 196616 | tf_op jit(solution)/shard_map/ppermute | solution.py:56
  59.5 1.8 %collective-permute-done.18.refs_3_ = bf16[128,256]{1,0:T(8,128)(2,1)S(1)} collective-permute-done((bf16[128,256]{1,0:T(8,128)(2,1)S(1)}, bf16[128,256]{1,0:T(8,128)(2,1)S(1)}, u32[]{:S(2)}, u32[]{:S(2)}) %collective-permute-start.18) | collective-permute-done | bytes 65568 | tf_op jit(solution)/shard_map/ppermute | solution.py:56
  62.2 2.8 %collective-permute-start.20 = (bf16[168,256]{1,0:T(8,128)(2,1)S(1)}, bf16[168,256]{1,0:T(8,128)(2,1)S(1)}, u32[]{:S(2)}, u32[]{:S(2)}) collective-permute-start(bf16[168,256]{1,0:T(8,128)(2,1)S(1)} %shard_map.51.s0), channel_id=1, source_target_pairs={{0,128},{4,132},{8,136},{12,140},{16,144},{20,148},{24,152},{28,15... | collective-permute-start | bytes 258056 | tf_op jit(solution)/shard_map/ppermute | solution.py:56
  65.6 2.6 %collective-permute-done.19.s1 = bf16[168,256]{1,0:T(8,128)(2,1)S(1)} collective-permute-done((bf16[168,256]{1,0:T(8,128)(2,1)S(1)}, bf16[168,256]{1,0:T(8,128)(2,1)S(1)}, u32[]{:S(2)}, u32[]{:S(2)}) %collective-permute-start.19) | collective-permute-done | bytes 86048 | tf_op jit(solution)/shard_map/ppermute | solution.py:56
  68.2 2.2 %collective-permute-done.20.s2 = bf16[168,256]{1,0:T(8,128)(2,1)S(1)} collective-permute-done((bf16[168,256]{1,0:T(8,128)(2,1)S(1)}, bf16[168,256]{1,0:T(8,128)(2,1)S(1)}, u32[]{:S(2)}, u32[]{:S(2)}) %collective-permute-start.20) | collective-permute-done | bytes 86048 | tf_op jit(solution)/shard_map/ppermute | solution.py:56
  70.4 2.0 %collective-permute-done.21.s3 = bf16[168,256]{1,0:T(8,128)(2,1)S(1)} collective-permute-done((bf16[168,256]{1,0:T(8,128)(2,1)S(1)}, bf16[168,256]{1,0:T(8,128)(2,1)S(1)}, u32[]{:S(2)}, u32[]{:S(2)}) %collective-permute-start.21) | collective-permute-done | bytes 86048 | tf_op jit(solution)/shard_map/ppermute | solution.py:56
  75.0 2.8 %collective-permute-start.23 = (f32[1,128]{1,0:T(1,128)S(1)}, f32[1,128]{1,0:T(1,128)S(1)}, u32[]{:S(2)}, u32[]{:S(2)}) collective-permute-start(f32[1,128]{1,0:T(1,128)S(1)} %shard_map.53.p0), channel_id=1, source_target_pairs={{0,3},{1,2},{2,1},{3,0},{4,7},{5,6},{6,5},{7,4},{8,11},{9,10},{10,... | collective-permute-start | bytes 1544 | tf_op jit(solution)/shard_map/ppermute | solution.py:322
  78.9 3.7 %collective-permute-done.24 = bf16[176,256]{1,0:T(8,128)(2,1)S(1)} collective-permute-done((bf16[176,256]{1,0:T(8,128)(2,1)S(1)}, bf16[176,256]{1,0:T(8,128)(2,1)S(1)}, u32[]{:S(2)}, u32[]{:S(2)}) %collective-permute-start.24) | collective-permute-done | bytes 90144 | tf_op jit(solution)/shard_map/ppermute | solution.py:56
  82.5 1.7 %collective-permute-start.25 = (bf16[2,176,256]{2,1,0:T(8,128)(2,1)S(1)}, bf16[2,176,256]{2,1,0:T(8,128)(2,1)S(1)}, u32[]{:S(2)}, u32[]{:S(2)}) collective-permute-start(bf16[2,176,256]{2,1,0:T(8,128)(2,1)S(1)} %pad_maximum_fusion.refs_3_), channel_id=1, source_target_pairs={{0,8},{4,12},{8,16},{12,20},{16,24},{20,28},{24,0},{28,4},{32,40},... | collective-permute-start | bytes 540680 | tf_op jit(solution)/shard_map/ppermute | solution.py:56
  84.2 2.2 %collective-permute-start.26 = (bf16[2,176,256]{2,1,0:T(8,128)(2,1)S(1)}, bf16[2,176,256]{2,1,0:T(8,128)(2,1)S(1)}, u32[]{:S(2)}, u32[]{:S(2)}) collective-permute-start(bf16[2,176,256]{2,1,0:T(8,128)(2,1)S(1)} %pad_maximum_fusion.refs_3_), channel_id=1, source_target_pairs={{0,16},{4,20},{8,24},{12,28},{16,0},{20,4},{24,8},{28,12},{32,48},... | collective-permute-start | bytes 540680 | tf_op jit(solution)/shard_map/ppermute | solution.py:56
  86.7 7.5 %collective-permute-start.28 = (bf16[2,176,256]{2,1,0:T(8,128)(2,1)S(1)}, bf16[2,176,256]{2,1,0:T(8,128)(2,1)S(1)}, u32[]{:S(2)}, u32[]{:S(2)}) collective-permute-start(bf16[2,176,256]{2,1,0:T(8,128)(2,1)S(1)} %pad_maximum_fusion.refs_3_), channel_id=1, source_target_pairs={{0,4},{4,0},{8,12},{12,8},{16,20},{20,16},{24,28},{28,24},{32,36},... | collective-permute-start | bytes 540680 | tf_op jit(solution)/shard_map/ppermute | solution.py:56
  94.2 1.9 %collective-permute-start.29 = (bf16[2,176,256]{2,1,0:T(8,128)(2,1)S(1)}, bf16[2,176,256]{2,1,0:T(8,128)(2,1)S(1)}, u32[]{:S(2)}, u32[]{:S(2)}) collective-permute-start(bf16[2,176,256]{2,1,0:T(8,128)(2,1)S(1)} %collective-permute-done.25.refs_4_), channel_id=1, source_target_pairs={{0,4},{4,0},{8,12},{12,8},{16,20},{20,16},{24,28},{28,24},{32,36},... | collective-permute-start | bytes 540680 | tf_op jit(solution)/shard_map/ppermute | solution.py:56
  96.1 3.4 %collective-permute-start.30 = (bf16[2,176,256]{2,1,0:T(8,128)(2,1)S(1)}, bf16[2,176,256]{2,1,0:T(8,128)(2,1)S(1)}, u32[]{:S(2)}, u32[]{:S(2)}) collective-permute-start(bf16[2,176,256]{2,1,0:T(8,128)(2,1)S(1)} %collective-permute-done.26.refs_5_), channel_id=1, source_target_pairs={{0,4},{4,0},{8,12},{12,8},{16,20},{20,16},{24,28},{28,24},{32,36},... | collective-permute-start | bytes 540680 | tf_op jit(solution)/shard_map/ppermute | solution.py:56
  (51 shorter events, 20.9 us)
Async XLA Ops:
  2.3 9.4 %collective-permute-start.9 = (bf16[2,552,128]{2,1,0:T(8,128)(2,1)S(1)}, bf16[2,552,128]{2,1,0:T(8,128)(2,1)S(1)}, u32[]{:S(2)}, u32[]{:S(2)}) collective-permute-start(bf16[2,552,128]{2,1,0:T(8,128)(2,1)S(1)} %get-tuple-element.31), channel_id=1, source_target_pairs={{0,40},{4,44},{8,48},{12,52},{16,56},{20,60},{24,32},{28,36},{32,8... | collective-permute-start | bytes 847880 | tf_op jit(solution)/shard_map/ppermute | solution.py:56
  5.8 11.5 %collective-permute-start.11 = (bf16[2,552,128]{2,1,0:T(8,128)(2,1)S(1)}, bf16[2,552,128]{2,1,0:T(8,128)(2,1)S(1)}, u32[]{:S(2)}, u32[]{:S(2)}) collective-permute-start(bf16[2,552,128]{2,1,0:T(8,128)(2,1)S(1)} %get-tuple-element.32), channel_id=1, source_target_pairs={{0,24},{4,28},{8,0},{12,4},{16,8},{20,12},{24,16},{28,20},{32,56},... | collective-permute-start | bytes 847880 | tf_op jit(solution)/shard_map/ppermute | solution.py:56
  7.2 11.6 %collective-permute-start.13 = (bf16[2,552,128]{2,1,0:T(8,128)(2,1)S(1)}, bf16[2,552,128]{2,1,0:T(8,128)(2,1)S(1)}, u32[]{:S(2)}, u32[]{:S(2)}) collective-permute-start(bf16[2,552,128]{2,1,0:T(8,128)(2,1)S(1)} %get-tuple-element.33), channel_id=1, source_target_pairs={{0,56},{4,60},{8,32},{12,36},{16,40},{20,44},{24,48},{28,52},{32,2... | collective-permute-start | bytes 847880 | tf_op jit(solution)/shard_map/ppermute | solution.py:56
  8.0 18.2 %collective-permute-start.5 = (bf16[2,552,128]{2,1,0:T(8,128)(2,1)S(1)}, bf16[2,552,128]{2,1,0:T(8,128)(2,1)S(1)}, u32[]{:S(2)}, u32[]{:S(2)}) collective-permute-start(bf16[2,552,128]{2,1,0:T(8,128)(2,1)S(1)} %get-tuple-element.29), channel_id=1, source_target_pairs={{0,48},{4,52},{8,56},{12,60},{16,32},{20,36},{24,40},{28,44},{32,1... | collective-permute-start | bytes 847880 | tf_op jit(solution)/shard_map/ppermute | solution.py:56
  9.9 21.3 %collective-permute-start.7 = (bf16[2,552,128]{2,1,0:T(8,128)(2,1)S(1)}, bf16[2,552,128]{2,1,0:T(8,128)(2,1)S(1)}, u32[]{:S(2)}, u32[]{:S(2)}) collective-permute-start(bf16[2,552,128]{2,1,0:T(8,128)(2,1)S(1)} %get-tuple-element.30), channel_id=1, source_target_pairs={{0,8},{4,12},{8,16},{12,20},{16,24},{20,28},{24,0},{28,4},{32,40},... | collective-permute-start | bytes 847880 | tf_op jit(solution)/shard_map/ppermute | solution.py:56
  11.7 19.6 %collective-permute-start.4 = (bf16[2,552,128]{2,1,0:T(8,128)(2,1)S(1)}, bf16[2,552,128]{2,1,0:T(8,128)(2,1)S(1)}, u32[]{:S(2)}, u32[]{:S(2)}) collective-permute-start(bf16[2,552,128]{2,1,0:T(8,128)(2,1)S(1)} %get-tuple-element.28.refs_0_), channel_id=1, source_target_pairs={{0,4},{4,0},{8,12},{12,8},{16,20},{20,16},{24,28},{28,24},{32,36},... | collective-permute-start | bytes 847880 | tf_op jit(solution)/shard_map/ppermute | solution.py:56
  17.3 14.4 %collective-permute-start = (bf16[2,552,128]{2,1,0:T(8,128)(2,1)S(1)}, bf16[2,552,128]{2,1,0:T(8,128)(2,1)S(1)}, u32[]{:S(2)}, u32[]{:S(2)}) collective-permute-start(bf16[2,552,128]{2,1,0:T(8,128)(2,1)S(1)} %get-tuple-element.26), channel_id=1, source_target_pairs={{0,16},{4,20},{8,24},{12,28},{16,0},{20,4},{24,8},{28,12},{32,48},... | collective-permute-start | bytes 847880 | tf_op jit(solution)/shard_map/ppermute | solution.py:56
  18.8 18.7 %collective-permute-start.2 = (bf16[2,552,128]{2,1,0:T(8,128)(2,1)S(1)}, bf16[2,552,128]{2,1,0:T(8,128)(2,1)S(1)}, u32[]{:S(2)}, u32[]{:S(2)}) collective-permute-start(bf16[2,552,128]{2,1,0:T(8,128)(2,1)S(1)} %get-tuple-element.27), channel_id=1, source_target_pairs={{0,32},{4,36},{8,40},{12,44},{16,48},{20,52},{24,56},{28,60},{32,0... | collective-permute-start | bytes 847880 | tf_op jit(solution)/shard_map/ppermute | solution.py:56
  26.3 11.4 %collective-permute-start.10 = (bf16[2,552,128]{2,1,0:T(8,128)(2,1)S(1)}, bf16[2,552,128]{2,1,0:T(8,128)(2,1)S(1)}, u32[]{:S(2)}, u32[]{:S(2)}) collective-permute-start(bf16[2,552,128]{2,1,0:T(8,128)(2,1)S(1)} %collective-permute-done.9.refs_6_), channel_id=1, source_target_pairs={{0,4},{4,0},{8,12},{12,8},{16,20},{20,16},{24,28},{28,24},{32,36},... | collective-permute-start | bytes 847880 | tf_op jit(solution)/shard_map/ppermute | solution.py:56
  31.2 6.8 %collective-permute-start.12 = (bf16[2,552,128]{2,1,0:T(8,128)(2,1)S(1)}, bf16[2,552,128]{2,1,0:T(8,128)(2,1)S(1)}, u32[]{:S(2)}, u32[]{:S(2)}) collective-permute-start(bf16[2,552,128]{2,1,0:T(8,128)(2,1)S(1)} %collective-permute-done.11.refs_8_), channel_id=1, source_target_pairs={{0,4},{4,0},{8,12},{12,8},{16,20},{20,16},{24,28},{28,24},{32,36},... | collective-permute-start | bytes 847880 | tf_op jit(solution)/shard_map/ppermute | solution.py:56
  31.3 6.9 %collective-permute-start.14 = (bf16[2,552,128]{2,1,0:T(8,128)(2,1)S(1)}, bf16[2,552,128]{2,1,0:T(8,128)(2,1)S(1)}, u32[]{:S(2)}, u32[]{:S(2)}) collective-permute-start(bf16[2,552,128]{2,1,0:T(8,128)(2,1)S(1)} %collective-permute-done.13.refs_10_), channel_id=1, source_target_pairs={{0,4},{4,0},{8,12},{12,8},{16,20},{20,16},{24,28},{28,24},{32,36},... | collective-permute-start | bytes 847880 | tf_op jit(solution)/shard_map/ppermute | solution.py:56
  31.7 6.9 %collective-permute-start.6 = (bf16[2,552,128]{2,1,0:T(8,128)(2,1)S(1)}, bf16[2,552,128]{2,1,0:T(8,128)(2,1)S(1)}, u32[]{:S(2)}, u32[]{:S(2)}) collective-permute-start(bf16[2,552,128]{2,1,0:T(8,128)(2,1)S(1)} %collective-permute-done.5.refs_2_), channel_id=1, source_target_pairs={{0,4},{4,0},{8,12},{12,8},{16,20},{20,16},{24,28},{28,24},{32,36},... | collective-permute-start | bytes 847880 | tf_op jit(solution)/shard_map/ppermute | solution.py:56
  37.7 6.0 %collective-permute-start.1 = (bf16[2,552,128]{2,1,0:T(8,128)(2,1)S(1)}, bf16[2,552,128]{2,1,0:T(8,128)(2,1)S(1)}, u32[]{:S(2)}, u32[]{:S(2)}) collective-permute-start(bf16[2,552,128]{2,1,0:T(8,128)(2,1)S(1)} %collective-permute-done.refs_0_), channel_id=1, source_target_pairs={{0,4},{4,0},{8,12},{12,8},{16,20},{20,16},{24,28},{28,24},{32,36},... | collective-permute-start | bytes 847880 | tf_op jit(solution)/shard_map/ppermute | solution.py:56
  38.0 5.8 %collective-permute-start.3 = (bf16[2,552,128]{2,1,0:T(8,128)(2,1)S(1)}, bf16[2,552,128]{2,1,0:T(8,128)(2,1)S(1)}, u32[]{:S(2)}, u32[]{:S(2)}) collective-permute-start(bf16[2,552,128]{2,1,0:T(8,128)(2,1)S(1)} %collective-permute-done.2.refs_2_), channel_id=1, source_target_pairs={{0,4},{4,0},{8,12},{12,8},{16,20},{20,16},{24,28},{28,24},{32,36},... | collective-permute-start | bytes 847880 | tf_op jit(solution)/shard_map/ppermute | solution.py:56
  44.1 6.4 %collective-permute-start.15 = (bf16[128,256]{1,0:T(8,128)(2,1)S(1)}, bf16[128,256]{1,0:T(8,128)(2,1)S(1)}, u32[]{:S(2)}, u32[]{:S(2)}) collective-permute-start(bf16[128,256]{1,0:T(8,128)(2,1)S(1)} %get-tuple-element.41.refs_0_), channel_id=1, source_target_pairs={{0,64},{4,68},{8,72},{12,76},{16,80},{20,84},{24,88},{28,92},{32,9... | collective-permute-start | bytes 196616 | tf_op jit(solution)/shard_map/ppermute | solution.py:56
  52.5 7.0 %collective-permute-start.17 = (bf16[128,256]{1,0:T(8,128)(2,1)S(1)}, bf16[128,256]{1,0:T(8,128)(2,1)S(1)}, u32[]{:S(2)}, u32[]{:S(2)}) collective-permute-start(bf16[128,256]{1,0:T(8,128)(2,1)S(1)} %get-tuple-element.43.refs_0_), channel_id=1, source_target_pairs={{0,192},{4,196},{8,200},{12,204},{16,208},{20,212},{24,216},{28,22... | collective-permute-start | bytes 196616 | tf_op jit(solution)/shard_map/ppermute | solution.py:56
  61.7 6.5 %collective-permute-start.19 = (bf16[168,256]{1,0:T(8,128)(2,1)S(1)}, bf16[168,256]{1,0:T(8,128)(2,1)S(1)}, u32[]{:S(2)}, u32[]{:S(2)}) collective-permute-start(bf16[168,256]{1,0:T(8,128)(2,1)S(1)} %shard_map.51.s0), channel_id=1, source_target_pairs={{0,64},{4,68},{8,72},{12,76},{16,80},{20,84},{24,88},{28,92},{32,9... | collective-permute-start | bytes 258056 | tf_op jit(solution)/shard_map/ppermute | solution.py:56
  62.2 8.2 %collective-permute-start.20 = (bf16[168,256]{1,0:T(8,128)(2,1)S(1)}, bf16[168,256]{1,0:T(8,128)(2,1)S(1)}, u32[]{:S(2)}, u32[]{:S(2)}) collective-permute-start(bf16[168,256]{1,0:T(8,128)(2,1)S(1)} %shard_map.51.s0), channel_id=1, source_target_pairs={{0,128},{4,132},{8,136},{12,140},{16,144},{20,148},{24,152},{28,15... | collective-permute-start | bytes 258056 | tf_op jit(solution)/shard_map/ppermute | solution.py:56
  65.0 7.4 %collective-permute-start.21 = (bf16[168,256]{1,0:T(8,128)(2,1)S(1)}, bf16[168,256]{1,0:T(8,128)(2,1)S(1)}, u32[]{:S(2)}, u32[]{:S(2)}) collective-permute-start(bf16[168,256]{1,0:T(8,128)(2,1)S(1)} %shard_map.51.s0), channel_id=1, source_target_pairs={{0,192},{4,196},{8,200},{12,204},{16,208},{20,212},{24,216},{28,22... | collective-permute-start | bytes 258056 | tf_op jit(solution)/shard_map/ppermute | solution.py:56
  82.5 11.7 %collective-permute-start.25 = (bf16[2,176,256]{2,1,0:T(8,128)(2,1)S(1)}, bf16[2,176,256]{2,1,0:T(8,128)(2,1)S(1)}, u32[]{:S(2)}, u32[]{:S(2)}) collective-permute-start(bf16[2,176,256]{2,1,0:T(8,128)(2,1)S(1)} %pad_maximum_fusion.refs_3_), channel_id=1, source_target_pairs={{0,8},{4,12},{8,16},{12,20},{16,24},{20,28},{24,0},{28,4},{32,40},... | collective-permute-start | bytes 540680 | tf_op jit(solution)/shard_map/ppermute | solution.py:56
  84.2 11.9 %collective-permute-start.26 = (bf16[2,176,256]{2,1,0:T(8,128)(2,1)S(1)}, bf16[2,176,256]{2,1,0:T(8,128)(2,1)S(1)}, u32[]{:S(2)}, u32[]{:S(2)}) collective-permute-start(bf16[2,176,256]{2,1,0:T(8,128)(2,1)S(1)} %pad_maximum_fusion.refs_3_), channel_id=1, source_target_pairs={{0,16},{4,20},{8,24},{12,28},{16,0},{20,4},{24,8},{28,12},{32,48},... | collective-permute-start | bytes 540680 | tf_op jit(solution)/shard_map/ppermute | solution.py:56
  86.4 13.1 %collective-permute-start.27 = (bf16[2,176,256]{2,1,0:T(8,128)(2,1)S(1)}, bf16[2,176,256]{2,1,0:T(8,128)(2,1)S(1)}, u32[]{:S(2)}, u32[]{:S(2)}) collective-permute-start(bf16[2,176,256]{2,1,0:T(8,128)(2,1)S(1)} %pad_maximum_fusion.refs_3_), channel_id=1, source_target_pairs={{0,24},{4,28},{8,0},{12,4},{16,8},{20,12},{24,16},{28,20},{32,56},... | collective-permute-start | bytes 540680 | tf_op jit(solution)/shard_map/ppermute | solution.py:56
  86.7 12.9 %collective-permute-start.28 = (bf16[2,176,256]{2,1,0:T(8,128)(2,1)S(1)}, bf16[2,176,256]{2,1,0:T(8,128)(2,1)S(1)}, u32[]{:S(2)}, u32[]{:S(2)}) collective-permute-start(bf16[2,176,256]{2,1,0:T(8,128)(2,1)S(1)} %pad_maximum_fusion.refs_3_), channel_id=1, source_target_pairs={{0,4},{4,0},{8,12},{12,8},{16,20},{20,16},{24,28},{28,24},{32,36},... | collective-permute-start | bytes 540680 | tf_op jit(solution)/shard_map/ppermute | solution.py:56
  94.2 5.4 %collective-permute-start.29 = (bf16[2,176,256]{2,1,0:T(8,128)(2,1)S(1)}, bf16[2,176,256]{2,1,0:T(8,128)(2,1)S(1)}, u32[]{:S(2)}, u32[]{:S(2)}) collective-permute-start(bf16[2,176,256]{2,1,0:T(8,128)(2,1)S(1)} %collective-permute-done.25.refs_4_), channel_id=1, source_target_pairs={{0,4},{4,0},{8,12},{12,8},{16,20},{20,16},{24,28},{28,24},{32,36},... | collective-permute-start | bytes 540680 | tf_op jit(solution)/shard_map/ppermute | solution.py:56
  (8 other events, 27.0 us)

commit v6 on v5

--- a/solution.py
+++ b/solution.py
@@ -9,7 +9,7 @@
 Z, X, C = 8, 4, 2
 CLUSTERS = Z * X * C
 ROWS = 176
-EARLY = 6
+EARLY = 4
 ROOM = 16 * 1024 * 1024
 BF, F32 = jnp.bfloat16, jnp.float32
 
@@ -36,7 +36,7 @@
     ]
 
 
-SLOTS = ((0, 0), (2, 1), (1, 0), (1, 1), (3, 0), (3, 1), (2, 0), (0, 1))
+SLOTS = ((0, 0), (1, 0), (3, 0), (0, 1), (2, 0), (1, 1), (3, 1), (2, 1))
 
 
 def ring_step(turn, count, spread):
@@ -46,10 +46,6 @@
 
 def on_z_ring(turn):
     return ring_step(turn, 2 * X * C, lambda q, n: place(2 * q + n // (X * C), n // C % X, n % C))
-
-
-def on_sub_ring(turn):
-    return ring_step(turn, 1, lambda y, n: y)
 
 
 def moved(value, pairs):
@@ -245,8 +241,8 @@
     power_ref[...] = power[:, 0:128] + power[:, 128:256]
 
 
-def tail_kernel(value_ref, p0, p1, out_ref):
-    power = p0[...] + p1[...]
+def tail_kernel(value_ref, p0, p1, p2, p3, out_ref):
+    power = (p0[...] + p2[...]) + (p1[...] + p3[...])
     row = lax.broadcasted_iota(jnp.int32, (8, 256), 0)
     tail = jnp.zeros((8, 256), F32)
     for k in range(3):
@@ -258,16 +254,12 @@
 
 
 def finish_kernel(vectors, x_ref, pair_ref, c_ref, *refs):
-    parts, out_ref, rows, held, sems = refs[:8], refs[8], refs[9], refs[10], refs[11]
+    parts, (out_ref, rows, held, sems) = refs[:16], refs[16:]
     x, pair, c = x_ref[0], pair_ref[0], c_ref[0]
-    blocks = [
-        side * 8 + lax.rem(x + X - d, X) * 2 + parity
-        for side in (c, 1 - c)
-        for d in range(X)
-        for parity in (pair, 1 - pair)
-    ]
+    order = [(0, pair), (0, 1 - pair)] + [(d, parity) for parity in (pair, 1 - pair) for d in (1, 3, 2)]
+    blocks = [side * 8 + lax.rem(x + X - d, X) * 2 + parity for side in (c, 1 - c) for d, parity in order]
     for k in range(16):
-        tail = parts[k // 2][k % 2, 168:176, :].astype(F32)
+        tail = parts[k][168:176, :].astype(F32)
         power = (tail[0:1, :] + tail[1:2, :]) + tail[2:3, :]
         rows[blocks[k]] = power[:, 0:128]
     power = rows[0]
@@ -277,7 +269,7 @@
     factor = jnp.concatenate([factor, factor], axis=1)
     stores = []
     for k in range(16):
-        value = parts[k // 2][k % 2, 0:168, :].astype(F32) * factor
+        value = parts[k][0:168, :].astype(F32) * factor
         held[k] = value.astype(BF)
         stores.append(pltpu.make_async_copy(held.at[k], out_ref.at[blocks[k]], sems.at[k]))
         stores[k].start()
@@ -317,12 +309,15 @@
     for d in (2, 1, 3):
         shares[d] = moved(share, shifted(dz=2 * d))
     value, power = whole(consensus_kernel, shares, [near(SUM, BF), near((1, 128), F32)])
-    near_power = lax.ppermute(power, "sub", on_sub_ring(0))
-    power = whole(pair_kernel, (power, near_power), near((1, 128), F32))
-    far_power = lax.ppermute(power, "sub", on_sub_ring(1))
-    mine = whole(tail_kernel, (value, power, far_power), near((ROWS, 256), BF))
-    both = jnp.stack([mine, moved(mine, pair_shifted(0, 1))])
-    same = [both] + [moved(both, shifted(dx=d)) for d in (1, 2, 3)]
+    powers = [power, power, power, power]
+    for d in (2, 1, 3):
+        powers[d] = lax.ppermute(power, "sub", [(y, (y + d) % 4) for y in range(4)])
+    mine = whole(tail_kernel, (value, *powers), near((ROWS, 256), BF))
+    theirs = moved(mine, pair_shifted(0, 1))
+    same = [mine, theirs]
+    for value in (mine, theirs):
+        for d in (1, 3, 2):
+            same.append(moved(value, shifted(dx=d)))
     other = [moved(part, shifted(dc=1)) for part in same]
     total = blocks * lax.axis_size("sub") * vectors
     return whole(

time: 102 us -> 98.8 us (0.969)
  the two profiles are of different devices: /device:TPU:1 before, /device:TPU:2 now
where the time goes in v6:
time: 98.8 us; the launch traced here: 97.2 us
  starting transfers between devices  54.9 us (56%)
  waiting for transfers between devices  32.3 us (33%)
  Pallas kernels  9.73 us (10%)
    ppermute x37, starting transfers between devices, moved(): return lax.ppermute(value, 'cluster', pairs)  48.9 us
    ppermute x37, waiting for transfers between devices, moved(): return lax.ppermute(value, 'cluster', pairs)  30.1 us
    pallas_call x9, Pallas kernels, whole(): pl.pallas_call(kernel, in_specs=[pl.BlockSpec(memory_space=pltpu.SMEM if...  9.73 us
    ppermute x3, starting transfers between devices, per_device(): powers[d] = lax.ppermute(power, 'sub', [(y, (y + d) % 4) for y in range(4)])  5.91 us
    ppermute x3, waiting for transfers between devices, per_device(): powers[d] = lax.ppermute(power, 'sub', [(y, (y + d) % 4) for y in range(4)])  2.22 us
  transfers between devices with their start and end apart: 40, of which 16 were waited for; matrix products, arithmetic and copies ran while one was open for 0% of the time, Pallas kernels for 5%

profile of v6, /device:TPU:2, one launch (start us, length us, event | category | flops | bytes accessed | tf_op | source)
XLA Modules:
  0.0 97.2 jit_solution(9393053981319351901)
XLA Ops:
  0.0 2.3 %shard_map.46 = (bf16[2,552,128]{2,1,0:T(8,128)(2,1)S(1)}, bf16[2,552,128]{2,1,0:T(8,128)(2,1)S(1)}, bf16[2,552,128]{2,1,0:T(8,128)(2,1)S(1)}, bf16[2,552,128]{2...) custom-call(s32[1]{0:T(128)} %bitcast.x_ref.refs_0_, ...), custom_call_target="tpu_custom_call" | custom-call | flops 6000000 | bytes 5000000 | tf_op jit(solution)/shard_map/pallas_call | solution.py:105
  6.3 2.1 %collective-permute-start = (bf16[2,552,128]{2,1,0:T(8,128)(2,1)S(1)}, bf16[2,552,128]{2,1,0:T(8,128)(2,1)S(1)}, u32[]{:S(2)}, u32[]{:S(2)}) collective-permute-start(bf16[2,552,128]{2,1,0:T(8,128)(2,1)S(1)} %get-tuple-element.26), channel_id=1, source_target_pairs={{0,16},{4,20},{8,24},{12,28},{16,0},{20,4},{24,8},{28,12},{32,48},... | collective-permute-start | bytes 847880 | tf_op jit(solution)/shard_map/ppermute | solution.py:52
  8.5 2.4 %collective-permute-done.9.refs_2_ = bf16[2,552,128]{2,1,0:T(8,128)(2,1)S(1)} collective-permute-done((bf16[2,552,128]{2,1,0:T(8,128)(2,1)S(1)}, bf16[2,552,128]{2,1,0:T(8,128)(2,1)S(1)}, u32[]{:S(2)}, u32[]{:S(2)}) %collective-permute-start.9) | collective-permute-done | bytes 282656 | tf_op jit(solution)/shard_map/ppermute | solution.py:52
  10.9 4.0 %collective-permute-start.2 = (bf16[2,552,128]{2,1,0:T(8,128)(2,1)S(1)}, bf16[2,552,128]{2,1,0:T(8,128)(2,1)S(1)}, u32[]{:S(2)}, u32[]{:S(2)}) collective-permute-start(bf16[2,552,128]{2,1,0:T(8,128)(2,1)S(1)} %get-tuple-element.27), channel_id=1, source_target_pairs={{0,40},{4,44},{8,48},{12,52},{16,56},{20,60},{24,32},{28,36},{32,8... | collective-permute-start | bytes 847880 | tf_op jit(solution)/shard_map/ppermute | solution.py:52
  14.9 6.0 %collective-permute-start.4 = (bf16[2,552,128]{2,1,0:T(8,128)(2,1)S(1)}, bf16[2,552,128]{2,1,0:T(8,128)(2,1)S(1)}, u32[]{:S(2)}, u32[]{:S(2)}) collective-permute-start(bf16[2,552,128]{2,1,0:T(8,128)(2,1)S(1)} %get-tuple-element.28), channel_id=1, source_target_pairs={{0,56},{4,60},{8,32},{12,36},{16,40},{20,44},{24,48},{28,52},{32,2... | collective-permute-start | bytes 847880 | tf_op jit(solution)/shard_map/ppermute | solution.py:52
  20.8 2.7 %collective-permute-start.6 = (bf16[2,552,128]{2,1,0:T(8,128)(2,1)S(1)}, bf16[2,552,128]{2,1,0:T(8,128)(2,1)S(1)}, u32[]{:S(2)}, u32[]{:S(2)}) collective-permute-start(bf16[2,552,128]{2,1,0:T(8,128)(2,1)S(1)} %get-tuple-element.29), channel_id=1, source_target_pairs={{0,48},{4,52},{8,56},{12,60},{16,32},{20,36},{24,40},{28,44},{32,1... | collective-permute-start | bytes 847880 | tf_op jit(solution)/shard_map/ppermute | solution.py:52
  24.1 5.4 %collective-permute-done.4.refs_4_ = bf16[2,552,128]{2,1,0:T(8,128)(2,1)S(1)} collective-permute-done((bf16[2,552,128]{2,1,0:T(8,128)(2,1)S(1)}, bf16[2,552,128]{2,1,0:T(8,128)(2,1)S(1)}, u32[]{:S(2)}, u32[]{:S(2)}) %collective-permute-start.4) | collective-permute-done | bytes 282656 | tf_op jit(solution)/shard_map/ppermute | solution.py:52
  29.5 3.6 %collective-permute-done.6.refs_6_ = bf16[2,552,128]{2,1,0:T(8,128)(2,1)S(1)} collective-permute-done((bf16[2,552,128]{2,1,0:T(8,128)(2,1)S(1)}, bf16[2,552,128]{2,1,0:T(8,128)(2,1)S(1)}, u32[]{:S(2)}, u32[]{:S(2)}) %collective-permute-start.6) | collective-permute-done | bytes 282656 | tf_op jit(solution)/shard_map/ppermute | solution.py:52
  33.7 3.2 %shard_map.47 = (f32[168,256]{1,0:T(8,128)S(1)}, f32[168,256]{1,0:T(8,128)S(1)}, f32[168,256]{1,0:T(8,128)S(1)}, f32[256,256]{1,0:T(8,128)S(1)}) custom-call(bf16[2,552,128]{2,1,0:T(8,128)(2,1)S(1)} %get-tuple-element.30.refs_0_, bf16[2,552,128]{2,1,0:T(8,128)(2,1)S(1)} %collective-permute-done.8.refs_1_, ...), custom_call_target="tpu_custom_call" | custom-call | flops 2000000000 | bytes 3000000 | tf_op jit(solution)/shard_map/pallas_call | solution.py:105
  37.3 3.5 %collective-permute-start.15 = (bf16[128,256]{1,0:T(8,128)(2,1)S(1)}, bf16[128,256]{1,0:T(8,128)(2,1)S(1)}, u32[]{:S(2)}, u32[]{:S(2)}) collective-permute-start(bf16[128,256]{1,0:T(8,128)(2,1)S(1)} %get-tuple-element.41.refs_0_), channel_id=1, source_target_pairs={{0,64},{4,68},{8,72},{12,76},{16,80},{20,84},{24,88},{28,92},{32,9... | collective-permute-start | bytes 196616 | tf_op jit(solution)/shard_map/ppermute | solution.py:52
  40.9 4.5 %collective-permute-start.16 = (bf16[128,256]{1,0:T(8,128)(2,1)S(1)}, bf16[128,256]{1,0:T(8,128)(2,1)S(1)}, u32[]{:S(2)}, u32[]{:S(2)}) collective-permute-start(bf16[128,256]{1,0:T(8,128)(2,1)S(1)} %get-tuple-element.42.refs_1_), channel_id=1, source_target_pairs={{0,192},{4,196},{8,200},{12,204},{16,208},{20,212},{24,216},{28,22... | collective-permute-start | bytes 196616 | tf_op jit(solution)/shard_map/ppermute | solution.py:52
  45.4 3.1 %collective-permute-done.16.refs_3_ = bf16[128,256]{1,0:T(8,128)(2,1)S(1)} collective-permute-done((bf16[128,256]{1,0:T(8,128)(2,1)S(1)}, bf16[128,256]{1,0:T(8,128)(2,1)S(1)}, u32[]{:S(2)}, u32[]{:S(2)}) %collective-permute-start.16) | collective-permute-done | bytes 65568 | tf_op jit(solution)/shard_map/ppermute | solution.py:52
  48.5 4.8 %collective-permute-start.17 = (bf16[128,256]{1,0:T(8,128)(2,1)S(1)}, bf16[128,256]{1,0:T(8,128)(2,1)S(1)}, u32[]{:S(2)}, u32[]{:S(2)}) collective-permute-start(bf16[128,256]{1,0:T(8,128)(2,1)S(1)} %get-tuple-element.43.refs_0_), channel_id=1, source_target_pairs={{0,192},{4,196},{8,200},{12,204},{16,208},{20,212},{24,216},{28,22... | collective-permute-start | bytes 196616 | tf_op jit(solution)/shard_map/ppermute | solution.py:52
  53.5 2.1 %shard_map.48 = (f32[168,256]{1,0:T(8,128)S(1)}, f32[168,256]{1,0:T(8,128)S(1)}, f32[168,256]{1,0:T(8,128)S(1)}) custom-call(bf16[2,552,128]{2,1,0:T(8,128)(2,1)S(1)} %collective-permute-done.refs_0_, bf16[2,552,128]{2,1,0:T(8,128)(2,1)S(1)} %collective-permute-done.1.refs_1_, bf16[2,552,128]{2,1,0:T(8,128)(2,1)S(1)} %collective-permute-done.2.refs_2_, ...), custom_call_target="tpu_custom_call" | custom-call | flops 2000000000 | bytes 3000000 | tf_op jit(solution)/shard_map/pallas_call | solution.py:105
  55.6 2.8 %collective-permute-done.18.refs_3_ = bf16[128,256]{1,0:T(8,128)(2,1)S(1)} collective-permute-done((bf16[128,256]{1,0:T(8,128)(2,1)S(1)}, bf16[128,256]{1,0:T(8,128)(2,1)S(1)}, u32[]{:S(2)}, u32[]{:S(2)}) %collective-permute-start.18) | collective-permute-done | bytes 65568 | tf_op jit(solution)/shard_map/ppermute | solution.py:52
  60.2 2.4 %collective-permute-start.20 = (bf16[168,256]{1,0:T(8,128)(2,1)S(1)}, bf16[168,256]{1,0:T(8,128)(2,1)S(1)}, u32[]{:S(2)}, u32[]{:S(2)}) collective-permute-start(bf16[168,256]{1,0:T(8,128)(2,1)S(1)} %shard_map.51.s0), channel_id=1, source_target_pairs={{0,128},{4,132},{8,136},{12,140},{16,144},{20,148},{24,152},{28,15... | collective-permute-start | bytes 258056 | tf_op jit(solution)/shard_map/ppermute | solution.py:52
  62.5 2.0 %collective-permute-start.21 = (bf16[168,256]{1,0:T(8,128)(2,1)S(1)}, bf16[168,256]{1,0:T(8,128)(2,1)S(1)}, u32[]{:S(2)}, u32[]{:S(2)}) collective-permute-start(bf16[168,256]{1,0:T(8,128)(2,1)S(1)} %shard_map.51.s0), channel_id=1, source_target_pairs={{0,192},{4,196},{8,200},{12,204},{16,208},{20,212},{24,216},{28,22... | collective-permute-start | bytes 258056 | tf_op jit(solution)/shard_map/ppermute | solution.py:52
  64.5 2.0 %collective-permute-done.19.s1 = bf16[168,256]{1,0:T(8,128)(2,1)S(1)} collective-permute-done((bf16[168,256]{1,0:T(8,128)(2,1)S(1)}, bf16[168,256]{1,0:T(8,128)(2,1)S(1)}, u32[]{:S(2)}, u32[]{:S(2)}) %collective-permute-start.19) | collective-permute-done | bytes 86048 | tf_op jit(solution)/shard_map/ppermute | solution.py:52
  66.5 3.0 %collective-permute-done.20.s2 = bf16[168,256]{1,0:T(8,128)(2,1)S(1)} collective-permute-done((bf16[168,256]{1,0:T(8,128)(2,1)S(1)}, bf16[168,256]{1,0:T(8,128)(2,1)S(1)}, u32[]{:S(2)}, u32[]{:S(2)}) %collective-permute-start.20) | collective-permute-done | bytes 86048 | tf_op jit(solution)/shard_map/ppermute | solution.py:52
  69.6 2.2 %collective-permute-done.21.s3 = bf16[168,256]{1,0:T(8,128)(2,1)S(1)} collective-permute-done((bf16[168,256]{1,0:T(8,128)(2,1)S(1)}, bf16[168,256]{1,0:T(8,128)(2,1)S(1)}, u32[]{:S(2)}, u32[]{:S(2)}) %collective-permute-start.21) | collective-permute-done | bytes 86048 | tf_op jit(solution)/shard_map/ppermute | solution.py:52
  73.5 2.9 %collective-permute-start.23 = (f32[1,128]{1,0:T(1,128)S(1)}, f32[1,128]{1,0:T(1,128)S(1)}, u32[]{:S(2)}, u32[]{:S(2)}) collective-permute-start(f32[1,128]{1,0:T(1,128)S(1)} %get-tuple-element.46.p0), channel_id=1, source_target_pairs={{0,2},{1,3},{2,0},{3,1},{4,6},{5,7},{6,4},{7,5},{8,10},{9,11},{10,... | collective-permute-start | bytes 1544 | tf_op jit(solution)/shard_map/ppermute | solution.py:314
  82.2 2.7 %collective-permute-start.28 = (bf16[176,256]{1,0:T(8,128)(2,1)S(1)}, bf16[176,256]{1,0:T(8,128)(2,1)S(1)}, u32[]{:S(2)}, u32[]{:S(2)}) collective-permute-start(bf16[176,256]{1,0:T(8,128)(2,1)S(1)} %shard_map.53.refs_3_), channel_id=1, source_target_pairs={{0,16},{4,20},{8,24},{12,28},{16,0},{20,4},{24,8},{28,12},{32,48},... | collective-permute-start | bytes 270344 | tf_op jit(solution)/shard_map/ppermute | solution.py:52
  85.9 2.0 %collective-permute-start.30 = (bf16[176,256]{1,0:T(8,128)(2,1)S(1)}, bf16[176,256]{1,0:T(8,128)(2,1)S(1)}, u32[]{:S(2)}, u32[]{:S(2)}) collective-permute-start(bf16[176,256]{1,0:T(8,128)(2,1)S(1)} %collective-permute-done.25.refs_4_), channel_id=1, source_target_pairs={{0,24},{4,28},{8,0},{12,4},{16,8},{20,12},{24,16},{28,20},{32,56},... | collective-permute-start | bytes 270344 | tf_op jit(solution)/shard_map/ppermute | solution.py:52
  90.7 3.3 %collective-permute-done.31.refs_10_ = bf16[176,256]{1,0:T(8,128)(2,1)S(1)} collective-permute-done((bf16[176,256]{1,0:T(8,128)(2,1)S(1)}, bf16[176,256]{1,0:T(8,128)(2,1)S(1)}, u32[]{:S(2)}, u32[]{:S(2)}) %collective-permute-start.31) | collective-permute-done | bytes 90144 | tf_op jit(solution)/shard_map/ppermute | solution.py:52
  (65 shorter events, 22.0 us)
Async XLA Ops:
  2.3 8.6 %collective-permute-start.9 = (bf16[2,552,128]{2,1,0:T(8,128)(2,1)S(1)}, bf16[2,552,128]{2,1,0:T(8,128)(2,1)S(1)}, u32[]{:S(2)}, u32[]{:S(2)}) collective-permute-start(bf16[2,552,128]{2,1,0:T(8,128)(2,1)S(1)} %get-tuple-element.31), channel_id=1, source_target_pairs={{0,8},{4,12},{8,16},{12,20},{16,24},{20,28},{24,0},{28,4},{32,40},... | collective-permute-start | bytes 847880 | tf_op jit(solution)/shard_map/ppermute | solution.py:52
  3.9 11.0 %collective-permute-start.11 = (bf16[2,552,128]{2,1,0:T(8,128)(2,1)S(1)}, bf16[2,552,128]{2,1,0:T(8,128)(2,1)S(1)}, u32[]{:S(2)}, u32[]{:S(2)}) collective-permute-start(bf16[2,552,128]{2,1,0:T(8,128)(2,1)S(1)} %get-tuple-element.32), channel_id=1, source_target_pairs={{0,24},{4,28},{8,0},{12,4},{16,8},{20,12},{24,16},{28,20},{32,56},... | collective-permute-start | bytes 847880 | tf_op jit(solution)/shard_map/ppermute | solution.py:52
  4.7 16.1 %collective-permute-start.13 = (bf16[2,552,128]{2,1,0:T(8,128)(2,1)S(1)}, bf16[2,552,128]{2,1,0:T(8,128)(2,1)S(1)}, u32[]{:S(2)}, u32[]{:S(2)}) collective-permute-start(bf16[2,552,128]{2,1,0:T(8,128)(2,1)S(1)} %get-tuple-element.33), channel_id=1, source_target_pairs={{0,32},{4,36},{8,40},{12,44},{16,48},{20,52},{24,56},{28,60},{32,0... | collective-permute-start | bytes 847880 | tf_op jit(solution)/shard_map/ppermute | solution.py:52
  6.3 17.2 %collective-permute-start.8 = (bf16[2,552,128]{2,1,0:T(8,128)(2,1)S(1)}, bf16[2,552,128]{2,1,0:T(8,128)(2,1)S(1)}, u32[]{:S(2)}, u32[]{:S(2)}) collective-permute-start(bf16[2,552,128]{2,1,0:T(8,128)(2,1)S(1)} %get-tuple-element.30.refs_0_), channel_id=1, source_target_pairs={{0,4},{4,0},{8,12},{12,8},{16,20},{20,16},{24,28},{28,24},{32,36},... | collective-permute-start | bytes 847880 | tf_op jit(solution)/shard_map/ppermute | solution.py:52
  6.3 17.2 %collective-permute-start = (bf16[2,552,128]{2,1,0:T(8,128)(2,1)S(1)}, bf16[2,552,128]{2,1,0:T(8,128)(2,1)S(1)}, u32[]{:S(2)}, u32[]{:S(2)}) collective-permute-start(bf16[2,552,128]{2,1,0:T(8,128)(2,1)S(1)} %get-tuple-element.26), channel_id=1, source_target_pairs={{0,16},{4,20},{8,24},{12,28},{16,0},{20,4},{24,8},{28,12},{32,48},... | collective-permute-start | bytes 847880 | tf_op jit(solution)/shard_map/ppermute | solution.py:52
  10.9 13.1 %collective-permute-start.2 = (bf16[2,552,128]{2,1,0:T(8,128)(2,1)S(1)}, bf16[2,552,128]{2,1,0:T(8,128)(2,1)S(1)}, u32[]{:S(2)}, u32[]{:S(2)}) collective-permute-start(bf16[2,552,128]{2,1,0:T(8,128)(2,1)S(1)} %get-tuple-element.27), channel_id=1, source_target_pairs={{0,40},{4,44},{8,48},{12,52},{16,56},{20,60},{24,32},{28,36},{32,8... | collective-permute-start | bytes 847880 | tf_op jit(solution)/shard_map/ppermute | solution.py:52
  14.9 14.7 %collective-permute-start.4 = (bf16[2,552,128]{2,1,0:T(8,128)(2,1)S(1)}, bf16[2,552,128]{2,1,0:T(8,128)(2,1)S(1)}, u32[]{:S(2)}, u32[]{:S(2)}) collective-permute-start(bf16[2,552,128]{2,1,0:T(8,128)(2,1)S(1)} %get-tuple-element.28), channel_id=1, source_target_pairs={{0,56},{4,60},{8,32},{12,36},{16,40},{20,44},{24,48},{28,52},{32,2... | collective-permute-start | bytes 847880 | tf_op jit(solution)/shard_map/ppermute | solution.py:52
  20.8 12.3 %collective-permute-start.6 = (bf16[2,552,128]{2,1,0:T(8,128)(2,1)S(1)}, bf16[2,552,128]{2,1,0:T(8,128)(2,1)S(1)}, u32[]{:S(2)}, u32[]{:S(2)}) collective-permute-start(bf16[2,552,128]{2,1,0:T(8,128)(2,1)S(1)} %get-tuple-element.29), channel_id=1, source_target_pairs={{0,48},{4,52},{8,56},{12,60},{16,32},{20,36},{24,40},{28,44},{32,1... | collective-permute-start | bytes 847880 | tf_op jit(solution)/shard_map/ppermute | solution.py:52
  23.5 9.6 %collective-permute-start.10 = (bf16[2,552,128]{2,1,0:T(8,128)(2,1)S(1)}, bf16[2,552,128]{2,1,0:T(8,128)(2,1)S(1)}, u32[]{:S(2)}, u32[]{:S(2)}) collective-permute-start(bf16[2,552,128]{2,1,0:T(8,128)(2,1)S(1)} %collective-permute-done.9.refs_2_), channel_id=1, source_target_pairs={{0,4},{4,0},{8,12},{12,8},{16,20},{20,16},{24,28},{28,24},{32,36},... | collective-permute-start | bytes 847880 | tf_op jit(solution)/shard_map/ppermute | solution.py:52
  23.5 10.1 %collective-permute-start.12 = (bf16[2,552,128]{2,1,0:T(8,128)(2,1)S(1)}, bf16[2,552,128]{2,1,0:T(8,128)(2,1)S(1)}, u32[]{:S(2)}, u32[]{:S(2)}) collective-permute-start(bf16[2,552,128]{2,1,0:T(8,128)(2,1)S(1)} %collective-permute-done.11.refs_4_), channel_id=1, source_target_pairs={{0,4},{4,0},{8,12},{12,8},{16,20},{20,16},{24,28},{28,24},{32,36},... | collective-permute-start | bytes 847880 | tf_op jit(solution)/shard_map/ppermute | solution.py:52
  24.0 9.7 %collective-permute-start.14 = (bf16[2,552,128]{2,1,0:T(8,128)(2,1)S(1)}, bf16[2,552,128]{2,1,0:T(8,128)(2,1)S(1)}, u32[]{:S(2)}, u32[]{:S(2)}) collective-permute-start(bf16[2,552,128]{2,1,0:T(8,128)(2,1)S(1)} %collective-permute-done.13.refs_6_), channel_id=1, source_target_pairs={{0,4},{4,0},{8,12},{12,8},{16,20},{20,16},{24,28},{28,24},{32,36},... | collective-permute-start | bytes 847880 | tf_op jit(solution)/shard_map/ppermute | solution.py:52
  29.5 7.4 %collective-permute-start.1 = (bf16[2,552,128]{2,1,0:T(8,128)(2,1)S(1)}, bf16[2,552,128]{2,1,0:T(8,128)(2,1)S(1)}, u32[]{:S(2)}, u32[]{:S(2)}) collective-permute-start(bf16[2,552,128]{2,1,0:T(8,128)(2,1)S(1)} %collective-permute-done.refs_0_), channel_id=1, source_target_pairs={{0,4},{4,0},{8,12},{12,8},{16,20},{20,16},{24,28},{28,24},{32,36},... | collective-permute-start | bytes 847880 | tf_op jit(solution)/shard_map/ppermute | solution.py:52
  37.3 8.0 %collective-permute-start.15 = (bf16[128,256]{1,0:T(8,128)(2,1)S(1)}, bf16[128,256]{1,0:T(8,128)(2,1)S(1)}, u32[]{:S(2)}, u32[]{:S(2)}) collective-permute-start(bf16[128,256]{1,0:T(8,128)(2,1)S(1)} %get-tuple-element.41.refs_0_), channel_id=1, source_target_pairs={{0,64},{4,68},{8,72},{12,76},{16,80},{20,84},{24,88},{28,92},{32,9... | collective-permute-start | bytes 196616 | tf_op jit(solution)/shard_map/ppermute | solution.py:52
  40.9 7.6 %collective-permute-start.16 = (bf16[128,256]{1,0:T(8,128)(2,1)S(1)}, bf16[128,256]{1,0:T(8,128)(2,1)S(1)}, u32[]{:S(2)}, u32[]{:S(2)}) collective-permute-start(bf16[128,256]{1,0:T(8,128)(2,1)S(1)} %get-tuple-element.42.refs_1_), channel_id=1, source_target_pairs={{0,192},{4,196},{8,200},{12,204},{16,208},{20,212},{24,216},{28,22... | collective-permute-start | bytes 196616 | tf_op jit(solution)/shard_map/ppermute | solution.py:52
  48.5 7.1 %collective-permute-start.17 = (bf16[128,256]{1,0:T(8,128)(2,1)S(1)}, bf16[128,256]{1,0:T(8,128)(2,1)S(1)}, u32[]{:S(2)}, u32[]{:S(2)}) collective-permute-start(bf16[128,256]{1,0:T(8,128)(2,1)S(1)} %get-tuple-element.43.refs_0_), channel_id=1, source_target_pairs={{0,192},{4,196},{8,200},{12,204},{16,208},{20,212},{24,216},{28,22... | collective-permute-start | bytes 196616 | tf_op jit(solution)/shard_map/ppermute | solution.py:52
  58.9 7.7 %collective-permute-start.19 = (bf16[168,256]{1,0:T(8,128)(2,1)S(1)}, bf16[168,256]{1,0:T(8,128)(2,1)S(1)}, u32[]{:S(2)}, u32[]{:S(2)}) collective-permute-start(bf16[168,256]{1,0:T(8,128)(2,1)S(1)} %shard_map.51.s0), channel_id=1, source_target_pairs={{0,64},{4,68},{8,72},{12,76},{16,80},{20,84},{24,88},{28,92},{32,9... | collective-permute-start | bytes 258056 | tf_op jit(solution)/shard_map/ppermute | solution.py:52
  60.2 9.4 %collective-permute-start.20 = (bf16[168,256]{1,0:T(8,128)(2,1)S(1)}, bf16[168,256]{1,0:T(8,128)(2,1)S(1)}, u32[]{:S(2)}, u32[]{:S(2)}) collective-permute-start(bf16[168,256]{1,0:T(8,128)(2,1)S(1)} %shard_map.51.s0), channel_id=1, source_target_pairs={{0,128},{4,132},{8,136},{12,140},{16,144},{20,148},{24,152},{28,15... | collective-permute-start | bytes 258056 | tf_op jit(solution)/shard_map/ppermute | solution.py:52
  62.5 9.2 %collective-permute-start.21 = (bf16[168,256]{1,0:T(8,128)(2,1)S(1)}, bf16[168,256]{1,0:T(8,128)(2,1)S(1)}, u32[]{:S(2)}, u32[]{:S(2)}) collective-permute-start(bf16[168,256]{1,0:T(8,128)(2,1)S(1)} %shard_map.51.s0), channel_id=1, source_target_pairs={{0,192},{4,196},{8,200},{12,204},{16,208},{20,212},{24,216},{28,22... | collective-permute-start | bytes 258056 | tf_op jit(solution)/shard_map/ppermute | solution.py:52
  71.8 5.9 %collective-permute-start.22 = (f32[1,128]{1,0:T(1,128)S(1)}, f32[1,128]{1,0:T(1,128)S(1)}, u32[]{:S(2)}, u32[]{:S(2)}) collective-permute-start(f32[1,128]{1,0:T(1,128)S(1)} %get-tuple-element.46.p0), channel_id=1, source_target_pairs={{0,1},{1,2},{2,3},{3,0},{4,5},{5,6},{6,7},{7,4},{8,9},{9,10},{10,1... | collective-permute-start | bytes 1544 | tf_op jit(solution)/shard_map/ppermute | solution.py:314
  80.1 5.9 %collective-permute-start.26 = (bf16[176,256]{1,0:T(8,128)(2,1)S(1)}, bf16[176,256]{1,0:T(8,128)(2,1)S(1)}, u32[]{:S(2)}, u32[]{:S(2)}) collective-permute-start(bf16[176,256]{1,0:T(8,128)(2,1)S(1)} %shard_map.53.refs_3_), channel_id=1, source_target_pairs={{0,8},{4,12},{8,16},{12,20},{16,24},{20,28},{24,0},{28,4},{32,40},... | collective-permute-start | bytes 270344 | tf_op jit(solution)/shard_map/ppermute | solution.py:52
  81.2 6.7 %collective-permute-start.27 = (bf16[176,256]{1,0:T(8,128)(2,1)S(1)}, bf16[176,256]{1,0:T(8,128)(2,1)S(1)}, u32[]{:S(2)}, u32[]{:S(2)}) collective-permute-start(bf16[176,256]{1,0:T(8,128)(2,1)S(1)} %shard_map.53.refs_3_), channel_id=1, source_target_pairs={{0,24},{4,28},{8,0},{12,4},{16,8},{20,12},{24,16},{28,20},{32,56},... | collective-permute-start | bytes 270344 | tf_op jit(solution)/shard_map/ppermute | solution.py:52
  82.2 7.0 %collective-permute-start.28 = (bf16[176,256]{1,0:T(8,128)(2,1)S(1)}, bf16[176,256]{1,0:T(8,128)(2,1)S(1)}, u32[]{:S(2)}, u32[]{:S(2)}) collective-permute-start(bf16[176,256]{1,0:T(8,128)(2,1)S(1)} %shard_map.53.refs_3_), channel_id=1, source_target_pairs={{0,16},{4,20},{8,24},{12,28},{16,0},{20,4},{24,8},{28,12},{32,48},... | collective-permute-start | bytes 270344 | tf_op jit(solution)/shard_map/ppermute | solution.py:52
  87.9 6.0 %collective-permute-start.31 = (bf16[176,256]{1,0:T(8,128)(2,1)S(1)}, bf16[176,256]{1,0:T(8,128)(2,1)S(1)}, u32[]{:S(2)}, u32[]{:S(2)}) collective-permute-start(bf16[176,256]{1,0:T(8,128)(2,1)S(1)} %collective-permute-done.25.refs_4_), channel_id=1, source_target_pairs={{0,16},{4,20},{8,24},{12,28},{16,0},{20,4},{24,8},{28,12},{32,48},... | collective-permute-start | bytes 270344 | tf_op jit(solution)/shard_map/ppermute | solution.py:52
  89.2 5.3 %collective-permute-start.34 = (bf16[176,256]{1,0:T(8,128)(2,1)S(1)}, bf16[176,256]{1,0:T(8,128)(2,1)S(1)}, u32[]{:S(2)}, u32[]{:S(2)}) collective-permute-start(bf16[176,256]{1,0:T(8,128)(2,1)S(1)} %collective-permute-done.26.refs_5_), channel_id=1, source_target_pairs={{0,4},{4,0},{8,12},{12,8},{16,20},{20,16},{24,28},{28,24},{32,36},... | collective-permute-start | bytes 270344 | tf_op jit(solution)/shard_map/ppermute | solution.py:52
  (16 other events, 61.1 us)

commit v7 on v6

--- a/solution.py
+++ b/solution.py
@@ -9,7 +9,6 @@
 Z, X, C = 8, 4, 2
 CLUSTERS = Z * X * C
 ROWS = 176
-EARLY = 4
 ROOM = 16 * 1024 * 1024
 BF, F32 = jnp.bfloat16, jnp.float32
 
@@ -62,7 +61,7 @@
 
 
 def pack_kernel(x_ref, pair_ref, c_ref, *refs):
-    far, outs, near, sems = refs[:4], refs[4:12], refs[12:16], refs[16]
+    far, invs, sigs, near, sems = refs[:4], refs[4:12], refs[12:20], refs[20:24], refs[24]
     loads = [pltpu.make_async_copy(a, b, sems.at[k]) for k, (a, b) in enumerate(zip(far, near))]
     for load in loads:
         load.start()
@@ -76,19 +75,19 @@
     scales = dot(inside, jnp.exp2(expo.astype(F32)).astype(BF))
     lane = lax.broadcasted_iota(jnp.int32, (168, 16), 1)
     places = [
-        (out, k, side * 8 + lax.rem(x + dx, X) * 2 + (1 - pair if dp else pair))
-        for out, (dx, dp) in zip(outs, SLOTS)
+        (slot, k, side * 8 + lax.rem(x + dx, X) * 2 + (1 - pair if dp else pair))
+        for slot, (dx, dp) in enumerate(SLOTS)
         for k, side in enumerate((c, 1 - c))
     ]
     loads[1].wait()
+    for slot, k, r in places:
+        invs[slot][k] = inv_ref[r]
     loads[2].wait()
-    for out, k, r in places:
-        out[k, 0:256, :] = inv_ref[r]
-        out[k, 256:384, :] = chan_ref[r]
     loads[3].wait()
-    for out, k, r in places:
+    for slot, k, r in places:
+        sigs[slot][k, 0:128, :] = chan_ref[r]
         scale = jnp.sum(jnp.where(lane == r, scales, 0.0), axis=1, keepdims=True)
-        out[k, 384:552, :] = (mant_ref[r].astype(F32) * scale).astype(BF)
+        sigs[slot][k, 128:296, :] = (mant_ref[r].astype(F32) * scale).astype(BF)
 
 
 def near(shape, dtype):
@@ -116,61 +115,66 @@
 def packed(*ins):
     cost = pl.CostEstimate(flops=6000000, bytes_accessed=5000000, transcendentals=0)
     scratch = [pltpu.VMEM(value.shape, value.dtype) for value in ins[3:]] + [pltpu.SemaphoreType.DMA((4,))]
-    return whole(pack_kernel, ins, [near((2, 552, 128), BF)] * 8, scratch, cost, pltpu.HBM)
-
-
-def square_of(raw):
-    return complex_square(raw[0:128, :].T, raw[128:256, :].T)
-
-
-def add_means(raws, av):
-    for raw in raws:
-        top, square = square_of(raw)
-        av[0:128, :] += top.astype(F32)
-        av[128:256, :] += dot(top, square)
-
-
-def add_estimates(raws, p, d, t, av=None):
+    outs = [near((2, 256, 128), BF)] * 8 + [near((2, 296, 128), BF)] * 8
+    outs = whole(pack_kernel, ins, outs, scratch, cost, pltpu.HBM)
+    return outs[:8], outs[8:]
+
+
+def square_of(inv):
+    return complex_square(inv[0:128, :].T, inv[128:256, :].T)
+
+
+def add_estimates(invs, sigs, p, d, t):
     sums = None
-    for raw in raws:
-        top, square = square_of(raw)
-        cr, ci = raw[256:320, :], raw[320:384, :]
+    for inv, sig in zip(invs, sigs):
+        _, square = square_of(inv)
+        cr, ci = sig[0:64, :], sig[64:128, :]
         match = jnp.concatenate(
             [jnp.concatenate([cr, -ci], axis=1), jnp.concatenate([ci, cr], axis=1)], axis=0
         )
-        m = dot(raw[384:552, :], match).astype(BF)
+        m = dot(sig[128:296, :], match).astype(BF)
         t1 = dot(m, square)
         t2 = dot(t1.astype(BF), square)
         t3 = dot(t2.astype(BF), square)
-        new = (t1, t2, t3) + ((top.astype(F32), dot(top, square)) if av is not None else ())
+        new = (t1, t2, t3)
         sums = new if sums is None else tuple(u + v for u, v in zip(sums, new))
-    t1, t2, t3 = sums[:3]
-    p[0:168, :] += t1
-    d[0:168, :] += t2 - 2.0 * t1
-    t[0:168, :] += 3.0 * t1 - 1.5 * t2 + 0.25 * t3
-    if av is not None:
-        av[0:128, :] += sums[3]
-        av[128:256, :] += sums[4]
-
-
-def early_kernel(*refs):
-    raws, (p, d, t, av), held = refs[: 2 * EARLY], refs[2 * EARLY : -1], refs[-1]
-    for k, raw in enumerate(raws):
-        held[k] = raw[k % 2]
-    for ref in (p, d, t, av):
-        ref[...] = jnp.zeros_like(ref)
+    t1, t2, t3 = sums
+    p[...] += t1
+    d[...] += t2 - 2.0 * t1
+    t[...] += 3.0 * t1 - 1.5 * t2 + 0.25 * t3
+
+
+def estimate_kernel(before, *refs):
+    invs, sigs, old, rest = refs[:8], refs[8:16], refs[16 : 16 + before], refs[16 + before :]
+    p, d, t, held_inv, held_sig = rest
+    for k in range(8):
+        held_inv[k] = invs[k][k % 2]
+        held_sig[k] = sigs[k][k % 2]
+    for k, ref in enumerate((p, d, t)):
+        ref[...] = old[k][...] if before else jnp.zeros_like(ref)
 
     def two(k, carry):
-        add_estimates((held[2 * k], held[2 * k + 1]), p, d, t, av)
+        k = 2 * k
+        add_estimates((held_inv[k], held_inv[k + 1]), (held_sig[k], held_sig[k + 1]), p, d, t)
         return carry
 
-    lax.fori_loop(0, EARLY, two, 0)
+    lax.fori_loop(0, 4, two, 0)
 
 
 def mean_kernel(*refs):
-    raws, before, first_ref, second_ref, av = refs[:-4], *refs[-4:]
-    av[...] = before[...]
-    add_means([raw[k % 2, 0:256, :] for k, raw in enumerate(raws)], av)
+    invs, first_ref, second_ref, av, held = refs[:-4], *refs[-4:]
+    av[...] = jnp.zeros_like(av)
+    for k, inv in enumerate(invs):
+        held[k] = inv[k % 2]
+
+    def four(k, carry):
+        for j in range(4):
+            top, square = square_of(held[4 * k + j])
+            av[0:128, :] += top.astype(F32)
+            av[128:256, :] += dot(top, square)
+        return carry
+
+    lax.fori_loop(0, 4, four, 0)
     ones = (
         lax.broadcasted_iota(jnp.int32, (128, 256), 0) == lax.broadcasted_iota(jnp.int32, (128, 256), 1)
     ).astype(F32) * 16.0
@@ -185,32 +189,24 @@
         out[...] = (a[...].astype(F32) + b[...].astype(F32)).astype(out.dtype)
 
 
-def late_kernel(*refs):
-    n = 2 * (8 - EARLY)
-    raws, before, sums = refs[:n], refs[n : n + 3], refs[n + 3 :]
-    for ref, old in zip(sums, before):
-        ref[...] = old[...]
-    for k in range(0, n, 2):
-        add_estimates((raws[k][0], raws[k + 1][1]), *sums)
-
-
 SUM = (168, 256)
-SUMS = (SUM, SUM, SUM, (256, 256))
 COST = pl.CostEstimate(flops=2000000000, bytes_accessed=3000000, transcendentals=0)
 
 
-def early_sums(raws):
-    scratch = [pltpu.VMEM((2 * EARLY, 552, 128), BF)]
-    return whole(early_kernel, raws, [near(shape, F32) for shape in SUMS], scratch, COST)
-
-
-def mean_sums(raws, before):
-    scratch = [pltpu.VMEM((256, 256), F32)]
-    return whole(mean_kernel, [*raws, before], [near((128, 256), BF)] * 2, scratch, COST)
-
-
-def late_sums(raws, before):
-    return whole(late_kernel, [*raws, *before], [near(SUM, F32)] * 3, cost=COST)
+def estimates(invs, sigs, before=()):
+    scratch = [pltpu.VMEM((8, 256, 128), BF), pltpu.VMEM((8, 296, 128), BF)]
+    return whole(
+        lambda *refs: estimate_kernel(len(before), *refs),
+        [*invs, *sigs, *before],
+        [near(SUM, F32)] * 3,
+        scratch,
+        COST,
+    )
+
+
+def mean_sums(invs):
+    scratch = [pltpu.VMEM((256, 256), F32), pltpu.VMEM((16, 256, 128), BF)]
+    return whole(mean_kernel, invs, [near((128, 256), BF)] * 2, scratch, COST)
 
 
 def dot_wide(a, b):
@@ -288,22 +284,25 @@
     sent = packed(
         *here, expo, inverses[0].reshape(blocks, 256, 128), channel[0].reshape(blocks, 128, 128), mant
     )
-    raws = [sent[0]]
-    for k in range(1, 8):
-        raws.append(moved(sent[k], pair_shifted(*SLOTS[k])))
-    swapped = []
-    for k in range(8):
-        swapped.append(moved(raws[k], shifted(dc=1)))
-    slots = [part for pair in zip(raws, swapped) for part in pair]
-    before = early_sums(slots[: 2 * EARLY])
-    means = mean_sums(slots[2 * EARLY :], before[3])
+
+    def regrouped(parts):
+        raws, slots = [parts[0]], []
+        for k in range(1, 8):
+            raws.append(moved(parts[k], pair_shifted(*SLOTS[k])))
+        for k in range(8):
+            slots += [raws[k], moved(raws[k], shifted(dc=1))]
+        return slots
+
+    invs, sigs = regrouped(sent[0]), regrouped(sent[1])
+    means = mean_sums(invs)
     first = moved(means[0], on_z_ring(0))
     second = moved(means[1], on_z_ring(1))
+    sums = estimates(invs[:8], sigs[:8])
     means = whole(pair_kernel, (*means, first, second), [near((128, 256), BF)] * 2)
     first = moved(means[0], on_z_ring(1))
     second = moved(means[1], on_z_ring(0))
     means = (means[0], first, means[1], second)
-    sums = late_sums(slots[2 * EARLY :], before[:3])
+    sums = estimates(invs[8:], sigs[8:], sums)
     share = whole(share_kernel, (*sums, *means), near(SUM, BF))
     shares = [share, share, share, share]
     for d in (2, 1, 3):

time: 98.8 us -> 107 us (1.083)
  the two profiles are of different devices: /device:TPU:2 before, /device:TPU:1 now
where the time goes in v7:
time: 107 us
  starting transfers between devices  79.4 us (74%)
  waiting for transfers between devices  15.7 us (15%)
  Pallas kernels  11.4 us (11%)
    ppermute x52, starting transfers between devices, moved(): return lax.ppermute(value, 'cluster', pairs)  74.4 us
    ppermute x52, waiting for transfers between devices, moved(): return lax.ppermute(value, 'cluster', pairs)  14.4 us
    pallas_call x9, Pallas kernels, whole(): pl.pallas_call(kernel, in_specs=[pl.BlockSpec(memory_space=pltpu.SMEM if...  11.4 us
    ppermute x3, starting transfers between devices, per_device(): powers[d] = lax.ppermute(power, 'sub', [(y, (y + d) % 4) for y in range(4)])  5.05 us
  transfers between devices with their start and end apart: 55, of which 16 were waited for; matrix products, arithmetic and copies ran while one was open for 0% of the time, Pallas kernels for 7%

profile of v7, /device:TPU:1, one launch (start us, length us, event | category | flops | bytes accessed | tf_op | source)
XLA Modules:
  0.0 106.8 jit_solution(12305501884148035120)
XLA Ops:
  0.0 2.3 %shard_map.46 = (bf16[2,256,128]{2,1,0:T(8,128)(2,1)S(1)}, bf16[2,256,128]{2,1,0:T(8,128)(2,1)S(1)}, bf16[2,256,128]{2,1,0:T(8,128)(2,1)S(1)}, bf16[2,256,128]{2...) custom-call(s32[1]{0:T(128)} %bitcast.x_ref.refs_0_, ...), custom_call_target="tpu_custom_call" | custom-call | flops 6000000 | bytes 5000000 | tf_op jit(solution)/shard_map/pallas_call | solution.py:104
  2.3 3.6 %collective-permute-start = (bf16[2,256,128]{2,1,0:T(8,128)(2,1)S(1)}, bf16[2,256,128]{2,1,0:T(8,128)(2,1)S(1)}, u32[]{:S(2)}, u32[]{:S(2)}) collective-permute-start(bf16[2,256,128]{2,1,0:T(8,128)(2,1)S(1)} %get-tuple-element.33), channel_id=1, source_target_pairs={{0,16},{4,20},{8,24},{12,28},{16,0},{20,4},{24,8},{28,12},{32,48},... | collective-permute-start | bytes 393224 | tf_op jit(solution)/shard_map/ppermute | solution.py:51
  6.3 2.4 %collective-permute-start.19 = (bf16[2,256,128]{2,1,0:T(8,128)(2,1)S(1)}, bf16[2,256,128]{2,1,0:T(8,128)(2,1)S(1)}, u32[]{:S(2)}, u32[]{:S(2)}) collective-permute-start(bf16[2,256,128]{2,1,0:T(8,128)(2,1)S(1)} %get-tuple-element.43), channel_id=1, source_target_pairs={{0,24},{4,28},{8,0},{12,4},{16,8},{20,12},{24,16},{28,20},{32,56},... | collective-permute-start | bytes 393224 | tf_op jit(solution)/shard_map/ppermute | solution.py:51
  10.3 3.6 %collective-permute-start.4 = (bf16[2,256,128]{2,1,0:T(8,128)(2,1)S(1)}, bf16[2,256,128]{2,1,0:T(8,128)(2,1)S(1)}, u32[]{:S(2)}, u32[]{:S(2)}) collective-permute-start(bf16[2,256,128]{2,1,0:T(8,128)(2,1)S(1)} %get-tuple-element.35), channel_id=1, source_target_pairs={{0,56},{4,60},{8,32},{12,36},{16,40},{20,44},{24,48},{28,52},{32,2... | collective-permute-start | bytes 393224 | tf_op jit(solution)/shard_map/ppermute | solution.py:51
  13.9 2.6 %collective-permute-start.6 = (bf16[2,256,128]{2,1,0:T(8,128)(2,1)S(1)}, bf16[2,256,128]{2,1,0:T(8,128)(2,1)S(1)}, u32[]{:S(2)}, u32[]{:S(2)}) collective-permute-start(bf16[2,256,128]{2,1,0:T(8,128)(2,1)S(1)} %get-tuple-element.36), channel_id=1, source_target_pairs={{0,48},{4,52},{8,56},{12,60},{16,32},{20,36},{24,40},{28,44},{32,1... | collective-permute-start | bytes 393224 | tf_op jit(solution)/shard_map/ppermute | solution.py:51
  16.5 1.9 %collective-permute-start.16 = (bf16[2,256,128]{2,1,0:T(8,128)(2,1)S(1)}, bf16[2,256,128]{2,1,0:T(8,128)(2,1)S(1)}, u32[]{:S(2)}, u32[]{:S(2)}) collective-permute-start(bf16[2,256,128]{2,1,0:T(8,128)(2,1)S(1)} %get-tuple-element.41.refs_0_), channel_id=1, source_target_pairs={{0,4},{4,0},{8,12},{12,8},{16,20},{20,16},{24,28},{28,24},{32,36},... | collective-permute-start | bytes 393224 | tf_op jit(solution)/shard_map/ppermute | solution.py:51
  18.4 2.3 %collective-permute-start.26 = (bf16[2,296,128]{2,1,0:T(8,128)(2,1)S(1)}, bf16[2,296,128]{2,1,0:T(8,128)(2,1)S(1)}, u32[]{:S(2)}, u32[]{:S(2)}) collective-permute-start(bf16[2,296,128]{2,1,0:T(8,128)(2,1)S(1)} %get-tuple-element.47), channel_id=1, source_target_pairs={{0,24},{4,28},{8,0},{12,4},{16,8},{20,12},{24,16},{28,20},{32,56},... | collective-permute-start | bytes 454664 | tf_op jit(solution)/shard_map/ppermute | solution.py:51
  21.6 2.3 %collective-permute-start.23 = (bf16[2,296,128]{2,1,0:T(8,128)(2,1)S(1)}, bf16[2,296,128]{2,1,0:T(8,128)(2,1)S(1)}, u32[]{:S(2)}, u32[]{:S(2)}) collective-permute-start(bf16[2,296,128]{2,1,0:T(8,128)(2,1)S(1)} %get-tuple-element.45.refs_8_), channel_id=1, source_target_pairs={{0,4},{4,0},{8,12},{12,8},{16,20},{20,16},{24,28},{28,24},{32,36},... | collective-permute-start | bytes 454664 | tf_op jit(solution)/shard_map/ppermute | solution.py:51
  23.9 2.3 %collective-permute-start.10 = (bf16[2,296,128]{2,1,0:T(8,128)(2,1)S(1)}, bf16[2,296,128]{2,1,0:T(8,128)(2,1)S(1)}, u32[]{:S(2)}, u32[]{:S(2)}) collective-permute-start(bf16[2,296,128]{2,1,0:T(8,128)(2,1)S(1)} %get-tuple-element.38), channel_id=1, source_target_pairs={{0,40},{4,44},{8,48},{12,52},{16,56},{20,60},{24,32},{28,36},{32,8... | collective-permute-start | bytes 454664 | tf_op jit(solution)/shard_map/ppermute | solution.py:51
  28.6 3.4 %collective-permute-done.10.refs_10_ = bf16[2,296,128]{2,1,0:T(8,128)(2,1)S(1)} collective-permute-done((bf16[2,296,128]{2,1,0:T(8,128)(2,1)S(1)}, bf16[2,296,128]{2,1,0:T(8,128)(2,1)S(1)}, u32[]{:S(2)}, u32[]{:S(2)}) %collective-permute-start.10) | collective-permute-done | bytes 151584 | tf_op jit(solution)/shard_map/ppermute | solution.py:51
  35.1 4.2 %collective-permute-start.14 = (bf16[2,296,128]{2,1,0:T(8,128)(2,1)S(1)}, bf16[2,296,128]{2,1,0:T(8,128)(2,1)S(1)}, u32[]{:S(2)}, u32[]{:S(2)}) collective-permute-start(bf16[2,296,128]{2,1,0:T(8,128)(2,1)S(1)} %get-tuple-element.40), channel_id=1, source_target_pairs={{0,48},{4,52},{8,56},{12,60},{16,32},{20,36},{24,40},{28,44},{32,1... | collective-permute-start | bytes 454664 | tf_op jit(solution)/shard_map/ppermute | solution.py:51
  43.5 3.0 %collective-permute-start.30 = (bf16[128,256]{1,0:T(8,128)(2,1)S(1)}, bf16[128,256]{1,0:T(8,128)(2,1)S(1)}, u32[]{:S(2)}, u32[]{:S(2)}) collective-permute-start(bf16[128,256]{1,0:T(8,128)(2,1)S(1)} %get-tuple-element.55.refs_0_), channel_id=1, source_target_pairs={{0,64},{4,68},{8,72},{12,76},{16,80},{20,84},{24,88},{28,92},{32,9... | collective-permute-start | bytes 196616 | tf_op jit(solution)/shard_map/ppermute | solution.py:51
  48.2 5.6 %collective-permute-start.31 = (bf16[128,256]{1,0:T(8,128)(2,1)S(1)}, bf16[128,256]{1,0:T(8,128)(2,1)S(1)}, u32[]{:S(2)}, u32[]{:S(2)}) collective-permute-start(bf16[128,256]{1,0:T(8,128)(2,1)S(1)} %get-tuple-element.56.refs_1_), channel_id=1, source_target_pairs={{0,192},{4,196},{8,200},{12,204},{16,208},{20,212},{24,216},{28,22... | collective-permute-start | bytes 196616 | tf_op jit(solution)/shard_map/ppermute | solution.py:51
  53.8 3.0 %shard_map.47 = (f32[168,256]{1,0:T(8,128)S(1)}, f32[168,256]{1,0:T(8,128)S(1)}, f32[168,256]{1,0:T(8,128)S(1)}) custom-call(bf16[2,256,128]{2,1,0:T(8,128)(2,1)S(1)} %get-tuple-element.41.refs_0_, bf16[2,256,128]{2,1,0:T(8,128)(2,1)S(1)} %collective-permute-done.16.refs_1_, bf16[2,256,128]{2,1,0:T(8,128)(2,1)S(1)} %collective-permute-done.17.refs_2_, ...), custom_call_target="tpu_custom_call" | custom-call | flops 2000000000 | bytes 3000000 | tf_op jit(solution)/shard_map/pallas_call | solution.py:104
  56.8 3.0 %collective-permute-start.32 = (bf16[128,256]{1,0:T(8,128)(2,1)S(1)}, bf16[128,256]{1,0:T(8,128)(2,1)S(1)}, u32[]{:S(2)}, u32[]{:S(2)}) collective-permute-start(bf16[128,256]{1,0:T(8,128)(2,1)S(1)} %get-tuple-element.57.refs_0_), channel_id=1, source_target_pairs={{0,192},{4,196},{8,200},{12,204},{16,208},{20,212},{24,216},{28,22... | collective-permute-start | bytes 196616 | tf_op jit(solution)/shard_map/ppermute | solution.py:51
  60.4 3.0 %shard_map.48 = (f32[168,256]{1,0:T(8,128)S(1)}, f32[168,256]{1,0:T(8,128)S(1)}, f32[168,256]{1,0:T(8,128)S(1)}) custom-call(bf16[2,256,128]{2,1,0:T(8,128)(2,1)S(1)} %collective-permute-done.refs_0_.refs_8_, bf16[2,256,128]{2,1,0:T(8,128)(2,1)S(1)} %collective-permute-done.1.refs_1_.refs_9_, ...), custom_call_target="tpu_custom_call" | custom-call | flops 2000000000 | bytes 3000000 | tf_op jit(solution)/shard_map/pallas_call | solution.py:104
  65.7 2.5 %collective-permute-start.35 = (bf16[168,256]{1,0:T(8,128)(2,1)S(1)}, bf16[168,256]{1,0:T(8,128)(2,1)S(1)}, u32[]{:S(2)}, u32[]{:S(2)}) collective-permute-start(bf16[168,256]{1,0:T(8,128)(2,1)S(1)} %shard_map.51.s0), channel_id=1, source_target_pairs={{0,128},{4,132},{8,136},{12,140},{16,144},{20,148},{24,152},{28,15... | collective-permute-start | bytes 258056 | tf_op jit(solution)/shard_map/ppermute | solution.py:51
  68.2 2.1 %collective-permute-start.36 = (bf16[168,256]{1,0:T(8,128)(2,1)S(1)}, bf16[168,256]{1,0:T(8,128)(2,1)S(1)}, u32[]{:S(2)}, u32[]{:S(2)}) collective-permute-start(bf16[168,256]{1,0:T(8,128)(2,1)S(1)} %shard_map.51.s0), channel_id=1, source_target_pairs={{0,192},{4,196},{8,200},{12,204},{16,208},{20,212},{24,216},{28,22... | collective-permute-start | bytes 258056 | tf_op jit(solution)/shard_map/ppermute | solution.py:51
  70.6 4.0 %collective-permute-done.35.s2 = bf16[168,256]{1,0:T(8,128)(2,1)S(1)} collective-permute-done((bf16[168,256]{1,0:T(8,128)(2,1)S(1)}, bf16[168,256]{1,0:T(8,128)(2,1)S(1)}, u32[]{:S(2)}, u32[]{:S(2)}) %collective-permute-start.35) | collective-permute-done | bytes 86048 | tf_op jit(solution)/shard_map/ppermute | solution.py:51
  77.1 2.6 %collective-permute-start.38 = (f32[1,128]{1,0:T(1,128)S(1)}, f32[1,128]{1,0:T(1,128)S(1)}, u32[]{:S(2)}, u32[]{:S(2)}) collective-permute-start(f32[1,128]{1,0:T(1,128)S(1)} %get-tuple-element.60.p0), channel_id=1, source_target_pairs={{0,2},{1,3},{2,0},{3,1},{4,6},{5,7},{6,4},{7,5},{8,10},{9,11},{10,... | collective-permute-start | bytes 1544 | tf_op jit(solution)/shard_map/ppermute | solution.py:313
  82.3 1.8 %collective-permute-start.41 = (bf16[176,256]{1,0:T(8,128)(2,1)S(1)}, bf16[176,256]{1,0:T(8,128)(2,1)S(1)}, u32[]{:S(2)}, u32[]{:S(2)}) collective-permute-start(bf16[176,256]{1,0:T(8,128)(2,1)S(1)} %shard_map.53.refs_3_), channel_id=1, source_target_pairs={{0,8},{4,12},{8,16},{12,20},{16,24},{20,28},{24,0},{28,4},{32,40},... | collective-permute-start | bytes 270344 | tf_op jit(solution)/shard_map/ppermute | solution.py:51
  86.0 8.7 %collective-permute-start.47 = (bf16[176,256]{1,0:T(8,128)(2,1)S(1)}, bf16[176,256]{1,0:T(8,128)(2,1)S(1)}, u32[]{:S(2)}, u32[]{:S(2)}) collective-permute-start(bf16[176,256]{1,0:T(8,128)(2,1)S(1)} %shard_map.53.refs_3_), channel_id=1, source_target_pairs={{0,4},{4,0},{8,12},{12,8},{16,20},{20,16},{24,28},{28,24},{32,36},... | collective-permute-start | bytes 270344 | tf_op jit(solution)/shard_map/ppermute | solution.py:51
  94.7 2.7 %collective-permute-start.45 = (bf16[176,256]{1,0:T(8,128)(2,1)S(1)}, bf16[176,256]{1,0:T(8,128)(2,1)S(1)}, u32[]{:S(2)}, u32[]{:S(2)}) collective-permute-start(bf16[176,256]{1,0:T(8,128)(2,1)S(1)} %collective-permute-done.40.refs_4_), channel_id=1, source_target_pairs={{0,24},{4,28},{8,0},{12,4},{16,8},{20,12},{24,16},{28,20},{32,56},... | collective-permute-start | bytes 270344 | tf_op jit(solution)/shard_map/ppermute | solution.py:51
  102.2 1.7 %collective-permute-start.52 = (bf16[176,256]{1,0:T(8,128)(2,1)S(1)}, bf16[176,256]{1,0:T(8,128)(2,1)S(1)}, u32[]{:S(2)}, u32[]{:S(2)}) collective-permute-start(bf16[176,256]{1,0:T(8,128)(2,1)S(1)} %collective-permute-done.44.refs_8_), channel_id=1, source_target_pairs={{0,4},{4,0},{8,12},{12,8},{16,20},{20,16},{24,28},{28,24},{32,36},... | collective-permute-start | bytes 270344 | tf_op jit(solution)/shard_map/ppermute | solution.py:51
  (95 shorter events, 32.0 us)
Async XLA Ops:
  2.3 8.0 %collective-permute-start = (bf16[2,256,128]{2,1,0:T(8,128)(2,1)S(1)}, bf16[2,256,128]{2,1,0:T(8,128)(2,1)S(1)}, u32[]{:S(2)}, u32[]{:S(2)}) collective-permute-start(bf16[2,256,128]{2,1,0:T(8,128)(2,1)S(1)} %get-tuple-element.33), channel_id=1, source_target_pairs={{0,16},{4,20},{8,24},{12,28},{16,0},{20,4},{24,8},{28,12},{32,48},... | collective-permute-start | bytes 393224 | tf_op jit(solution)/shard_map/ppermute | solution.py:51
  5.9 7.9 %collective-permute-start.17 = (bf16[2,256,128]{2,1,0:T(8,128)(2,1)S(1)}, bf16[2,256,128]{2,1,0:T(8,128)(2,1)S(1)}, u32[]{:S(2)}, u32[]{:S(2)}) collective-permute-start(bf16[2,256,128]{2,1,0:T(8,128)(2,1)S(1)} %get-tuple-element.42), channel_id=1, source_target_pairs={{0,8},{4,12},{8,16},{12,20},{16,24},{20,28},{24,0},{28,4},{32,40},... | collective-permute-start | bytes 393224 | tf_op jit(solution)/shard_map/ppermute | solution.py:51
  6.3 7.6 %collective-permute-start.19 = (bf16[2,256,128]{2,1,0:T(8,128)(2,1)S(1)}, bf16[2,256,128]{2,1,0:T(8,128)(2,1)S(1)}, u32[]{:S(2)}, u32[]{:S(2)}) collective-permute-start(bf16[2,256,128]{2,1,0:T(8,128)(2,1)S(1)} %get-tuple-element.43), channel_id=1, source_target_pairs={{0,24},{4,28},{8,0},{12,4},{16,8},{20,12},{24,16},{28,20},{32,56},... | collective-permute-start | bytes 393224 | tf_op jit(solution)/shard_map/ppermute | solution.py:51
  8.6 7.8 %collective-permute-start.21 = (bf16[2,256,128]{2,1,0:T(8,128)(2,1)S(1)}, bf16[2,256,128]{2,1,0:T(8,128)(2,1)S(1)}, u32[]{:S(2)}, u32[]{:S(2)}) collective-permute-start(bf16[2,256,128]{2,1,0:T(8,128)(2,1)S(1)} %get-tuple-element.44), channel_id=1, source_target_pairs={{0,32},{4,36},{8,40},{12,44},{16,48},{20,52},{24,56},{28,60},{32,0... | collective-permute-start | bytes 393224 | tf_op jit(solution)/shard_map/ppermute | solution.py:51
  10.3 8.1 %collective-permute-start.2 = (bf16[2,256,128]{2,1,0:T(8,128)(2,1)S(1)}, bf16[2,256,128]{2,1,0:T(8,128)(2,1)S(1)}, u32[]{:S(2)}, u32[]{:S(2)}) collective-permute-start(bf16[2,256,128]{2,1,0:T(8,128)(2,1)S(1)} %get-tuple-element.34), channel_id=1, source_target_pairs={{0,40},{4,44},{8,48},{12,52},{16,56},{20,60},{24,32},{28,36},{32,8... | collective-permute-start | bytes 393224 | tf_op jit(solution)/shard_map/ppermute | solution.py:51
  10.3 10.4 %collective-permute-start.4 = (bf16[2,256,128]{2,1,0:T(8,128)(2,1)S(1)}, bf16[2,256,128]{2,1,0:T(8,128)(2,1)S(1)}, u32[]{:S(2)}, u32[]{:S(2)}) collective-permute-start(bf16[2,256,128]{2,1,0:T(8,128)(2,1)S(1)} %get-tuple-element.35), channel_id=1, source_target_pairs={{0,56},{4,60},{8,32},{12,36},{16,40},{20,44},{24,48},{28,52},{32,2... | collective-permute-start | bytes 393224 | tf_op jit(solution)/shard_map/ppermute | solution.py:51
  13.8 12.3 %collective-permute-start.24 = (bf16[2,296,128]{2,1,0:T(8,128)(2,1)S(1)}, bf16[2,296,128]{2,1,0:T(8,128)(2,1)S(1)}, u32[]{:S(2)}, u32[]{:S(2)}) collective-permute-start(bf16[2,296,128]{2,1,0:T(8,128)(2,1)S(1)} %get-tuple-element.46), channel_id=1, source_target_pairs={{0,8},{4,12},{8,16},{12,20},{16,24},{20,28},{24,0},{28,4},{32,40},... | collective-permute-start | bytes 454664 | tf_op jit(solution)/shard_map/ppermute | solution.py:51
  13.9 7.7 %collective-permute-start.6 = (bf16[2,256,128]{2,1,0:T(8,128)(2,1)S(1)}, bf16[2,256,128]{2,1,0:T(8,128)(2,1)S(1)}, u32[]{:S(2)}, u32[]{:S(2)}) collective-permute-start(bf16[2,256,128]{2,1,0:T(8,128)(2,1)S(1)} %get-tuple-element.36), channel_id=1, source_target_pairs={{0,48},{4,52},{8,56},{12,60},{16,32},{20,36},{24,40},{28,44},{32,1... | collective-permute-start | bytes 393224 | tf_op jit(solution)/shard_map/ppermute | solution.py:51
  18.4 9.1 %collective-permute-start.26 = (bf16[2,296,128]{2,1,0:T(8,128)(2,1)S(1)}, bf16[2,296,128]{2,1,0:T(8,128)(2,1)S(1)}, u32[]{:S(2)}, u32[]{:S(2)}) collective-permute-start(bf16[2,296,128]{2,1,0:T(8,128)(2,1)S(1)} %get-tuple-element.47), channel_id=1, source_target_pairs={{0,24},{4,28},{8,0},{12,4},{16,8},{20,12},{24,16},{28,20},{32,56},... | collective-permute-start | bytes 454664 | tf_op jit(solution)/shard_map/ppermute | solution.py:51
  23.9 8.1 %collective-permute-start.10 = (bf16[2,296,128]{2,1,0:T(8,128)(2,1)S(1)}, bf16[2,296,128]{2,1,0:T(8,128)(2,1)S(1)}, u32[]{:S(2)}, u32[]{:S(2)}) collective-permute-start(bf16[2,296,128]{2,1,0:T(8,128)(2,1)S(1)} %get-tuple-element.38), channel_id=1, source_target_pairs={{0,40},{4,44},{8,48},{12,52},{16,56},{20,60},{24,32},{28,36},{32,8... | collective-permute-start | bytes 454664 | tf_op jit(solution)/shard_map/ppermute | solution.py:51
  26.2 7.5 %collective-permute-start.12 = (bf16[2,296,128]{2,1,0:T(8,128)(2,1)S(1)}, bf16[2,296,128]{2,1,0:T(8,128)(2,1)S(1)}, u32[]{:S(2)}, u32[]{:S(2)}) collective-permute-start(bf16[2,296,128]{2,1,0:T(8,128)(2,1)S(1)} %get-tuple-element.39), channel_id=1, source_target_pairs={{0,56},{4,60},{8,32},{12,36},{16,40},{20,44},{24,48},{28,52},{32,2... | collective-permute-start | bytes 454664 | tf_op jit(solution)/shard_map/ppermute | solution.py:51
  35.1 8.5 %collective-permute-start.14 = (bf16[2,296,128]{2,1,0:T(8,128)(2,1)S(1)}, bf16[2,296,128]{2,1,0:T(8,128)(2,1)S(1)}, u32[]{:S(2)}, u32[]{:S(2)}) collective-permute-start(bf16[2,296,128]{2,1,0:T(8,128)(2,1)S(1)} %get-tuple-element.40), channel_id=1, source_target_pairs={{0,48},{4,52},{8,56},{12,60},{16,32},{20,36},{24,40},{28,44},{32,1... | collective-permute-start | bytes 454664 | tf_op jit(solution)/shard_map/ppermute | solution.py:51
  46.5 13.3 %collective-permute-start.11 = (bf16[2,296,128]{2,1,0:T(8,128)(2,1)S(1)}, bf16[2,296,128]{2,1,0:T(8,128)(2,1)S(1)}, u32[]{:S(2)}, u32[]{:S(2)}) collective-permute-start(bf16[2,296,128]{2,1,0:T(8,128)(2,1)S(1)} %collective-permute-done.10.refs_10_), channel_id=1, source_target_pairs={{0,4},{4,0},{8,12},{12,8},{16,20},{20,16},{24,28},{28,24},{32,36},... | collective-permute-start | bytes 454664 | tf_op jit(solution)/shard_map/ppermute | solution.py:51
  47.5 12.9 %collective-permute-start.13 = (bf16[2,296,128]{2,1,0:T(8,128)(2,1)S(1)}, bf16[2,296,128]{2,1,0:T(8,128)(2,1)S(1)}, u32[]{:S(2)}, u32[]{:S(2)}) collective-permute-start(bf16[2,296,128]{2,1,0:T(8,128)(2,1)S(1)} %collective-permute-done.12.refs_12_), channel_id=1, source_target_pairs={{0,4},{4,0},{8,12},{12,8},{16,20},{20,16},{24,28},{28,24},{32,36},... | collective-permute-start | bytes 454664 | tf_op jit(solution)/shard_map/ppermute | solution.py:51
  47.6 12.8 %collective-permute-start.15 = (bf16[2,296,128]{2,1,0:T(8,128)(2,1)S(1)}, bf16[2,296,128]{2,1,0:T(8,128)(2,1)S(1)}, u32[]{:S(2)}, u32[]{:S(2)}) collective-permute-start(bf16[2,296,128]{2,1,0:T(8,128)(2,1)S(1)} %collective-permute-done.14.refs_14_), channel_id=1, source_target_pairs={{0,4},{4,0},{8,12},{12,8},{16,20},{20,16},{24,28},{28,24},{32,36},... | collective-permute-start | bytes 454664 | tf_op jit(solution)/shard_map/ppermute | solution.py:51
  48.0 12.4 %collective-permute-start.9 = (bf16[2,296,128]{2,1,0:T(8,128)(2,1)S(1)}, bf16[2,296,128]{2,1,0:T(8,128)(2,1)S(1)}, u32[]{:S(2)}, u32[]{:S(2)}) collective-permute-start(bf16[2,296,128]{2,1,0:T(8,128)(2,1)S(1)} %collective-permute-done.8.refs_8_), channel_id=1, source_target_pairs={{0,4},{4,0},{8,12},{12,8},{16,20},{20,16},{24,28},{28,24},{32,36},... | collective-permute-start | bytes 454664 | tf_op jit(solution)/shard_map/ppermute | solution.py:51
  48.2 8.6 %collective-permute-start.31 = (bf16[128,256]{1,0:T(8,128)(2,1)S(1)}, bf16[128,256]{1,0:T(8,128)(2,1)S(1)}, u32[]{:S(2)}, u32[]{:S(2)}) collective-permute-start(bf16[128,256]{1,0:T(8,128)(2,1)S(1)} %get-tuple-element.56.refs_1_), channel_id=1, source_target_pairs={{0,192},{4,196},{8,200},{12,204},{16,208},{20,212},{24,216},{28,22... | collective-permute-start | bytes 196616 | tf_op jit(solution)/shard_map/ppermute | solution.py:51
  65.7 8.9 %collective-permute-start.35 = (bf16[168,256]{1,0:T(8,128)(2,1)S(1)}, bf16[168,256]{1,0:T(8,128)(2,1)S(1)}, u32[]{:S(2)}, u32[]{:S(2)}) collective-permute-start(bf16[168,256]{1,0:T(8,128)(2,1)S(1)} %shard_map.51.s0), channel_id=1, source_target_pairs={{0,128},{4,132},{8,136},{12,140},{16,144},{20,148},{24,152},{28,15... | collective-permute-start | bytes 258056 | tf_op jit(solution)/shard_map/ppermute | solution.py:51
  68.2 7.5 %collective-permute-start.36 = (bf16[168,256]{1,0:T(8,128)(2,1)S(1)}, bf16[168,256]{1,0:T(8,128)(2,1)S(1)}, u32[]{:S(2)}, u32[]{:S(2)}) collective-permute-start(bf16[168,256]{1,0:T(8,128)(2,1)S(1)} %shard_map.51.s0), channel_id=1, source_target_pairs={{0,192},{4,196},{8,200},{12,204},{16,208},{20,212},{24,216},{28,22... | collective-permute-start | bytes 258056 | tf_op jit(solution)/shard_map/ppermute | solution.py:51
  82.2 12.5 %collective-permute-start.40 = (bf16[176,256]{1,0:T(8,128)(2,1)S(1)}, bf16[176,256]{1,0:T(8,128)(2,1)S(1)}, u32[]{:S(2)}, u32[]{:S(2)}) collective-permute-start(bf16[176,256]{1,0:T(8,128)(2,1)S(1)} %shard_map.53.refs_3_), channel_id=1, source_target_pairs={{0,32},{4,36},{8,40},{12,44},{16,48},{20,52},{24,56},{28,60},{32,0... | collective-permute-start | bytes 270344 | tf_op jit(solution)/shard_map/ppermute | solution.py:51
  82.3 12.4 %collective-permute-start.41 = (bf16[176,256]{1,0:T(8,128)(2,1)S(1)}, bf16[176,256]{1,0:T(8,128)(2,1)S(1)}, u32[]{:S(2)}, u32[]{:S(2)}) collective-permute-start(bf16[176,256]{1,0:T(8,128)(2,1)S(1)} %shard_map.53.refs_3_), channel_id=1, source_target_pairs={{0,8},{4,12},{8,16},{12,20},{16,24},{20,28},{24,0},{28,4},{32,40},... | collective-permute-start | bytes 270344 | tf_op jit(solution)/shard_map/ppermute | solution.py:51
  84.1 13.2 %collective-permute-start.42 = (bf16[176,256]{1,0:T(8,128)(2,1)S(1)}, bf16[176,256]{1,0:T(8,128)(2,1)S(1)}, u32[]{:S(2)}, u32[]{:S(2)}) collective-permute-start(bf16[176,256]{1,0:T(8,128)(2,1)S(1)} %shard_map.53.refs_3_), channel_id=1, source_target_pairs={{0,24},{4,28},{8,0},{12,4},{16,8},{20,12},{24,16},{28,20},{32,56},... | collective-permute-start | bytes 270344 | tf_op jit(solution)/shard_map/ppermute | solution.py:51
  85.0 13.1 %collective-permute-start.43 = (bf16[176,256]{1,0:T(8,128)(2,1)S(1)}, bf16[176,256]{1,0:T(8,128)(2,1)S(1)}, u32[]{:S(2)}, u32[]{:S(2)}) collective-permute-start(bf16[176,256]{1,0:T(8,128)(2,1)S(1)} %shard_map.53.refs_3_), channel_id=1, source_target_pairs={{0,16},{4,20},{8,24},{12,28},{16,0},{20,4},{24,8},{28,12},{32,48},... | collective-permute-start | bytes 270344 | tf_op jit(solution)/shard_map/ppermute | solution.py:51
  86.0 13.8 %collective-permute-start.47 = (bf16[176,256]{1,0:T(8,128)(2,1)S(1)}, bf16[176,256]{1,0:T(8,128)(2,1)S(1)}, u32[]{:S(2)}, u32[]{:S(2)}) collective-permute-start(bf16[176,256]{1,0:T(8,128)(2,1)S(1)} %shard_map.53.refs_3_), channel_id=1, source_target_pairs={{0,4},{4,0},{8,12},{12,8},{16,20},{20,16},{24,28},{28,24},{32,36},... | collective-permute-start | bytes 270344 | tf_op jit(solution)/shard_map/ppermute | solution.py:51
  (31 other events, 169.5 us)

commit v8 on v7

--- a/solution.py
+++ b/solution.py
@@ -36,6 +36,19 @@
 
 
 SLOTS = ((0, 0), (1, 0), (3, 0), (0, 1), (2, 0), (1, 1), (3, 1), (2, 1))
+
+
+def core_shifted(shifts):
+    return [
+        (place(z, x, c), place(z ^ shifts[c][1], (x + shifts[c][0]) % X, c))
+        for z in range(Z)
+        for x in range(X)
+        for c in range(C)
+    ]
+
+
+HALVES = (((1, 0), (3, 0)), ((0, 1), (2, 1)), ((1, 1), (2, 0)))
+LAST = (3, 1)
 
 
 def ring_step(turn, count, spread):
@@ -237,7 +250,7 @@
     power_ref[...] = power[:, 0:128] + power[:, 128:256]
 
 
-def tail_kernel(value_ref, p0, p1, p2, p3, out_ref):
+def tail_kernel(value_ref, other_ref, p0, p1, p2, p3, mine_ref, both_ref):
     power = (p0[...] + p2[...]) + (p1[...] + p3[...])
     row = lax.broadcasted_iota(jnp.int32, (8, 256), 0)
     tail = jnp.zeros((8, 256), F32)
@@ -245,29 +258,56 @@
         term = power.astype(BF).astype(F32)
         power = power - term
         tail = jnp.where(row == k, jnp.concatenate([term, jnp.zeros_like(term)], axis=1), tail)
-    out_ref[0:168, :] = value_ref[...]
-    out_ref[168:176, :] = tail.astype(BF)
+    tail = tail.astype(BF)
+    mine_ref[0:168, :] = value_ref[...]
+    mine_ref[168:176, :] = tail
+    both_ref[0, 0:168, :] = value_ref[...]
+    both_ref[0, 168:176, :] = tail
+    both_ref[1, 0:168, :] = other_ref[...]
+    both_ref[1, 168:176, :] = jnp.zeros_like(tail)
 
 
 def finish_kernel(vectors, x_ref, pair_ref, c_ref, *refs):
-    parts, (out_ref, rows, held, sems) = refs[:16], refs[16:]
+    (both, *halves), (last, last_other), rest = refs[:7], refs[7:9], refs[9:]
+    out_ref, rows, held, sems = rest
     x, pair, c = x_ref[0], pair_ref[0], c_ref[0]
-    order = [(0, pair), (0, 1 - pair)] + [(d, parity) for parity in (pair, 1 - pair) for d in (1, 3, 2)]
-    blocks = [side * 8 + lax.rem(x + X - d, X) * 2 + parity for side in (c, 1 - c) for d, parity in order]
-    for k in range(16):
-        tail = parts[k][168:176, :].astype(F32)
+
+    def chip(dx, dp):
+        parity = pair + dp - 2 * pair * dp
+        return lax.rem(x + X - dx, X) * 2 + parity
+
+    parts, powers = [], []
+
+    def add(ref, side, at, k=None):
+        parts.append((ref if k is None else ref.at[k], side * 8 + at))
+
+    for k in range(2):
+        add(both, c if k == 0 else 1 - c, chip(0, 0), k)
+    powers.append((both.at[0], chip(0, 0)))
+    for n, half in enumerate(halves):
+        side = c if n < 3 else 1 - c
+        (a0, a1), (b0, b1) = HALVES[n % 3]
+        at = chip(a0 + side * (b0 - a0), a1 + side * (b1 - a1))
+        add(half, side, at, 0)
+        add(half, 1 - side, at, 1)
+        powers.append((half.at[0], at))
+    add(last, c, chip(*LAST))
+    add(last_other, 1 - c, chip(*LAST))
+    powers.append((last, chip(*LAST)))
+    for ref, at in powers:
+        tail = ref[168:176, :].astype(F32)
         power = (tail[0:1, :] + tail[1:2, :]) + tail[2:3, :]
-        rows[blocks[k]] = power[:, 0:128]
+        rows[at] = power[:, 0:128]
     power = rows[0]
-    for k in range(1, 16):
+    for k in range(1, 8):
         power += rows[k]
     factor = lax.rsqrt(power * (1.0 / vectors) + 1e-06)
     factor = jnp.concatenate([factor, factor], axis=1)
     stores = []
-    for k in range(16):
-        value = parts[k][0:168, :].astype(F32) * factor
+    for k, (ref, at) in enumerate(parts):
+        value = ref[0:168, :].astype(F32) * factor
         held[k] = value.astype(BF)
-        stores.append(pltpu.make_async_copy(held.at[k], out_ref.at[blocks[k]], sems.at[k]))
+        stores.append(pltpu.make_async_copy(held.at[k], out_ref.at[at], sems.at[k]))
         stores[k].start()
     for store in stores:
         store.wait()
@@ -308,23 +348,26 @@
     for d in (2, 1, 3):
         shares[d] = moved(share, shifted(dz=2 * d))
     value, power = whole(consensus_kernel, shares, [near(SUM, BF), near((1, 128), F32)])
+    other, other_power = moved(value, shifted(dc=1)), moved(power, shifted(dc=1))
+    power = whole(pair_kernel, (power, other_power), near((1, 128), F32))
     powers = [power, power, power, power]
     for d in (2, 1, 3):
         powers[d] = lax.ppermute(power, "sub", [(y, (y + d) % 4) for y in range(4)])
-    mine = whole(tail_kernel, (value, *powers), near((ROWS, 256), BF))
-    theirs = moved(mine, pair_shifted(0, 1))
-    same = [mine, theirs]
-    for value in (mine, theirs):
-        for d in (1, 3, 2):
-            same.append(moved(value, shifted(dx=d)))
-    other = [moved(part, shifted(dc=1)) for part in same]
+    outs = [near((ROWS, 256), BF), near((2, ROWS, 256), BF)]
+    mine, both = whole(tail_kernel, (value, other, *powers), outs)
+    got = []
+    for shifts in HALVES:
+        got.append(moved(both, core_shifted(shifts)))
+    last = moved(mine, pair_shifted(*LAST))
+    got += [moved(part, shifted(dc=1)) for part in got]
+    last_other = moved(last, shifted(dc=1))
     total = blocks * lax.axis_size("sub") * vectors
     return whole(
         lambda *refs: finish_kernel(total, *refs),
-        (*here, *same, *other),
+        (*here, both, *got, last, last_other),
         jax.ShapeDtypeStruct((blocks, vectors, 256), BF),
         (
-            pltpu.VMEM((16, 1, 128), F32),
+            pltpu.VMEM((8, 1, 128), F32),
             pltpu.VMEM((16, vectors, 256), BF),
             pltpu.SemaphoreType.DMA((16,)),
         ),

time: 107 us -> 105 us (0.981)
  the two profiles are of different devices: /device:TPU:1 before, /device:TPU:33 now
where the time goes in v8:
time: 105 us; the launch traced here: 104 us
  starting transfers between devices  75.4 us (72%)
  waiting for transfers between devices  17.4 us (17%)
  Pallas kernels  11.4 us (11%)
    ppermute x47, starting transfers between devices, moved(): return lax.ppermute(value, 'cluster', pairs)  70.4 us
    ppermute x47, waiting for transfers between devices, moved(): return lax.ppermute(value, 'cluster', pairs)  16.1 us
    pallas_call x10, Pallas kernels, whole(): pl.pallas_call(kernel, in_specs=[pl.BlockSpec(memory_space=pltpu.SMEM if...  11.4 us
    ppermute x3, starting transfers between devices, per_device(): powers[d] = lax.ppermute(power, 'sub', [(y, (y + d) % 4) for y in range(4)])  4.97 us
  transfers between devices with their start and end apart: 50, of which 13 were waited for; matrix products, arithmetic and copies ran while one was open for 0% of the time, Pallas kernels for 7%

profile of v8, /device:TPU:33, one launch (start us, length us, event | category | flops | bytes accessed | tf_op | source)
XLA Modules:
  0.0 104.4 jit_solution(17025400977937865712)
XLA Ops:
  0.0 2.3 %shard_map.46 = (bf16[2,256,128]{2,1,0:T(8,128)(2,1)S(1)}, bf16[2,256,128]{2,1,0:T(8,128)(2,1)S(1)}, bf16[2,256,128]{2,1,0:T(8,128)(2,1)S(1)}, bf16[2,256,128]{2...) custom-call(s32[1]{0:T(128)} %bitcast.x_ref.refs_0_, ...), custom_call_target="tpu_custom_call" | custom-call | flops 6000000 | bytes 5000000 | tf_op jit(solution)/shard_map/pallas_call | solution.py:117
  2.3 2.8 %collective-permute-start = (bf16[2,256,128]{2,1,0:T(8,128)(2,1)S(1)}, bf16[2,256,128]{2,1,0:T(8,128)(2,1)S(1)}, u32[]{:S(2)}, u32[]{:S(2)}) collective-permute-start(bf16[2,256,128]{2,1,0:T(8,128)(2,1)S(1)} %get-tuple-element.35), channel_id=1, source_target_pairs={{0,16},{4,20},{8,24},{12,28},{16,0},{20,4},{24,8},{28,12},{32,48},... | collective-permute-start | bytes 393224 | tf_op jit(solution)/shard_map/ppermute | solution.py:64
  5.4 2.4 %collective-permute-start.19 = (bf16[2,256,128]{2,1,0:T(8,128)(2,1)S(1)}, bf16[2,256,128]{2,1,0:T(8,128)(2,1)S(1)}, u32[]{:S(2)}, u32[]{:S(2)}) collective-permute-start(bf16[2,256,128]{2,1,0:T(8,128)(2,1)S(1)} %get-tuple-element.45), channel_id=1, source_target_pairs={{0,24},{4,28},{8,0},{12,4},{16,8},{20,12},{24,16},{28,20},{32,56},... | collective-permute-start | bytes 393224 | tf_op jit(solution)/shard_map/ppermute | solution.py:64
  8.3 3.1 %collective-permute-start.4 = (bf16[2,256,128]{2,1,0:T(8,128)(2,1)S(1)}, bf16[2,256,128]{2,1,0:T(8,128)(2,1)S(1)}, u32[]{:S(2)}, u32[]{:S(2)}) collective-permute-start(bf16[2,256,128]{2,1,0:T(8,128)(2,1)S(1)} %get-tuple-element.37), channel_id=1, source_target_pairs={{0,56},{4,60},{8,32},{12,36},{16,40},{20,44},{24,48},{28,52},{32,2... | collective-permute-start | bytes 393224 | tf_op jit(solution)/shard_map/ppermute | solution.py:64
  13.5 3.7 %collective-permute-start.16 = (bf16[2,256,128]{2,1,0:T(8,128)(2,1)S(1)}, bf16[2,256,128]{2,1,0:T(8,128)(2,1)S(1)}, u32[]{:S(2)}, u32[]{:S(2)}) collective-permute-start(bf16[2,256,128]{2,1,0:T(8,128)(2,1)S(1)} %get-tuple-element.43.refs_0_), channel_id=1, source_target_pairs={{0,4},{4,0},{8,12},{12,8},{16,20},{20,16},{24,28},{28,24},{32,36},... | collective-permute-start | bytes 393224 | tf_op jit(solution)/shard_map/ppermute | solution.py:64
  18.1 1.6 %collective-permute-start.28 = (bf16[2,296,128]{2,1,0:T(8,128)(2,1)S(1)}, bf16[2,296,128]{2,1,0:T(8,128)(2,1)S(1)}, u32[]{:S(2)}, u32[]{:S(2)}) collective-permute-start(bf16[2,296,128]{2,1,0:T(8,128)(2,1)S(1)} %get-tuple-element.50), channel_id=1, source_target_pairs={{0,32},{4,36},{8,40},{12,44},{16,48},{20,52},{24,56},{28,60},{32,0... | collective-permute-start | bytes 454664 | tf_op jit(solution)/shard_map/ppermute | solution.py:64
  19.7 2.9 %collective-permute-start.23 = (bf16[2,296,128]{2,1,0:T(8,128)(2,1)S(1)}, bf16[2,296,128]{2,1,0:T(8,128)(2,1)S(1)}, u32[]{:S(2)}, u32[]{:S(2)}) collective-permute-start(bf16[2,296,128]{2,1,0:T(8,128)(2,1)S(1)} %get-tuple-element.47.refs_8_), channel_id=1, source_target_pairs={{0,4},{4,0},{8,12},{12,8},{16,20},{20,16},{24,28},{28,24},{32,36},... | collective-permute-start | bytes 454664 | tf_op jit(solution)/shard_map/ppermute | solution.py:64
  23.4 3.3 %collective-permute-start.12 = (bf16[2,296,128]{2,1,0:T(8,128)(2,1)S(1)}, bf16[2,296,128]{2,1,0:T(8,128)(2,1)S(1)}, u32[]{:S(2)}, u32[]{:S(2)}) collective-permute-start(bf16[2,296,128]{2,1,0:T(8,128)(2,1)S(1)} %get-tuple-element.41), channel_id=1, source_target_pairs={{0,56},{4,60},{8,32},{12,36},{16,40},{20,44},{24,48},{28,52},{32,2... | collective-permute-start | bytes 454664 | tf_op jit(solution)/shard_map/ppermute | solution.py:64
  27.6 3.6 %collective-permute-done.10.refs_10_ = bf16[2,296,128]{2,1,0:T(8,128)(2,1)S(1)} collective-permute-done((bf16[2,296,128]{2,1,0:T(8,128)(2,1)S(1)}, bf16[2,296,128]{2,1,0:T(8,128)(2,1)S(1)}, u32[]{:S(2)}, u32[]{:S(2)}) %collective-permute-start.10) | collective-permute-done | bytes 151584 | tf_op jit(solution)/shard_map/ppermute | solution.py:64
  39.4 3.3 %collective-permute-done.14.refs_14_ = bf16[2,296,128]{2,1,0:T(8,128)(2,1)S(1)} collective-permute-done((bf16[2,296,128]{2,1,0:T(8,128)(2,1)S(1)}, bf16[2,296,128]{2,1,0:T(8,128)(2,1)S(1)}, u32[]{:S(2)}, u32[]{:S(2)}) %collective-permute-start.14) | collective-permute-done | bytes 151584 | tf_op jit(solution)/shard_map/ppermute | solution.py:64
  42.8 3.0 %collective-permute-start.30 = (bf16[128,256]{1,0:T(8,128)(2,1)S(1)}, bf16[128,256]{1,0:T(8,128)(2,1)S(1)}, u32[]{:S(2)}, u32[]{:S(2)}) collective-permute-start(bf16[128,256]{1,0:T(8,128)(2,1)S(1)} %get-tuple-element.57.refs_0_), channel_id=1, source_target_pairs={{0,64},{4,68},{8,72},{12,76},{16,80},{20,84},{24,88},{28,92},{32,9... | collective-permute-start | bytes 196616 | tf_op jit(solution)/shard_map/ppermute | solution.py:64
  47.9 4.2 %collective-permute-start.31 = (bf16[128,256]{1,0:T(8,128)(2,1)S(1)}, bf16[128,256]{1,0:T(8,128)(2,1)S(1)}, u32[]{:S(2)}, u32[]{:S(2)}) collective-permute-start(bf16[128,256]{1,0:T(8,128)(2,1)S(1)} %get-tuple-element.58.refs_1_), channel_id=1, source_target_pairs={{0,192},{4,196},{8,200},{12,204},{16,208},{20,212},{24,216},{28,22... | collective-permute-start | bytes 196616 | tf_op jit(solution)/shard_map/ppermute | solution.py:64
  52.1 3.0 %shard_map.47 = (f32[168,256]{1,0:T(8,128)S(1)}, f32[168,256]{1,0:T(8,128)S(1)}, f32[168,256]{1,0:T(8,128)S(1)}) custom-call(bf16[2,256,128]{2,1,0:T(8,128)(2,1)S(1)} %get-tuple-element.43.refs_0_, bf16[2,256,128]{2,1,0:T(8,128)(2,1)S(1)} %collective-permute-done.16.refs_1_, bf16[2,256,128]{2,1,0:T(8,128)(2,1)S(1)} %collective-permute-done.17.refs_2_, ...), custom_call_target="tpu_custom_call" | custom-call | flops 2000000000 | bytes 3000000 | tf_op jit(solution)/shard_map/pallas_call | solution.py:117
  55.1 2.4 %collective-permute-start.32 = (bf16[128,256]{1,0:T(8,128)(2,1)S(1)}, bf16[128,256]{1,0:T(8,128)(2,1)S(1)}, u32[]{:S(2)}, u32[]{:S(2)}) collective-permute-start(bf16[128,256]{1,0:T(8,128)(2,1)S(1)} %get-tuple-element.59.refs_0_), channel_id=1, source_target_pairs={{0,192},{4,196},{8,200},{12,204},{16,208},{20,212},{24,216},{28,22... | collective-permute-start | bytes 196616 | tf_op jit(solution)/shard_map/ppermute | solution.py:64
  57.5 1.8 %collective-permute-start.33 = (bf16[128,256]{1,0:T(8,128)(2,1)S(1)}, bf16[128,256]{1,0:T(8,128)(2,1)S(1)}, u32[]{:S(2)}, u32[]{:S(2)}) collective-permute-start(bf16[128,256]{1,0:T(8,128)(2,1)S(1)} %get-tuple-element.60.refs_2_), channel_id=1, source_target_pairs={{0,64},{4,68},{8,72},{12,76},{16,80},{20,84},{24,88},{28,92},{32,9... | collective-permute-start | bytes 196616 | tf_op jit(solution)/shard_map/ppermute | solution.py:64
  59.3 3.0 %shard_map.48 = (f32[168,256]{1,0:T(8,128)S(1)}, f32[168,256]{1,0:T(8,128)S(1)}, f32[168,256]{1,0:T(8,128)S(1)}) custom-call(bf16[2,256,128]{2,1,0:T(8,128)(2,1)S(1)} %collective-permute-done.refs_0_.refs_8_, bf16[2,256,128]{2,1,0:T(8,128)(2,1)S(1)} %collective-permute-done.1.refs_1_.refs_9_, ...), custom_call_target="tpu_custom_call" | custom-call | flops 2000000000 | bytes 3000000 | tf_op jit(solution)/shard_map/pallas_call | solution.py:117
  62.7 1.9 %collective-permute-start.34 = (bf16[168,256]{1,0:T(8,128)(2,1)S(1)}, bf16[168,256]{1,0:T(8,128)(2,1)S(1)}, u32[]{:S(2)}, u32[]{:S(2)}) collective-permute-start(bf16[168,256]{1,0:T(8,128)(2,1)S(1)} %shard_map.51.s0), channel_id=1, source_target_pairs={{0,64},{4,68},{8,72},{12,76},{16,80},{20,84},{24,88},{28,92},{32,9... | collective-permute-start | bytes 258056 | tf_op jit(solution)/shard_map/ppermute | solution.py:64
  66.1 2.7 %collective-permute-start.36 = (bf16[168,256]{1,0:T(8,128)(2,1)S(1)}, bf16[168,256]{1,0:T(8,128)(2,1)S(1)}, u32[]{:S(2)}, u32[]{:S(2)}) collective-permute-start(bf16[168,256]{1,0:T(8,128)(2,1)S(1)} %shard_map.51.s0), channel_id=1, source_target_pairs={{0,192},{4,196},{8,200},{12,204},{16,208},{20,212},{24,216},{28,22... | collective-permute-start | bytes 258056 | tf_op jit(solution)/shard_map/ppermute | solution.py:64
  68.8 3.8 %collective-permute-done.35.s2 = bf16[168,256]{1,0:T(8,128)(2,1)S(1)} collective-permute-done((bf16[168,256]{1,0:T(8,128)(2,1)S(1)}, bf16[168,256]{1,0:T(8,128)(2,1)S(1)}, u32[]{:S(2)}, u32[]{:S(2)}) %collective-permute-start.35) | collective-permute-done | bytes 86048 | tf_op jit(solution)/shard_map/ppermute | solution.py:64
  72.7 6.6 %collective-permute-start.37 = (bf16[168,256]{1,0:T(8,128)(2,1)S(1)}, bf16[168,256]{1,0:T(8,128)(2,1)S(1)}, u32[]{:S(2)}, u32[]{:S(2)}) collective-permute-start(bf16[168,256]{1,0:T(8,128)(2,1)S(1)} %get-tuple-element.61.value_ref), channel_id=1, source_target_pairs={{0,4},{4,0},{8,12},{12,8},{16,20},{20,16},{24,28},{28,24},{32,36},... | collective-permute-start | bytes 258056 | tf_op jit(solution)/shard_map/ppermute | solution.py:64
  81.7 2.6 %collective-permute-start.40 = (f32[1,128]{1,0:T(1,128)S(1)}, f32[1,128]{1,0:T(1,128)S(1)}, u32[]{:S(2)}, u32[]{:S(2)}) collective-permute-start(f32[1,128]{1,0:T(1,128)S(1)} %shard_map.53.p0), channel_id=1, source_target_pairs={{0,2},{1,3},{2,0},{3,1},{4,6},{5,7},{6,4},{7,5},{8,10},{9,11},{10,... | collective-permute-start | bytes 1544 | tf_op jit(solution)/shard_map/ppermute | solution.py:355
  86.8 1.7 %collective-permute-start.42 = (bf16[2,176,256]{2,1,0:T(8,128)(2,1)S(1)}, bf16[2,176,256]{2,1,0:T(8,128)(2,1)S(1)}, u32[]{:S(2)}, u32[]{:S(2)}) collective-permute-start(bf16[2,176,256]{2,1,0:T(8,128)(2,1)S(1)} %get-tuple-element.63.refs_3_), channel_id=1, source_target_pairs={{0,8},{4,28},{8,16},{12,4},{16,24},{20,12},{24,0},{28,20},{32,40},... | collective-permute-start | bytes 540680 | tf_op jit(solution)/shard_map/ppermute | solution.py:64
  90.2 3.0 %collective-permute-start.48 = (bf16[176,256]{1,0:T(8,128)(2,1)S(1)}, bf16[176,256]{1,0:T(8,128)(2,1)S(1)}, u32[]{:S(2)}, u32[]{:S(2)}) collective-permute-start(bf16[176,256]{1,0:T(8,128)(2,1)S(1)} %get-tuple-element.64), channel_id=1, source_target_pairs={{0,56},{4,60},{8,32},{12,36},{16,40},{20,44},{24,48},{28,52},{32,2... | collective-permute-start | bytes 270344 | tf_op jit(solution)/shard_map/ppermute | solution.py:64
  94.0 7.2 %collective-permute-start.45 = (bf16[2,176,256]{2,1,0:T(8,128)(2,1)S(1)}, bf16[2,176,256]{2,1,0:T(8,128)(2,1)S(1)}, u32[]{:S(2)}, u32[]{:S(2)}) collective-permute-start(bf16[2,176,256]{2,1,0:T(8,128)(2,1)S(1)} %collective-permute-done.42.refs_4_), channel_id=1, source_target_pairs={{0,4},{4,0},{8,12},{12,8},{16,20},{20,16},{24,28},{28,24},{32,36},... | collective-permute-start | bytes 540680 | tf_op jit(solution)/shard_map/ppermute | solution.py:64
  (86 shorter events, 28.2 us)
Async XLA Ops:
  7.8 9.4 %collective-permute-start.2 = (bf16[2,256,128]{2,1,0:T(8,128)(2,1)S(1)}, bf16[2,256,128]{2,1,0:T(8,128)(2,1)S(1)}, u32[]{:S(2)}, u32[]{:S(2)}) collective-permute-start(bf16[2,256,128]{2,1,0:T(8,128)(2,1)S(1)} %get-tuple-element.36), channel_id=1, source_target_pairs={{0,40},{4,44},{8,48},{12,52},{16,56},{20,60},{24,32},{28,36},{32,8... | collective-permute-start | bytes 393224 | tf_op jit(solution)/shard_map/ppermute | solution.py:64
  8.3 9.8 %collective-permute-start.4 = (bf16[2,256,128]{2,1,0:T(8,128)(2,1)S(1)}, bf16[2,256,128]{2,1,0:T(8,128)(2,1)S(1)}, u32[]{:S(2)}, u32[]{:S(2)}) collective-permute-start(bf16[2,256,128]{2,1,0:T(8,128)(2,1)S(1)} %get-tuple-element.37), channel_id=1, source_target_pairs={{0,56},{4,60},{8,32},{12,36},{16,40},{20,44},{24,48},{28,52},{32,2... | collective-permute-start | bytes 393224 | tf_op jit(solution)/shard_map/ppermute | solution.py:64
  11.8 11.6 %collective-permute-start.24 = (bf16[2,296,128]{2,1,0:T(8,128)(2,1)S(1)}, bf16[2,296,128]{2,1,0:T(8,128)(2,1)S(1)}, u32[]{:S(2)}, u32[]{:S(2)}) collective-permute-start(bf16[2,296,128]{2,1,0:T(8,128)(2,1)S(1)} %get-tuple-element.48), channel_id=1, source_target_pairs={{0,8},{4,12},{8,16},{12,20},{16,24},{20,28},{24,0},{28,4},{32,40},... | collective-permute-start | bytes 454664 | tf_op jit(solution)/shard_map/ppermute | solution.py:64
  13.5 9.1 %collective-permute-start.16 = (bf16[2,256,128]{2,1,0:T(8,128)(2,1)S(1)}, bf16[2,256,128]{2,1,0:T(8,128)(2,1)S(1)}, u32[]{:S(2)}, u32[]{:S(2)}) collective-permute-start(bf16[2,256,128]{2,1,0:T(8,128)(2,1)S(1)} %get-tuple-element.43.refs_0_), channel_id=1, source_target_pairs={{0,4},{4,0},{8,12},{12,8},{16,20},{20,16},{24,28},{28,24},{32,36},... | collective-permute-start | bytes 393224 | tf_op jit(solution)/shard_map/ppermute | solution.py:64
  17.2 9.6 %collective-permute-start.26 = (bf16[2,296,128]{2,1,0:T(8,128)(2,1)S(1)}, bf16[2,296,128]{2,1,0:T(8,128)(2,1)S(1)}, u32[]{:S(2)}, u32[]{:S(2)}) collective-permute-start(bf16[2,296,128]{2,1,0:T(8,128)(2,1)S(1)} %get-tuple-element.49), channel_id=1, source_target_pairs={{0,24},{4,28},{8,0},{12,4},{16,8},{20,12},{24,16},{28,20},{32,56},... | collective-permute-start | bytes 454664 | tf_op jit(solution)/shard_map/ppermute | solution.py:64
  18.1 9.0 %collective-permute-start.28 = (bf16[2,296,128]{2,1,0:T(8,128)(2,1)S(1)}, bf16[2,296,128]{2,1,0:T(8,128)(2,1)S(1)}, u32[]{:S(2)}, u32[]{:S(2)}) collective-permute-start(bf16[2,296,128]{2,1,0:T(8,128)(2,1)S(1)} %get-tuple-element.50), channel_id=1, source_target_pairs={{0,32},{4,36},{8,40},{12,44},{16,48},{20,52},{24,56},{28,60},{32,0... | collective-permute-start | bytes 454664 | tf_op jit(solution)/shard_map/ppermute | solution.py:64
  22.6 8.5 %collective-permute-start.10 = (bf16[2,296,128]{2,1,0:T(8,128)(2,1)S(1)}, bf16[2,296,128]{2,1,0:T(8,128)(2,1)S(1)}, u32[]{:S(2)}, u32[]{:S(2)}) collective-permute-start(bf16[2,296,128]{2,1,0:T(8,128)(2,1)S(1)} %get-tuple-element.40), channel_id=1, source_target_pairs={{0,40},{4,44},{8,48},{12,52},{16,56},{20,60},{24,32},{28,36},{32,8... | collective-permute-start | bytes 454664 | tf_op jit(solution)/shard_map/ppermute | solution.py:64
  23.4 10.1 %collective-permute-start.12 = (bf16[2,296,128]{2,1,0:T(8,128)(2,1)S(1)}, bf16[2,296,128]{2,1,0:T(8,128)(2,1)S(1)}, u32[]{:S(2)}, u32[]{:S(2)}) collective-permute-start(bf16[2,296,128]{2,1,0:T(8,128)(2,1)S(1)} %get-tuple-element.41), channel_id=1, source_target_pairs={{0,56},{4,60},{8,32},{12,36},{16,40},{20,44},{24,48},{28,52},{32,2... | collective-permute-start | bytes 454664 | tf_op jit(solution)/shard_map/ppermute | solution.py:64
  26.8 7.7 %collective-permute-start.1 = (bf16[2,256,128]{2,1,0:T(8,128)(2,1)S(1)}, bf16[2,256,128]{2,1,0:T(8,128)(2,1)S(1)}, u32[]{:S(2)}, u32[]{:S(2)}) collective-permute-start(bf16[2,256,128]{2,1,0:T(8,128)(2,1)S(1)} %collective-permute-done.refs_0_.refs_8_), channel_id=1, source_target_pairs={{0,4},{4,0},{8,12},{12,8},{16,20},{20,16},{24,28},{28,24},{32,36},... | collective-permute-start | bytes 393224 | tf_op jit(solution)/shard_map/ppermute | solution.py:64
  34.9 7.8 %collective-permute-start.14 = (bf16[2,296,128]{2,1,0:T(8,128)(2,1)S(1)}, bf16[2,296,128]{2,1,0:T(8,128)(2,1)S(1)}, u32[]{:S(2)}, u32[]{:S(2)}) collective-permute-start(bf16[2,296,128]{2,1,0:T(8,128)(2,1)S(1)} %get-tuple-element.42), channel_id=1, source_target_pairs={{0,48},{4,52},{8,56},{12,60},{16,32},{20,36},{24,40},{28,44},{32,1... | collective-permute-start | bytes 454664 | tf_op jit(solution)/shard_map/ppermute | solution.py:64
  36.6 9.9 %collective-permute-start.8 = (bf16[2,296,128]{2,1,0:T(8,128)(2,1)S(1)}, bf16[2,296,128]{2,1,0:T(8,128)(2,1)S(1)}, u32[]{:S(2)}, u32[]{:S(2)}) collective-permute-start(bf16[2,296,128]{2,1,0:T(8,128)(2,1)S(1)} %get-tuple-element.39), channel_id=1, source_target_pairs={{0,16},{4,20},{8,24},{12,28},{16,0},{20,4},{24,8},{28,12},{32,48},... | collective-permute-start | bytes 454664 | tf_op jit(solution)/shard_map/ppermute | solution.py:64
  37.2 9.8 %collective-permute-start.25 = (bf16[2,296,128]{2,1,0:T(8,128)(2,1)S(1)}, bf16[2,296,128]{2,1,0:T(8,128)(2,1)S(1)}, u32[]{:S(2)}, u32[]{:S(2)}) collective-permute-start(bf16[2,296,128]{2,1,0:T(8,128)(2,1)S(1)} %collective-permute-done.24.refs_10_), channel_id=1, source_target_pairs={{0,4},{4,0},{8,12},{12,8},{16,20},{20,16},{24,28},{28,24},{32,36},... | collective-permute-start | bytes 454664 | tf_op jit(solution)/shard_map/ppermute | solution.py:64
  37.6 9.5 %collective-permute-start.27 = (bf16[2,296,128]{2,1,0:T(8,128)(2,1)S(1)}, bf16[2,296,128]{2,1,0:T(8,128)(2,1)S(1)}, u32[]{:S(2)}, u32[]{:S(2)}) collective-permute-start(bf16[2,296,128]{2,1,0:T(8,128)(2,1)S(1)} %collective-permute-done.26.refs_12_), channel_id=1, source_target_pairs={{0,4},{4,0},{8,12},{12,8},{16,20},{20,16},{24,28},{28,24},{32,36},... | collective-permute-start | bytes 454664 | tf_op jit(solution)/shard_map/ppermute | solution.py:64
  37.7 9.8 %collective-permute-start.29 = (bf16[2,296,128]{2,1,0:T(8,128)(2,1)S(1)}, bf16[2,296,128]{2,1,0:T(8,128)(2,1)S(1)}, u32[]{:S(2)}, u32[]{:S(2)}) collective-permute-start(bf16[2,296,128]{2,1,0:T(8,128)(2,1)S(1)} %collective-permute-done.28.refs_14_), channel_id=1, source_target_pairs={{0,4},{4,0},{8,12},{12,8},{16,20},{20,16},{24,28},{28,24},{32,36},... | collective-permute-start | bytes 454664 | tf_op jit(solution)/shard_map/ppermute | solution.py:64
  46.5 11.1 %collective-permute-start.11 = (bf16[2,296,128]{2,1,0:T(8,128)(2,1)S(1)}, bf16[2,296,128]{2,1,0:T(8,128)(2,1)S(1)}, u32[]{:S(2)}, u32[]{:S(2)}) collective-permute-start(bf16[2,296,128]{2,1,0:T(8,128)(2,1)S(1)} %collective-permute-done.10.refs_10_), channel_id=1, source_target_pairs={{0,4},{4,0},{8,12},{12,8},{16,20},{20,16},{24,28},{28,24},{32,36},... | collective-permute-start | bytes 454664 | tf_op jit(solution)/shard_map/ppermute | solution.py:64
  47.1 12.2 %collective-permute-start.13 = (bf16[2,296,128]{2,1,0:T(8,128)(2,1)S(1)}, bf16[2,296,128]{2,1,0:T(8,128)(2,1)S(1)}, u32[]{:S(2)}, u32[]{:S(2)}) collective-permute-start(bf16[2,296,128]{2,1,0:T(8,128)(2,1)S(1)} %collective-permute-done.12.refs_12_), channel_id=1, source_target_pairs={{0,4},{4,0},{8,12},{12,8},{16,20},{20,16},{24,28},{28,24},{32,36},... | collective-permute-start | bytes 454664 | tf_op jit(solution)/shard_map/ppermute | solution.py:64
  47.2 12.1 %collective-permute-start.15 = (bf16[2,296,128]{2,1,0:T(8,128)(2,1)S(1)}, bf16[2,296,128]{2,1,0:T(8,128)(2,1)S(1)}, u32[]{:S(2)}, u32[]{:S(2)}) collective-permute-start(bf16[2,296,128]{2,1,0:T(8,128)(2,1)S(1)} %collective-permute-done.14.refs_14_), channel_id=1, source_target_pairs={{0,4},{4,0},{8,12},{12,8},{16,20},{20,16},{24,28},{28,24},{32,36},... | collective-permute-start | bytes 454664 | tf_op jit(solution)/shard_map/ppermute | solution.py:64
  47.6 11.7 %collective-permute-start.9 = (bf16[2,296,128]{2,1,0:T(8,128)(2,1)S(1)}, bf16[2,296,128]{2,1,0:T(8,128)(2,1)S(1)}, u32[]{:S(2)}, u32[]{:S(2)}) collective-permute-start(bf16[2,296,128]{2,1,0:T(8,128)(2,1)S(1)} %collective-permute-done.8.refs_8_), channel_id=1, source_target_pairs={{0,4},{4,0},{8,12},{12,8},{16,20},{20,16},{24,28},{28,24},{32,36},... | collective-permute-start | bytes 454664 | tf_op jit(solution)/shard_map/ppermute | solution.py:64
  64.6 8.0 %collective-permute-start.35 = (bf16[168,256]{1,0:T(8,128)(2,1)S(1)}, bf16[168,256]{1,0:T(8,128)(2,1)S(1)}, u32[]{:S(2)}, u32[]{:S(2)}) collective-permute-start(bf16[168,256]{1,0:T(8,128)(2,1)S(1)} %shard_map.51.s0), channel_id=1, source_target_pairs={{0,128},{4,132},{8,136},{12,140},{16,144},{20,148},{24,152},{28,15... | collective-permute-start | bytes 258056 | tf_op jit(solution)/shard_map/ppermute | solution.py:64
  72.7 14.1 %collective-permute-start.37 = (bf16[168,256]{1,0:T(8,128)(2,1)S(1)}, bf16[168,256]{1,0:T(8,128)(2,1)S(1)}, u32[]{:S(2)}, u32[]{:S(2)}) collective-permute-start(bf16[168,256]{1,0:T(8,128)(2,1)S(1)} %get-tuple-element.61.value_ref), channel_id=1, source_target_pairs={{0,4},{4,0},{8,12},{12,8},{16,20},{20,16},{24,28},{28,24},{32,36},... | collective-permute-start | bytes 258056 | tf_op jit(solution)/shard_map/ppermute | solution.py:64
  88.5 12.7 %collective-permute-start.43 = (bf16[2,176,256]{2,1,0:T(8,128)(2,1)S(1)}, bf16[2,176,256]{2,1,0:T(8,128)(2,1)S(1)}, u32[]{:S(2)}, u32[]{:S(2)}) collective-permute-start(bf16[2,176,256]{2,1,0:T(8,128)(2,1)S(1)} %get-tuple-element.63.refs_3_), channel_id=1, source_target_pairs={{0,32},{4,52},{8,40},{12,60},{16,48},{20,36},{24,56},{28,44},{32,0... | collective-permute-start | bytes 540680 | tf_op jit(solution)/shard_map/ppermute | solution.py:64
  88.8 12.3 %collective-permute-start.44 = (bf16[2,176,256]{2,1,0:T(8,128)(2,1)S(1)}, bf16[2,176,256]{2,1,0:T(8,128)(2,1)S(1)}, u32[]{:S(2)}, u32[]{:S(2)}) collective-permute-start(bf16[2,176,256]{2,1,0:T(8,128)(2,1)S(1)} %get-tuple-element.63.refs_3_), channel_id=1, source_target_pairs={{0,40},{4,20},{8,48},{12,28},{16,56},{20,4},{24,32},{28,12},{32,8}... | collective-permute-start | bytes 540680 | tf_op jit(solution)/shard_map/ppermute | solution.py:64
  90.2 11.5 %collective-permute-start.48 = (bf16[176,256]{1,0:T(8,128)(2,1)S(1)}, bf16[176,256]{1,0:T(8,128)(2,1)S(1)}, u32[]{:S(2)}, u32[]{:S(2)}) collective-permute-start(bf16[176,256]{1,0:T(8,128)(2,1)S(1)} %get-tuple-element.64), channel_id=1, source_target_pairs={{0,56},{4,60},{8,32},{12,36},{16,40},{20,44},{24,48},{28,52},{32,2... | collective-permute-start | bytes 270344 | tf_op jit(solution)/shard_map/ppermute | solution.py:64
  94.0 9.0 %collective-permute-start.45 = (bf16[2,176,256]{2,1,0:T(8,128)(2,1)S(1)}, bf16[2,176,256]{2,1,0:T(8,128)(2,1)S(1)}, u32[]{:S(2)}, u32[]{:S(2)}) collective-permute-start(bf16[2,176,256]{2,1,0:T(8,128)(2,1)S(1)} %collective-permute-done.42.refs_4_), channel_id=1, source_target_pairs={{0,4},{4,0},{8,12},{12,8},{16,20},{20,16},{24,28},{28,24},{32,36},... | collective-permute-start | bytes 540680 | tf_op jit(solution)/shard_map/ppermute | solution.py:64
  (26 other events, 132.2 us)

commit v9 on v8

--- a/solution.py
+++ b/solution.py
@@ -159,35 +159,20 @@
 
 def estimate_kernel(before, *refs):
     invs, sigs, old, rest = refs[:8], refs[8:16], refs[16 : 16 + before], refs[16 + before :]
-    p, d, t, held_inv, held_sig = rest
-    for k in range(8):
-        held_inv[k] = invs[k][k % 2]
-        held_sig[k] = sigs[k][k % 2]
+    p, d, t = rest
     for k, ref in enumerate((p, d, t)):
         ref[...] = old[k][...] if before else jnp.zeros_like(ref)
-
-    def two(k, carry):
-        k = 2 * k
-        add_estimates((held_inv[k], held_inv[k + 1]), (held_sig[k], held_sig[k + 1]), p, d, t)
-        return carry
-
-    lax.fori_loop(0, 4, two, 0)
+    for k in range(0, 8, 2):
+        add_estimates((invs[k][0], invs[k + 1][1]), (sigs[k][0], sigs[k + 1][1]), p, d, t)
 
 
 def mean_kernel(*refs):
-    invs, first_ref, second_ref, av, held = refs[:-4], *refs[-4:]
+    invs, first_ref, second_ref, av = refs[:-3], *refs[-3:]
     av[...] = jnp.zeros_like(av)
     for k, inv in enumerate(invs):
-        held[k] = inv[k % 2]
-
-    def four(k, carry):
-        for j in range(4):
-            top, square = square_of(held[4 * k + j])
-            av[0:128, :] += top.astype(F32)
-            av[128:256, :] += dot(top, square)
-        return carry
-
-    lax.fori_loop(0, 4, four, 0)
+        top, square = square_of(inv[k % 2])
+        av[0:128, :] += top.astype(F32)
+        av[128:256, :] += dot(top, square)
     ones = (
         lax.broadcasted_iota(jnp.int32, (128, 256), 0) == lax.broadcasted_iota(jnp.int32, (128, 256), 1)
     ).astype(F32) * 16.0
@@ -207,18 +192,16 @@
 
 
 def estimates(invs, sigs, before=()):
-    scratch = [pltpu.VMEM((8, 256, 128), BF), pltpu.VMEM((8, 296, 128), BF)]
     return whole(
         lambda *refs: estimate_kernel(len(before), *refs),
         [*invs, *sigs, *before],
         [near(SUM, F32)] * 3,
-        scratch,
-        COST,
+        cost=COST,
     )
 
 
 def mean_sums(invs):
-    scratch = [pltpu.VMEM((256, 256), F32), pltpu.VMEM((16, 256, 128), BF)]
+    scratch = [pltpu.VMEM((256, 256), F32)]
     return whole(mean_kernel, invs, [near((128, 256), BF)] * 2, scratch, COST)
 
 

time: 105 us -> 104 us (level)
  Pallas kernels: 11.4 us -> 8.85 us
  waiting for transfers between devices: 17.4 us -> 18.6 us
  starting transfers between devices: 75.4 us -> 76.6 us
    pallas_call x10, Pallas kernels: 11.4 us -> 8.85 us  [whole(): pl.pallas_call(kernel, in_specs=[pl.BlockSpec(memory_space=pltpu.SMEM if...]
    ppermute x47, starting transfers between devices: 70.4 us -> 71.6 us  [moved(): return lax.ppermute(value, 'cluster', pairs)]
    ppermute x47, waiting for transfers between devices: 16.1 us -> 17.2 us  [moved(): return lax.ppermute(value, 'cluster', pairs)]
  transfers between devices with their start and end apart: 50 -> 50, of which waited for: 13 -> 15; matrix products, arithmetic and copies ran while one was open for 0% -> 0% of each run, Pallas kernels for 7% -> 5%
where the time goes in v9:
time: 104 us
  starting transfers between devices  76.6 us (74%)
  waiting for transfers between devices  18.6 us (18%)
  Pallas kernels  8.85 us (9%)
    ppermute x47, starting transfers between devices, moved(): return lax.ppermute(value, 'cluster', pairs)  71.6 us
    ppermute x47, waiting for transfers between devices, moved(): return lax.ppermute(value, 'cluster', pairs)  17.2 us
    pallas_call x10, Pallas kernels, whole(): pl.pallas_call(kernel, in_specs=[pl.BlockSpec(memory_space=pltpu.SMEM if...  8.85 us
    ppermute x3, starting transfers between devices, per_device(): powers[d] = lax.ppermute(power, 'sub', [(y, (y + d) % 4) for y in range(4)])  4.99 us
  transfers between devices with their start and end apart: 50, of which 15 were waited for; matrix products, arithmetic and copies ran while one was open for 0% of the time, Pallas kernels for 5%

profile of v9, /device:TPU:33, one launch (start us, length us, event | category | flops | bytes accessed | tf_op | source)
XLA Modules:
  0.0 104.3 jit_solution(7802004547690296226)
XLA Ops:
  0.0 2.3 %shard_map.46 = (bf16[2,256,128]{2,1,0:T(8,128)(2,1)S(1)}, bf16[2,256,128]{2,1,0:T(8,128)(2,1)S(1)}, bf16[2,256,128]{2,1,0:T(8,128)(2,1)S(1)}, bf16[2,256,128]{2...) custom-call(s32[1]{0:T(128)} %bitcast.x_ref.refs_0_, ...), custom_call_target="tpu_custom_call" | custom-call | flops 6000000 | bytes 5000000 | tf_op jit(solution)/shard_map/pallas_call | solution.py:117
  2.3 2.8 %collective-permute-start = (bf16[2,256,128]{2,1,0:T(8,128)(2,1)S(1)}, bf16[2,256,128]{2,1,0:T(8,128)(2,1)S(1)}, u32[]{:S(2)}, u32[]{:S(2)}) collective-permute-start(bf16[2,256,128]{2,1,0:T(8,128)(2,1)S(1)} %get-tuple-element.35), channel_id=1, source_target_pairs={{0,16},{4,20},{8,24},{12,28},{16,0},{20,4},{24,8},{28,12},{32,48},... | collective-permute-start | bytes 393224 | tf_op jit(solution)/shard_map/ppermute | solution.py:64
  5.4 2.4 %collective-permute-start.19 = (bf16[2,256,128]{2,1,0:T(8,128)(2,1)S(1)}, bf16[2,256,128]{2,1,0:T(8,128)(2,1)S(1)}, u32[]{:S(2)}, u32[]{:S(2)}) collective-permute-start(bf16[2,256,128]{2,1,0:T(8,128)(2,1)S(1)} %get-tuple-element.45), channel_id=1, source_target_pairs={{0,24},{4,28},{8,0},{12,4},{16,8},{20,12},{24,16},{28,20},{32,56},... | collective-permute-start | bytes 393224 | tf_op jit(solution)/shard_map/ppermute | solution.py:64
  8.3 3.1 %collective-permute-start.4 = (bf16[2,256,128]{2,1,0:T(8,128)(2,1)S(1)}, bf16[2,256,128]{2,1,0:T(8,128)(2,1)S(1)}, u32[]{:S(2)}, u32[]{:S(2)}) collective-permute-start(bf16[2,256,128]{2,1,0:T(8,128)(2,1)S(1)} %get-tuple-element.37), channel_id=1, source_target_pairs={{0,56},{4,60},{8,32},{12,36},{16,40},{20,44},{24,48},{28,52},{32,2... | collective-permute-start | bytes 393224 | tf_op jit(solution)/shard_map/ppermute | solution.py:64
  13.5 3.7 %collective-permute-start.16 = (bf16[2,256,128]{2,1,0:T(8,128)(2,1)S(1)}, bf16[2,256,128]{2,1,0:T(8,128)(2,1)S(1)}, u32[]{:S(2)}, u32[]{:S(2)}) collective-permute-start(bf16[2,256,128]{2,1,0:T(8,128)(2,1)S(1)} %get-tuple-element.43.refs_0_), channel_id=1, source_target_pairs={{0,4},{4,0},{8,12},{12,8},{16,20},{20,16},{24,28},{28,24},{32,36},... | collective-permute-start | bytes 393224 | tf_op jit(solution)/shard_map/ppermute | solution.py:64
  18.1 1.6 %collective-permute-start.28 = (bf16[2,296,128]{2,1,0:T(8,128)(2,1)S(1)}, bf16[2,296,128]{2,1,0:T(8,128)(2,1)S(1)}, u32[]{:S(2)}, u32[]{:S(2)}) collective-permute-start(bf16[2,296,128]{2,1,0:T(8,128)(2,1)S(1)} %get-tuple-element.50), channel_id=1, source_target_pairs={{0,32},{4,36},{8,40},{12,44},{16,48},{20,52},{24,56},{28,60},{32,0... | collective-permute-start | bytes 454664 | tf_op jit(solution)/shard_map/ppermute | solution.py:64
  19.7 2.9 %collective-permute-start.23 = (bf16[2,296,128]{2,1,0:T(8,128)(2,1)S(1)}, bf16[2,296,128]{2,1,0:T(8,128)(2,1)S(1)}, u32[]{:S(2)}, u32[]{:S(2)}) collective-permute-start(bf16[2,296,128]{2,1,0:T(8,128)(2,1)S(1)} %get-tuple-element.47.refs_8_), channel_id=1, source_target_pairs={{0,4},{4,0},{8,12},{12,8},{16,20},{20,16},{24,28},{28,24},{32,36},... | collective-permute-start | bytes 454664 | tf_op jit(solution)/shard_map/ppermute | solution.py:64
  23.4 3.3 %collective-permute-start.12 = (bf16[2,296,128]{2,1,0:T(8,128)(2,1)S(1)}, bf16[2,296,128]{2,1,0:T(8,128)(2,1)S(1)}, u32[]{:S(2)}, u32[]{:S(2)}) collective-permute-start(bf16[2,296,128]{2,1,0:T(8,128)(2,1)S(1)} %get-tuple-element.41), channel_id=1, source_target_pairs={{0,56},{4,60},{8,32},{12,36},{16,40},{20,44},{24,48},{28,52},{32,2... | collective-permute-start | bytes 454664 | tf_op jit(solution)/shard_map/ppermute | solution.py:64
  27.6 3.6 %collective-permute-done.10.refs_10_ = bf16[2,296,128]{2,1,0:T(8,128)(2,1)S(1)} collective-permute-done((bf16[2,296,128]{2,1,0:T(8,128)(2,1)S(1)}, bf16[2,296,128]{2,1,0:T(8,128)(2,1)S(1)}, u32[]{:S(2)}, u32[]{:S(2)}) %collective-permute-start.10) | collective-permute-done | bytes 151584 | tf_op jit(solution)/shard_map/ppermute | solution.py:64
  38.7 4.1 %collective-permute-done.14.refs_14_ = bf16[2,296,128]{2,1,0:T(8,128)(2,1)S(1)} collective-permute-done((bf16[2,296,128]{2,1,0:T(8,128)(2,1)S(1)}, bf16[2,296,128]{2,1,0:T(8,128)(2,1)S(1)}, u32[]{:S(2)}, u32[]{:S(2)}) %collective-permute-start.14) | collective-permute-done | bytes 151584 | tf_op jit(solution)/shard_map/ppermute | solution.py:64
  42.8 3.0 %collective-permute-start.30 = (bf16[128,256]{1,0:T(8,128)(2,1)S(1)}, bf16[128,256]{1,0:T(8,128)(2,1)S(1)}, u32[]{:S(2)}, u32[]{:S(2)}) collective-permute-start(bf16[128,256]{1,0:T(8,128)(2,1)S(1)} %get-tuple-element.57.refs_0_), channel_id=1, source_target_pairs={{0,64},{4,68},{8,72},{12,76},{16,80},{20,84},{24,88},{28,92},{32,9... | collective-permute-start | bytes 196616 | tf_op jit(solution)/shard_map/ppermute | solution.py:64
  47.9 4.2 %collective-permute-start.31 = (bf16[128,256]{1,0:T(8,128)(2,1)S(1)}, bf16[128,256]{1,0:T(8,128)(2,1)S(1)}, u32[]{:S(2)}, u32[]{:S(2)}) collective-permute-start(bf16[128,256]{1,0:T(8,128)(2,1)S(1)} %get-tuple-element.58.refs_1_), channel_id=1, source_target_pairs={{0,192},{4,196},{8,200},{12,204},{16,208},{20,212},{24,216},{28,22... | collective-permute-start | bytes 196616 | tf_op jit(solution)/shard_map/ppermute | solution.py:64
  52.1 2.1 %shard_map.47 = (f32[168,256]{1,0:T(8,128)S(1)}, f32[168,256]{1,0:T(8,128)S(1)}, f32[168,256]{1,0:T(8,128)S(1)}) custom-call(bf16[2,256,128]{2,1,0:T(8,128)(2,1)S(1)} %get-tuple-element.43.refs_0_, bf16[2,256,128]{2,1,0:T(8,128)(2,1)S(1)} %collective-permute-done.16.refs_1_, bf16[2,256,128]{2,1,0:T(8,128)(2,1)S(1)} %collective-permute-done.17.refs_2_, ...), custom_call_target="tpu_custom_call" | custom-call | flops 2000000000 | bytes 3000000 | tf_op jit(solution)/shard_map/pallas_call | solution.py:117
  54.5 3.1 %collective-permute-start.32 = (bf16[128,256]{1,0:T(8,128)(2,1)S(1)}, bf16[128,256]{1,0:T(8,128)(2,1)S(1)}, u32[]{:S(2)}, u32[]{:S(2)}) collective-permute-start(bf16[128,256]{1,0:T(8,128)(2,1)S(1)} %get-tuple-element.59.refs_0_), channel_id=1, source_target_pairs={{0,192},{4,196},{8,200},{12,204},{16,208},{20,212},{24,216},{28,22... | collective-permute-start | bytes 196616 | tf_op jit(solution)/shard_map/ppermute | solution.py:64
  57.5 1.8 %collective-permute-start.33 = (bf16[128,256]{1,0:T(8,128)(2,1)S(1)}, bf16[128,256]{1,0:T(8,128)(2,1)S(1)}, u32[]{:S(2)}, u32[]{:S(2)}) collective-permute-start(bf16[128,256]{1,0:T(8,128)(2,1)S(1)} %get-tuple-element.60.refs_2_), channel_id=1, source_target_pairs={{0,64},{4,68},{8,72},{12,76},{16,80},{20,84},{24,88},{28,92},{32,9... | collective-permute-start | bytes 196616 | tf_op jit(solution)/shard_map/ppermute | solution.py:64
  59.3 2.1 %shard_map.48 = (f32[168,256]{1,0:T(8,128)S(1)}, f32[168,256]{1,0:T(8,128)S(1)}, f32[168,256]{1,0:T(8,128)S(1)}) custom-call(bf16[2,256,128]{2,1,0:T(8,128)(2,1)S(1)} %collective-permute-done.refs_0_.refs_8_, bf16[2,256,128]{2,1,0:T(8,128)(2,1)S(1)} %collective-permute-done.1.refs_1_.refs_9_, ...), custom_call_target="tpu_custom_call" | custom-call | flops 2000000000 | bytes 3000000 | tf_op jit(solution)/shard_map/pallas_call | solution.py:117
  62.0 2.7 %collective-permute-start.34 = (bf16[168,256]{1,0:T(8,128)(2,1)S(1)}, bf16[168,256]{1,0:T(8,128)(2,1)S(1)}, u32[]{:S(2)}, u32[]{:S(2)}) collective-permute-start(bf16[168,256]{1,0:T(8,128)(2,1)S(1)} %shard_map.51.s0), channel_id=1, source_target_pairs={{0,64},{4,68},{8,72},{12,76},{16,80},{20,84},{24,88},{28,92},{32,9... | collective-permute-start | bytes 258056 | tf_op jit(solution)/shard_map/ppermute | solution.py:64
  65.4 3.5 %collective-permute-start.36 = (bf16[168,256]{1,0:T(8,128)(2,1)S(1)}, bf16[168,256]{1,0:T(8,128)(2,1)S(1)}, u32[]{:S(2)}, u32[]{:S(2)}) collective-permute-start(bf16[168,256]{1,0:T(8,128)(2,1)S(1)} %shard_map.51.s0), channel_id=1, source_target_pairs={{0,192},{4,196},{8,200},{12,204},{16,208},{20,212},{24,216},{28,22... | collective-permute-start | bytes 258056 | tf_op jit(solution)/shard_map/ppermute | solution.py:64
  68.8 3.4 %collective-permute-done.35.s2 = bf16[168,256]{1,0:T(8,128)(2,1)S(1)} collective-permute-done((bf16[168,256]{1,0:T(8,128)(2,1)S(1)}, bf16[168,256]{1,0:T(8,128)(2,1)S(1)}, u32[]{:S(2)}, u32[]{:S(2)}) %collective-permute-start.35) | collective-permute-done | bytes 86048 | tf_op jit(solution)/shard_map/ppermute | solution.py:64
  72.3 6.7 %collective-permute-start.37 = (bf16[168,256]{1,0:T(8,128)(2,1)S(1)}, bf16[168,256]{1,0:T(8,128)(2,1)S(1)}, u32[]{:S(2)}, u32[]{:S(2)}) collective-permute-start(bf16[168,256]{1,0:T(8,128)(2,1)S(1)} %get-tuple-element.61.value_ref), channel_id=1, source_target_pairs={{0,4},{4,0},{8,12},{12,8},{16,20},{20,16},{24,28},{28,24},{32,36},... | collective-permute-start | bytes 258056 | tf_op jit(solution)/shard_map/ppermute | solution.py:64
  81.5 2.6 %collective-permute-start.40 = (f32[1,128]{1,0:T(1,128)S(1)}, f32[1,128]{1,0:T(1,128)S(1)}, u32[]{:S(2)}, u32[]{:S(2)}) collective-permute-start(f32[1,128]{1,0:T(1,128)S(1)} %shard_map.53.p0), channel_id=1, source_target_pairs={{0,2},{1,3},{2,0},{3,1},{4,6},{5,7},{6,4},{7,5},{8,10},{9,11},{10,... | collective-permute-start | bytes 1544 | tf_op jit(solution)/shard_map/ppermute | solution.py:338
  86.6 1.9 %collective-permute-start.42 = (bf16[2,176,256]{2,1,0:T(8,128)(2,1)S(1)}, bf16[2,176,256]{2,1,0:T(8,128)(2,1)S(1)}, u32[]{:S(2)}, u32[]{:S(2)}) collective-permute-start(bf16[2,176,256]{2,1,0:T(8,128)(2,1)S(1)} %get-tuple-element.63.refs_3_), channel_id=1, source_target_pairs={{0,8},{4,28},{8,16},{12,4},{16,24},{20,12},{24,0},{28,20},{32,40},... | collective-permute-start | bytes 540680 | tf_op jit(solution)/shard_map/ppermute | solution.py:64
  90.1 2.9 %collective-permute-start.48 = (bf16[176,256]{1,0:T(8,128)(2,1)S(1)}, bf16[176,256]{1,0:T(8,128)(2,1)S(1)}, u32[]{:S(2)}, u32[]{:S(2)}) collective-permute-start(bf16[176,256]{1,0:T(8,128)(2,1)S(1)} %get-tuple-element.64), channel_id=1, source_target_pairs={{0,56},{4,60},{8,32},{12,36},{16,40},{20,44},{24,48},{28,52},{32,2... | collective-permute-start | bytes 270344 | tf_op jit(solution)/shard_map/ppermute | solution.py:64
  94.1 6.9 %collective-permute-start.45 = (bf16[2,176,256]{2,1,0:T(8,128)(2,1)S(1)}, bf16[2,176,256]{2,1,0:T(8,128)(2,1)S(1)}, u32[]{:S(2)}, u32[]{:S(2)}) collective-permute-start(bf16[2,176,256]{2,1,0:T(8,128)(2,1)S(1)} %collective-permute-done.42.refs_4_), channel_id=1, source_target_pairs={{0,4},{4,0},{8,12},{12,8},{16,20},{20,16},{24,28},{28,24},{32,36},... | collective-permute-start | bytes 540680 | tf_op jit(solution)/shard_map/ppermute | solution.py:64
  (86 shorter events, 27.3 us)
Async XLA Ops:
  7.8 9.4 %collective-permute-start.2 = (bf16[2,256,128]{2,1,0:T(8,128)(2,1)S(1)}, bf16[2,256,128]{2,1,0:T(8,128)(2,1)S(1)}, u32[]{:S(2)}, u32[]{:S(2)}) collective-permute-start(bf16[2,256,128]{2,1,0:T(8,128)(2,1)S(1)} %get-tuple-element.36), channel_id=1, source_target_pairs={{0,40},{4,44},{8,48},{12,52},{16,56},{20,60},{24,32},{28,36},{32,8... | collective-permute-start | bytes 393224 | tf_op jit(solution)/shard_map/ppermute | solution.py:64
  8.3 9.8 %collective-permute-start.4 = (bf16[2,256,128]{2,1,0:T(8,128)(2,1)S(1)}, bf16[2,256,128]{2,1,0:T(8,128)(2,1)S(1)}, u32[]{:S(2)}, u32[]{:S(2)}) collective-permute-start(bf16[2,256,128]{2,1,0:T(8,128)(2,1)S(1)} %get-tuple-element.37), channel_id=1, source_target_pairs={{0,56},{4,60},{8,32},{12,36},{16,40},{20,44},{24,48},{28,52},{32,2... | collective-permute-start | bytes 393224 | tf_op jit(solution)/shard_map/ppermute | solution.py:64
  11.8 11.6 %collective-permute-start.24 = (bf16[2,296,128]{2,1,0:T(8,128)(2,1)S(1)}, bf16[2,296,128]{2,1,0:T(8,128)(2,1)S(1)}, u32[]{:S(2)}, u32[]{:S(2)}) collective-permute-start(bf16[2,296,128]{2,1,0:T(8,128)(2,1)S(1)} %get-tuple-element.48), channel_id=1, source_target_pairs={{0,8},{4,12},{8,16},{12,20},{16,24},{20,28},{24,0},{28,4},{32,40},... | collective-permute-start | bytes 454664 | tf_op jit(solution)/shard_map/ppermute | solution.py:64
  13.5 9.1 %collective-permute-start.16 = (bf16[2,256,128]{2,1,0:T(8,128)(2,1)S(1)}, bf16[2,256,128]{2,1,0:T(8,128)(2,1)S(1)}, u32[]{:S(2)}, u32[]{:S(2)}) collective-permute-start(bf16[2,256,128]{2,1,0:T(8,128)(2,1)S(1)} %get-tuple-element.43.refs_0_), channel_id=1, source_target_pairs={{0,4},{4,0},{8,12},{12,8},{16,20},{20,16},{24,28},{28,24},{32,36},... | collective-permute-start | bytes 393224 | tf_op jit(solution)/shard_map/ppermute | solution.py:64
  17.2 9.6 %collective-permute-start.26 = (bf16[2,296,128]{2,1,0:T(8,128)(2,1)S(1)}, bf16[2,296,128]{2,1,0:T(8,128)(2,1)S(1)}, u32[]{:S(2)}, u32[]{:S(2)}) collective-permute-start(bf16[2,296,128]{2,1,0:T(8,128)(2,1)S(1)} %get-tuple-element.49), channel_id=1, source_target_pairs={{0,24},{4,28},{8,0},{12,4},{16,8},{20,12},{24,16},{28,20},{32,56},... | collective-permute-start | bytes 454664 | tf_op jit(solution)/shard_map/ppermute | solution.py:64
  18.1 9.0 %collective-permute-start.28 = (bf16[2,296,128]{2,1,0:T(8,128)(2,1)S(1)}, bf16[2,296,128]{2,1,0:T(8,128)(2,1)S(1)}, u32[]{:S(2)}, u32[]{:S(2)}) collective-permute-start(bf16[2,296,128]{2,1,0:T(8,128)(2,1)S(1)} %get-tuple-element.50), channel_id=1, source_target_pairs={{0,32},{4,36},{8,40},{12,44},{16,48},{20,52},{24,56},{28,60},{32,0... | collective-permute-start | bytes 454664 | tf_op jit(solution)/shard_map/ppermute | solution.py:64
  22.6 8.5 %collective-permute-start.10 = (bf16[2,296,128]{2,1,0:T(8,128)(2,1)S(1)}, bf16[2,296,128]{2,1,0:T(8,128)(2,1)S(1)}, u32[]{:S(2)}, u32[]{:S(2)}) collective-permute-start(bf16[2,296,128]{2,1,0:T(8,128)(2,1)S(1)} %get-tuple-element.40), channel_id=1, source_target_pairs={{0,40},{4,44},{8,48},{12,52},{16,56},{20,60},{24,32},{28,36},{32,8... | collective-permute-start | bytes 454664 | tf_op jit(solution)/shard_map/ppermute | solution.py:64
  23.4 10.1 %collective-permute-start.12 = (bf16[2,296,128]{2,1,0:T(8,128)(2,1)S(1)}, bf16[2,296,128]{2,1,0:T(8,128)(2,1)S(1)}, u32[]{:S(2)}, u32[]{:S(2)}) collective-permute-start(bf16[2,296,128]{2,1,0:T(8,128)(2,1)S(1)} %get-tuple-element.41), channel_id=1, source_target_pairs={{0,56},{4,60},{8,32},{12,36},{16,40},{20,44},{24,48},{28,52},{32,2... | collective-permute-start | bytes 454664 | tf_op jit(solution)/shard_map/ppermute | solution.py:64
  26.8 7.7 %collective-permute-start.1 = (bf16[2,256,128]{2,1,0:T(8,128)(2,1)S(1)}, bf16[2,256,128]{2,1,0:T(8,128)(2,1)S(1)}, u32[]{:S(2)}, u32[]{:S(2)}) collective-permute-start(bf16[2,256,128]{2,1,0:T(8,128)(2,1)S(1)} %collective-permute-done.refs_0_.refs_8_), channel_id=1, source_target_pairs={{0,4},{4,0},{8,12},{12,8},{16,20},{20,16},{24,28},{28,24},{32,36},... | collective-permute-start | bytes 393224 | tf_op jit(solution)/shard_map/ppermute | solution.py:64
  27.3 7.7 %collective-permute-start.20 = (bf16[2,256,128]{2,1,0:T(8,128)(2,1)S(1)}, bf16[2,256,128]{2,1,0:T(8,128)(2,1)S(1)}, u32[]{:S(2)}, u32[]{:S(2)}) collective-permute-start(bf16[2,256,128]{2,1,0:T(8,128)(2,1)S(1)} %collective-permute-done.19.refs_4_), channel_id=1, source_target_pairs={{0,4},{4,0},{8,12},{12,8},{16,20},{20,16},{24,28},{28,24},{32,36},... | collective-permute-start | bytes 393224 | tf_op jit(solution)/shard_map/ppermute | solution.py:64
  34.9 7.8 %collective-permute-start.14 = (bf16[2,296,128]{2,1,0:T(8,128)(2,1)S(1)}, bf16[2,296,128]{2,1,0:T(8,128)(2,1)S(1)}, u32[]{:S(2)}, u32[]{:S(2)}) collective-permute-start(bf16[2,296,128]{2,1,0:T(8,128)(2,1)S(1)} %get-tuple-element.42), channel_id=1, source_target_pairs={{0,48},{4,52},{8,56},{12,60},{16,32},{20,36},{24,40},{28,44},{32,1... | collective-permute-start | bytes 454664 | tf_op jit(solution)/shard_map/ppermute | solution.py:64
  36.6 9.9 %collective-permute-start.8 = (bf16[2,296,128]{2,1,0:T(8,128)(2,1)S(1)}, bf16[2,296,128]{2,1,0:T(8,128)(2,1)S(1)}, u32[]{:S(2)}, u32[]{:S(2)}) collective-permute-start(bf16[2,296,128]{2,1,0:T(8,128)(2,1)S(1)} %get-tuple-element.39), channel_id=1, source_target_pairs={{0,16},{4,20},{8,24},{12,28},{16,0},{20,4},{24,8},{28,12},{32,48},... | collective-permute-start | bytes 454664 | tf_op jit(solution)/shard_map/ppermute | solution.py:64
  37.2 9.8 %collective-permute-start.25 = (bf16[2,296,128]{2,1,0:T(8,128)(2,1)S(1)}, bf16[2,296,128]{2,1,0:T(8,128)(2,1)S(1)}, u32[]{:S(2)}, u32[]{:S(2)}) collective-permute-start(bf16[2,296,128]{2,1,0:T(8,128)(2,1)S(1)} %collective-permute-done.24.refs_10_), channel_id=1, source_target_pairs={{0,4},{4,0},{8,12},{12,8},{16,20},{20,16},{24,28},{28,24},{32,36},... | collective-permute-start | bytes 454664 | tf_op jit(solution)/shard_map/ppermute | solution.py:64
  37.6 9.5 %collective-permute-start.27 = (bf16[2,296,128]{2,1,0:T(8,128)(2,1)S(1)}, bf16[2,296,128]{2,1,0:T(8,128)(2,1)S(1)}, u32[]{:S(2)}, u32[]{:S(2)}) collective-permute-start(bf16[2,296,128]{2,1,0:T(8,128)(2,1)S(1)} %collective-permute-done.26.refs_12_), channel_id=1, source_target_pairs={{0,4},{4,0},{8,12},{12,8},{16,20},{20,16},{24,28},{28,24},{32,36},... | collective-permute-start | bytes 454664 | tf_op jit(solution)/shard_map/ppermute | solution.py:64
  37.7 9.8 %collective-permute-start.29 = (bf16[2,296,128]{2,1,0:T(8,128)(2,1)S(1)}, bf16[2,296,128]{2,1,0:T(8,128)(2,1)S(1)}, u32[]{:S(2)}, u32[]{:S(2)}) collective-permute-start(bf16[2,296,128]{2,1,0:T(8,128)(2,1)S(1)} %collective-permute-done.28.refs_14_), channel_id=1, source_target_pairs={{0,4},{4,0},{8,12},{12,8},{16,20},{20,16},{24,28},{28,24},{32,36},... | collective-permute-start | bytes 454664 | tf_op jit(solution)/shard_map/ppermute | solution.py:64
  46.5 11.1 %collective-permute-start.11 = (bf16[2,296,128]{2,1,0:T(8,128)(2,1)S(1)}, bf16[2,296,128]{2,1,0:T(8,128)(2,1)S(1)}, u32[]{:S(2)}, u32[]{:S(2)}) collective-permute-start(bf16[2,296,128]{2,1,0:T(8,128)(2,1)S(1)} %collective-permute-done.10.refs_10_), channel_id=1, source_target_pairs={{0,4},{4,0},{8,12},{12,8},{16,20},{20,16},{24,28},{28,24},{32,36},... | collective-permute-start | bytes 454664 | tf_op jit(solution)/shard_map/ppermute | solution.py:64
  47.1 12.2 %collective-permute-start.13 = (bf16[2,296,128]{2,1,0:T(8,128)(2,1)S(1)}, bf16[2,296,128]{2,1,0:T(8,128)(2,1)S(1)}, u32[]{:S(2)}, u32[]{:S(2)}) collective-permute-start(bf16[2,296,128]{2,1,0:T(8,128)(2,1)S(1)} %collective-permute-done.12.refs_12_), channel_id=1, source_target_pairs={{0,4},{4,0},{8,12},{12,8},{16,20},{20,16},{24,28},{28,24},{32,36},... | collective-permute-start | bytes 454664 | tf_op jit(solution)/shard_map/ppermute | solution.py:64
  47.2 12.1 %collective-permute-start.15 = (bf16[2,296,128]{2,1,0:T(8,128)(2,1)S(1)}, bf16[2,296,128]{2,1,0:T(8,128)(2,1)S(1)}, u32[]{:S(2)}, u32[]{:S(2)}) collective-permute-start(bf16[2,296,128]{2,1,0:T(8,128)(2,1)S(1)} %collective-permute-done.14.refs_14_), channel_id=1, source_target_pairs={{0,4},{4,0},{8,12},{12,8},{16,20},{20,16},{24,28},{28,24},{32,36},... | collective-permute-start | bytes 454664 | tf_op jit(solution)/shard_map/ppermute | solution.py:64
  47.6 11.7 %collective-permute-start.9 = (bf16[2,296,128]{2,1,0:T(8,128)(2,1)S(1)}, bf16[2,296,128]{2,1,0:T(8,128)(2,1)S(1)}, u32[]{:S(2)}, u32[]{:S(2)}) collective-permute-start(bf16[2,296,128]{2,1,0:T(8,128)(2,1)S(1)} %collective-permute-done.8.refs_8_), channel_id=1, source_target_pairs={{0,4},{4,0},{8,12},{12,8},{16,20},{20,16},{24,28},{28,24},{32,36},... | collective-permute-start | bytes 454664 | tf_op jit(solution)/shard_map/ppermute | solution.py:64
  72.3 14.3 %collective-permute-start.37 = (bf16[168,256]{1,0:T(8,128)(2,1)S(1)}, bf16[168,256]{1,0:T(8,128)(2,1)S(1)}, u32[]{:S(2)}, u32[]{:S(2)}) collective-permute-start(bf16[168,256]{1,0:T(8,128)(2,1)S(1)} %get-tuple-element.61.value_ref), channel_id=1, source_target_pairs={{0,4},{4,0},{8,12},{12,8},{16,20},{20,16},{24,28},{28,24},{32,36},... | collective-permute-start | bytes 258056 | tf_op jit(solution)/shard_map/ppermute | solution.py:64
  88.5 12.6 %collective-permute-start.43 = (bf16[2,176,256]{2,1,0:T(8,128)(2,1)S(1)}, bf16[2,176,256]{2,1,0:T(8,128)(2,1)S(1)}, u32[]{:S(2)}, u32[]{:S(2)}) collective-permute-start(bf16[2,176,256]{2,1,0:T(8,128)(2,1)S(1)} %get-tuple-element.63.refs_3_), channel_id=1, source_target_pairs={{0,32},{4,52},{8,40},{12,60},{16,48},{20,36},{24,56},{28,44},{32,0... | collective-permute-start | bytes 540680 | tf_op jit(solution)/shard_map/ppermute | solution.py:64
  88.7 12.3 %collective-permute-start.44 = (bf16[2,176,256]{2,1,0:T(8,128)(2,1)S(1)}, bf16[2,176,256]{2,1,0:T(8,128)(2,1)S(1)}, u32[]{:S(2)}, u32[]{:S(2)}) collective-permute-start(bf16[2,176,256]{2,1,0:T(8,128)(2,1)S(1)} %get-tuple-element.63.refs_3_), channel_id=1, source_target_pairs={{0,40},{4,20},{8,48},{12,28},{16,56},{20,4},{24,32},{28,12},{32,8}... | collective-permute-start | bytes 540680 | tf_op jit(solution)/shard_map/ppermute | solution.py:64
  90.1 11.5 %collective-permute-start.48 = (bf16[176,256]{1,0:T(8,128)(2,1)S(1)}, bf16[176,256]{1,0:T(8,128)(2,1)S(1)}, u32[]{:S(2)}, u32[]{:S(2)}) collective-permute-start(bf16[176,256]{1,0:T(8,128)(2,1)S(1)} %get-tuple-element.64), channel_id=1, source_target_pairs={{0,56},{4,60},{8,32},{12,36},{16,40},{20,44},{24,48},{28,52},{32,2... | collective-permute-start | bytes 270344 | tf_op jit(solution)/shard_map/ppermute | solution.py:64
  94.1 8.7 %collective-permute-start.45 = (bf16[2,176,256]{2,1,0:T(8,128)(2,1)S(1)}, bf16[2,176,256]{2,1,0:T(8,128)(2,1)S(1)}, u32[]{:S(2)}, u32[]{:S(2)}) collective-permute-start(bf16[2,176,256]{2,1,0:T(8,128)(2,1)S(1)} %collective-permute-done.42.refs_4_), channel_id=1, source_target_pairs={{0,4},{4,0},{8,12},{12,8},{16,20},{20,16},{24,28},{28,24},{32,36},... | collective-permute-start | bytes 540680 | tf_op jit(solution)/shard_map/ppermute | solution.py:64
  (26 other events, 132.0 us)
